TPU v7x, 128 devices: a whole 4x4x4 slice. The times are simulated.
128 devices in a mesh: flow: 64 (over x, y, z), group: 2 (over core).
Axes of the slice: x: 4, y: 4, z: 4, core: 2. Of those that a mesh axis runs over, the one named last changes fastest.
Arguments:
- density: float32 [256, 32, 256], P('flow', 'group'), may hold values from 0.8 to 1.2
- velocity: float32 [3, 256, 32, 256], P(None, 'flow', 'group'), may hold values from -0.5 to 0.5
- pressure: float32 [256, 32, 256], P('flow', 'group'), may hold values from 0.7 to 1.3
- wave_state: float32 [4, 8, 8, 8, 16384], P(None, None, None, None, ('flow', 'group')), may hold values from -1.8 to 1.8
- tables: float32 [4, 512, 512], replicated, may hold values from -0.75 to 0.75
- margin_element: int32 [128, 256], P(('flow', 'group')), may hold values from 0 to 16383, as said below
- margin_block: int32 [128, 256], P(('flow', 'group')), may hold values from 0 to 31
- margin_table: int32 [128, 256], P(('flow', 'group')), may hold values from 0 to 3
Outputs:
- flow_state: float32 [5, 256, 32, 256], P(None, 'flow', 'group')
- wave_out: float32 [4, 8, 8, 8, 16384], P(None, None, None, None, ('flow', 'group'))
- forcing: float32 [3, 8, 8, 8, 16384], P(None, None, None, None, ('flow', 'group'))
Inputs may be any that keep to these rules, and one draw needn't show every extreme that they name: `margin_element`: global element ids; element e belongs to the device at position e // 128 along flow then group. In every device's row at most 4 entries name elements of one owner, and some owner receives exactly 4 entries from it.
All inputs are finite; a program needn't handle non-finite values.
Results may differ from a plain program's by a relative error of at most 0.0003.
Values sent between devices are 32-bit elements; how exact they have to be, the bound alone decides.
No kernel may reach another device: no remote copies, remote signals or barrier semaphores. Data moves between devices by JAX's collectives and lax.ppermute only.
A program may use at most 128 MiB of HBM per device.

v0:
```python
import jax
import jax.numpy as jnp
import numpy as np
from jax import lax
from jax.sharding import PartitionSpec as P

NP = 8
EZ = 16
CAP = 4
STEPS = 2


GAMMA = 1.4
DT_FLOW = 0.08
ACOUSTIC_STEP = 0.01
MAXIMUM_DEGREE = lax.Precision.HIGHEST


def with_halo(value, sides, width):
    edges = {}
    for axis, dim in sides:
        size, length = (lax.axis_size(axis), value.shape[dim])
        up = [(i, (i + 1) % size) for i in range(size)]
        last = lax.slice_in_dim(value, length - width, length, axis=dim)
        initial = lax.slice_in_dim(value, 0, width, axis=dim)
        edges[dim] = (
            lax.ppermute(last, axis, up),
            lax.ppermute(initial, axis, [(b, a) for a, b in up]),
        )
    done = []
    for _, dim in sides:
        low, high = edges[dim]
        around = [(width, width) if d in done else (0, 0) for d in range(value.ndim)]
        value = jnp.concatenate([jnp.pad(low, around), value, jnp.pad(high, around)], axis=dim)
        done.append(dim)
    return value


def from_behind(value, axis, by):
    length = lax.axis_size(axis)
    return lax.ppermute(value, axis, [(i, (i + by) % length) for i in range(length)])


def in_blocks(value, dim, length):
    shape = value.shape
    parts = value.reshape(*shape[:dim], length, shape[dim] // length, *shape[dim + 1 :])
    return jnp.moveaxis(parts, dim, 0)


def in_order(parts, dim):
    parts = jnp.moveaxis(parts, 0, dim)
    shape = parts.shape
    return parts.reshape(*shape[:dim], shape[dim] * shape[dim + 1], *shape[dim + 2 :])


def joined_exchange(value, axis, axes, splits, concats):
    sizes = [lax.axis_size(a) for a in axes]
    parts = in_blocks(value, splits[0], sizes[0])
    parts = jnp.moveaxis(in_blocks(parts, splits[1] + 1, sizes[1]), 0, 1)
    inside = parts.shape[2:]
    parts = parts.reshape(-1, *inside)
    parts = lax.all_to_all(parts, axis, split_axis=0, concat_axis=0, tiled=True)
    parts = in_order(parts.reshape(*sizes, *inside), concats[0] + 1)
    return in_order(parts, concats[1])


def legendre_pair(quadrature_nodes, degree):
    previous = np.ones(quadrature_nodes.shape[0])
    current = quadrature_nodes * 1.0
    for order in range(2, degree + 1):
        previous, current = (
            current,
            ((2 * order - 1) * quadrature_nodes * current - (order - 1) * previous) / order,
        )
    return (previous, current)


def lobatto(point_count):
    degree = point_count - 1
    quadrature_nodes = -np.cos(np.pi * np.arange(point_count) / degree)
    for sweep in range(60):
        previous, current = legendre_pair(quadrature_nodes, degree)
        quadrature_nodes = quadrature_nodes - (quadrature_nodes * current - previous) / (
            point_count * current
        )
    previous, values = legendre_pair(quadrature_nodes, degree)
    quadrature_weights = 2.0 / (degree * (degree + 1) * values**2)
    identity = np.eye(point_count)
    differ = quadrature_nodes[:, None] - quadrature_nodes[None, :] + identity
    matrix = values[:, None] / values[None, :] / differ * (1.0 - identity)
    matrix[0, 0] = -degree * (degree + 1) / 4.0
    matrix[-1, -1] = degree * (degree + 1) / 4.0
    return (matrix, float(quadrature_weights[0]))


def physical(fields):
    density = fields[0]
    velocity = fields[1:4] / density
    pressure = (GAMMA - 1.0) * (fields[4] - 0.5 * density * jnp.sum(velocity * velocity, axis=0))
    return (density, velocity, pressure)


def euler_flux(fields, velocity, pressure, direction):
    normal = velocity[direction]
    components = [fields[0] * normal]
    for column in range(3):
        product = fields[1 + column] * normal
        if column == direction:
            product = product + pressure
        components.append(product)
    components.append((fields[4] + pressure) * normal)
    return jnp.stack(components)


def rusanov(left_side, right_side, direction):
    left_rho, left_vel, left_pre = physical(left_side)
    right_rho, right_vel, right_pre = physical(right_side)
    wave_speed = jnp.maximum(
        jnp.abs(left_vel[direction]) + jnp.sqrt(GAMMA * left_pre / left_rho),
        jnp.abs(right_vel[direction]) + jnp.sqrt(GAMMA * right_pre / right_rho),
    )
    return 0.5 * (
        euler_flux(left_side, left_vel, left_pre, direction)
        + euler_flux(right_side, right_vel, right_pre, direction)
    ) - 0.5 * wave_speed * (right_side - left_side)


def face_rims(fields):
    padded = with_halo(fields, (("flow", 1), ("group", 2)), 1)
    return (padded[:, :, 1:-1], padded[:, 1:-1])


def flow_rate(fields, along_x, along_y):
    face_flux = rusanov(along_x[:, :-1], along_x[:, 1:], 0)
    tendency = jnp.zeros_like(fields) - (face_flux[:, 1:] - face_flux[:, :-1])
    face_flux = rusanov(along_y[:, :, :-1], along_y[:, :, 1:], 1)
    tendency = tendency - (face_flux[:, :, 1:] - face_flux[:, :, :-1])
    face_flux = rusanov(fields, jnp.roll(fields, -1, 3), 2)
    return tendency - (face_flux - jnp.roll(face_flux, 1, 3))


def lamb_vector(fields, along_x, along_y):
    velocity = fields[1:4] / fields[0]
    wide_x = along_x[1:4] / along_x[0]
    wide_y = along_y[1:4] / along_y[0]
    slope_x = 0.5 * (wide_x[:, 2:] - wide_x[:, :-2])
    slope_y = 0.5 * (wide_y[:, :, 2:] - wide_y[:, :, :-2])
    slope_z = 0.5 * (jnp.roll(velocity, -1, 3) - jnp.roll(velocity, 1, 3))
    curl_x = slope_y[2] - slope_z[1]
    curl_y = slope_z[0] - slope_x[2]
    curl_z = slope_x[1] - slope_y[0]
    return jnp.stack(
        [
            curl_y * velocity[2] - curl_z * velocity[1],
            curl_z * velocity[0] - curl_x * velocity[2],
            curl_x * velocity[1] - curl_y * velocity[0],
        ]
    )


def derivative(values, derive, direction):
    forms = ("ai,ijke->ajke", "aj,ijke->iake", "ak,ijke->ijae")
    return jnp.einsum(forms[direction], derive, values, precision=MAXIMUM_DEGREE)


def place_lifts(lower_lift, upper_lift, direction, point_count):
    middle_shape = list(upper_lift.shape)
    middle_shape.insert(direction, point_count - 2)
    middle = jnp.zeros(middle_shape, upper_lift.dtype)
    return jnp.concatenate(
        [jnp.expand_dims(lower_lift, direction), middle, jnp.expand_dims(upper_lift, direction)],
        axis=direction,
    )


def upper_neighbour(faces, direction):
    local_count = faces.shape[-1]
    if direction == 0:
        return from_behind(faces, ("flow", "group"), -1)
    if direction == 1:
        return jnp.roll(faces, -EZ, 3)
    last_z = jnp.arange(local_count) % EZ == EZ - 1
    return jnp.where(last_z, jnp.roll(faces, EZ - 1, 3), jnp.roll(faces, -1, 3))


def lower_neighbour(faces, direction):
    local_count = faces.shape[-1]
    if direction == 0:
        return from_behind(faces, ("flow", "group"), 1)
    if direction == 1:
        return jnp.roll(faces, EZ, 3)
    first_z = jnp.arange(local_count) % EZ == 0
    return jnp.where(first_z, jnp.roll(faces, 1 - EZ, 3), jnp.roll(faces, 1, 3))


def wave_rate(wave_field, forcing):
    point_count = wave_field.shape[1]
    matrix, end_weight = lobatto(point_count)
    derive = jnp.asarray(matrix, jnp.float32)
    pressure = wave_field[0]
    pressure_rate = jnp.zeros_like(pressure)
    velocity_tendency = []
    last = point_count - 1
    for direction in range(3):
        normal = wave_field[1 + direction]
        lower_face = jnp.stack(
            [jnp.take(pressure, 0, axis=direction), jnp.take(normal, 0, axis=direction)]
        )
        upper_face = jnp.stack(
            [jnp.take(pressure, last, axis=direction), jnp.take(normal, last, axis=direction)]
        )
        above_face = upper_neighbour(lower_face, direction)
        below_face = lower_neighbour(upper_face, direction)
        upper_pressure_flux = 0.5 * (upper_face[1] + above_face[1]) - 0.5 * (
            above_face[0] - upper_face[0]
        )
        upper_normal_flux = 0.5 * (upper_face[0] + above_face[0]) - 0.5 * (
            above_face[1] - upper_face[1]
        )
        lower_pressure_flux = 0.5 * (below_face[1] + lower_face[1]) - 0.5 * (
            lower_face[0] - below_face[0]
        )
        lower_normal_flux = 0.5 * (below_face[0] + lower_face[0]) - 0.5 * (
            lower_face[1] - below_face[1]
        )
        pressure_lift = place_lifts(
            (lower_pressure_flux - lower_face[1]) / end_weight,
            -(upper_pressure_flux - upper_face[1]) / end_weight,
            direction,
            point_count,
        )
        normal_lift = place_lifts(
            (lower_normal_flux - lower_face[0]) / end_weight,
            -(upper_normal_flux - upper_face[0]) / end_weight,
            direction,
            point_count,
        )
        pressure_rate = pressure_rate - derivative(normal, derive, direction) + pressure_lift
        velocity_tendency.append(
            -derivative(pressure, derive, direction) + normal_lift + forcing[direction]
        )
    return jnp.stack([pressure_rate] + velocity_tendency)


def runge_kutta(start, rate, step_size):
    first_section = start + step_size * rate(start)
    second_section = 0.75 * start + 0.25 * (first_section + step_size * rate(first_section))
    return start / 3.0 + 2.0 / 3.0 * (second_section + step_size * rate(second_section))


def pack_partials(source, tables, element_ids, block_ids, table_ids, local_count):
    node_count = tables.shape[1]
    devices = lax.axis_size("flow") * lax.axis_size("group")
    entry_count = element_ids.shape[0]
    sorted_entries = source.reshape(3, -1, node_count)
    mapped_values = jnp.einsum("yki,xiq->xykq", sorted_entries, tables, precision=MAXIMUM_DEGREE)
    pieces = mapped_values[table_ids, :, block_ids, :]
    owner_index = element_ids // local_count
    local_index = element_ids % local_count
    same_owner = owner_index[:, None] == owner_index[None, :]
    earlier = jnp.arange(entry_count)[:, None] > jnp.arange(entry_count)[None, :]
    slot_rank = jnp.sum(same_owner & earlier, axis=1)
    slot_index = owner_index * CAP + slot_rank
    buffer = jnp.zeros((devices * CAP, 3, node_count), jnp.float32).at[slot_index].set(pieces)
    target_indices = (
        jnp.full((devices * CAP,), local_count, jnp.int32).at[slot_index].set(local_index)
    )
    return (buffer.reshape(devices, CAP, 3, node_count), target_indices.reshape(devices, CAP))


def gather_sources(source, tables, margin_element, margin_block, margin_table, local_count):
    node_count = tables.shape[1]
    buffer, target_indices = pack_partials(
        source, tables, margin_element[0], margin_block[0], margin_table[0], local_count
    )
    flow_count = lax.axis_size("flow")
    arrived, labels = (
        joined_exchange(
            buffer.reshape(flow_count, -1, CAP, 3, node_count),
            ("flow", "group"),
            ("flow", "group"),
            (0, 1),
            (0, 1),
        ),
        joined_exchange(
            target_indices.reshape(flow_count, -1, CAP),
            ("flow", "group"),
            ("flow", "group"),
            (0, 1),
            (0, 1),
        ),
    )
    flat_rows = arrived.reshape(-1, 3 * node_count)
    row_targets = labels.reshape(-1)
    summed = jax.ops.segment_sum(flat_rows, row_targets, num_segments=local_count + 1)[:local_count]
    return summed.reshape(local_count, 3, NP, NP, NP).transpose(1, 2, 3, 4, 0)


def local(
    density, velocity, pressure, wave_state, tables, margin_element, margin_block, margin_table
):
    momentum = density[None] * velocity
    energy = pressure / (GAMMA - 1.0) + 0.5 * density * jnp.sum(velocity * velocity, axis=0)
    fields = jnp.concatenate([density[None], momentum, energy[None]], axis=0)
    wave_field = wave_state
    local_count = wave_state.shape[-1]
    forcing = jnp.zeros((3, NP, NP, NP, local_count), jnp.float32)
    for step_index in range(STEPS):
        along_x, along_y = face_rims(fields)
        source = lamb_vector(fields, along_x, along_y)
        forcing = gather_sources(
            source, tables, margin_element, margin_block, margin_table, local_count
        )
        first_section = fields + DT_FLOW * flow_rate(fields, along_x, along_y)
        along_x, along_y = face_rims(first_section)
        second_section = 0.75 * fields + 0.25 * (
            first_section + DT_FLOW * flow_rate(first_section, along_x, along_y)
        )
        along_x, along_y = face_rims(second_section)
        fields = fields / 3.0 + 2.0 / 3.0 * (
            second_section + DT_FLOW * flow_rate(second_section, along_x, along_y)
        )
        wave_field = runge_kutta(
            wave_field, lambda current: wave_rate(current, forcing), ACOUSTIC_STEP
        )
    return (fields, wave_field, forcing)


def solution(mesh):
    in_specs = (
        P("flow", "group", None),
        P(None, "flow", "group", None),
        P("flow", "group", None),
        P(None, None, None, None, ("flow", "group")),
        P(),
        P(("flow", "group"), None),
        P(("flow", "group"), None),
        P(("flow", "group"), None),
    )
    out_specs = (
        P(None, "flow", "group", None),
        P(None, None, None, None, ("flow", "group")),
        P(None, None, None, None, ("flow", "group")),
    )
    return jax.shard_map(local, mesh=mesh, in_specs=in_specs, out_specs=out_specs, check_vma=False)
```

profile of v0, /device:TPU:0, one launch (start us, length us, event | category | flops | bytes accessed | tf_op | source)
XLA Modules:
  0.0 378.1 jit_solution(15875215656715294423)
XLA Ops:
  7.2 6.8 %collective-permute-start.1 = (f32[5,1,16,256]{3,2,1,0:T(8,128)}, f32[5,1,16,256]{3,2,1,0:T(8,128)S(1)}, u32[]{:S(2)}, u32[]{:S(2)}) collective-permute-start(f32[5,1,16,256]{3,2,1,0:T(8,128)} %get-tuple-element.468), channel_id=1, source_target_pairs={{2,0},{4,2},{6,4},{8,6},{10,8},{12,10},{14,12},{16,14},{18,16},{20... | collective-permute-start | bytes 245768 | tf_op jit(solution)/shard_map/ppermute | solution.py:28
  19.5 4.6 %all-to-all-start = ((s32[128,1,1,4]{3,2,1,0:T(1,128)}), s32[128,1,1,4]{3,2,1,0:T(1,128)S(1)}, u32[]{:S(2)}, u32[]{:S(2)}) async-start(s32[128,1,1,4]{3,2,1,0:T(1,128)} %bitcast.158), calls=%async_computation | async-start | bytes 131072 | tf_op jit(solution)/shard_map/all_to_all | solution.py:62
  37.7 7.7 %collective-permute-start.25 = (f32[2,8,8,128]{3,1,2,0:T(8,128)S(1)}, f32[2,8,8,128]{3,1,2,0:T(8,128)S(1)}, u32[]{:S(2)}, u32[]{:S(2)}) collective-permute-start(f32[2,8,8,128]{3,1,2,0:T(8,128)S(1)} %pad_maximum_fusion.65), channel_id=1, source_target_pairs={{0,127},{1,0},{2,1},{3,2},{4,3},{5,4},{6,5},{7,6},{8,7},{9,8},{10,... | collective-permute-start | bytes 196616 | tf_op jit(solution)/shard_map/ppermute | solution.py:41
  56.2 4.7 %fusion.4 = f32[4,3,32,512]{3,2,0,1:T(8,128)S(1)} fusion(f32[4,512,512]{2,1,0:T(8,128)} %param.30, f32[1,32,512]{2,1,0:T(8,128)S(1)} %stack.792, f32[1,32,512]{2,1,0:T(8,128)S(1)} %stack.791, f32[1,32,512]{2,1,0:T(8,128)S(1)} %stack.790), kind=kOutput, calls=%fused_computation.11 | convolution fusion | flops 1208057856 | bytes 5177344 | tf_op jit(solution)/shard_map/yki,xiq->xykq/dot_general | solution.py:256
  61.5 3.4 gather_fusion
  64.9 2.5 broadcast.666.clone
  67.4 29.9 %scatter_fusion = f32[512,3,512]{2,1,0:T(4,128)} fusion(f32[512,3,512]{2,1,0:T(4,128)} %broadcast.666.clone, s32[256]{0:T(256)S(1)} %bitcast.2998, f32[256,3,512]{2,1,0:T(4,128)} %gather_fusion), kind=kCustom, calls=%fused_computation.3 | custom fusion | bytes 4719616 | tf_op jit(solution)/shard_map/scatter | solution.py:264
  97.3 5.4 %copy.1123 = f32[128,1,1,4,3,512]{5,3,4,2,1,0:T(4,128)} copy(f32[128,1,1,4,3,512]{5,4,3,0,2,1:T(4,128)} %bitcast.2851) | data formatting | bytes 6291456 | tf_op jit(solution)/shard_map/reshape;transpose;transpose;reshape;reshape;reshape;reshape | solution.py:61
  102.7 9.2 %all-to-all-start.1 = ((f32[128,1,1,4,3,512]{5,3,4,2,1,0:T(4,128)}), f32[128,1,1,4,3,512]{5,3,4,2,1,0:T(4,128)}, u32[]{:S(2)}, u32[]{:S(2)}) async-start(f32[128,1,1,4,3,512]{5,3,4,2,1,0:T(4,128)} %copy.1123), calls=%async_computation.1 | async-start | bytes 6291456 | tf_op jit(solution)/shard_map/all_to_all | solution.py:62
  113.8 6.4 %collective-permute-start.5 = (f32[5,1,16,256]{3,2,1,0:T(8,128)S(1)}, f32[5,1,16,256]{3,2,1,0:T(8,128)S(1)}, u32[]{:S(2)}, u32[]{:S(2)}) collective-permute-start(f32[5,1,16,256]{3,2,1,0:T(8,128)S(1)} %copy-done.20), channel_id=1, source_target_pairs={{2,0},{4,2},{6,4},{8,6},{10,8},{12,10},{14,12},{16,14},{18,16},{20... | collective-permute-start | bytes 245768 | tf_op jit(solution)/shard_map/ppermute | solution.py:28
  121.8 33.0 %collective-permute-done.4 = f32[5,1,16,256]{3,2,1,0:T(8,128)S(1)} collective-permute-done((f32[5,1,16,256]{3,2,1,0:T(8,128)S(1)}, f32[5,1,16,256]{3,2,1,0:T(8,128)S(1)}, u32[]{:S(2)}, u32[]{:S(2)}) %collective-permute-start.4) | collective-permute-done | bytes 81952 | tf_op jit(solution)/shard_map/ppermute | solution.py:27
  157.4 7.4 %collective-permute-start.9 = (f32[5,1,16,256]{3,2,1,0:T(8,128)S(1)}, f32[5,1,16,256]{3,2,1,0:T(8,128)S(1)}, u32[]{:S(2)}, u32[]{:S(2)}) collective-permute-start(f32[5,1,16,256]{3,2,1,0:T(8,128)S(1)} %get-tuple-element.450), channel_id=1, source_target_pairs={{2,0},{4,2},{6,4},{8,6},{10,8},{12,10},{14,12},{16,14},{18,16},{20... | collective-permute-start | bytes 245768 | tf_op jit(solution)/shard_map/ppermute | solution.py:28
  169.4 7.5 %collective-permute-start.13 = (f32[5,1,16,256]{3,2,1,0:T(8,128)S(1)}, f32[5,1,16,256]{3,2,1,0:T(8,128)S(1)}, u32[]{:S(2)}, u32[]{:S(2)}) collective-permute-start(f32[5,1,16,256]{3,2,1,0:T(8,128)S(1)} %get-tuple-element.438), channel_id=1, source_target_pairs={{2,0},{4,2},{6,4},{8,6},{10,8},{12,10},{14,12},{16,14},{18,16},{20... | collective-permute-start | bytes 245768 | tf_op jit(solution)/shard_map/ppermute | solution.py:28
  182.9 7.6 %collective-permute-start.17 = (f32[5,1,16,256]{3,2,1,0:T(8,128)}, f32[5,1,16,256]{3,2,1,0:T(8,128)S(1)}, u32[]{:S(2)}, u32[]{:S(2)}) collective-permute-start(f32[5,1,16,256]{3,2,1,0:T(8,128)} %get-tuple-element.426), channel_id=1, source_target_pairs={{2,0},{4,2},{6,4},{8,6},{10,8},{12,10},{14,12},{16,14},{18,16},{20... | collective-permute-start | bytes 245768 | tf_op jit(solution)/shard_map/ppermute | solution.py:28
  194.5 3.4 gather_fusion.1
  200.4 29.9 %scatter_fusion.1 = f32[512,3,512]{2,1,0:T(4,128)} fusion(f32[512,3,512]{2,1,0:T(4,128)} %broadcast.666.clone.1, s32[256]{0:T(256)S(1)} %bitcast.2999, f32[256,3,512]{2,1,0:T(4,128)} %gather_fusion.1), kind=kCustom, calls=%fused_computation.5 | custom fusion | bytes 4719616 | tf_op jit(solution)/shard_map/scatter | solution.py:264
  230.3 5.4 %copy.1258 = f32[128,1,1,4,3,512]{5,3,4,2,1,0:T(4,128)} copy(f32[128,1,1,4,3,512]{5,4,3,0,2,1:T(4,128)} %bitcast.2850) | data formatting | bytes 6291456 | tf_op jit(solution)/shard_map/reshape;transpose;transpose;reshape;reshape;reshape;reshape | solution.py:61
  238.5 7.4 %collective-permute-start.21 = (f32[5,1,16,256]{3,2,1,0:T(8,128)S(1)}, f32[5,1,16,256]{3,2,1,0:T(8,128)S(1)}, u32[]{:S(2)}, u32[]{:S(2)}) collective-permute-start(f32[5,1,16,256]{3,2,1,0:T(8,128)S(1)} %get-tuple-element.414), channel_id=1, source_target_pairs={{2,0},{4,2},{6,4},{8,6},{10,8},{12,10},{14,12},{16,14},{18,16},{20... | collective-permute-start | bytes 245768 | tf_op jit(solution)/shard_map/ppermute | solution.py:28
  250.7 9.9 %all-to-all-start.2 = ((f32[128,1,1,4,3,512]{5,3,4,2,1,0:T(4,128)}), f32[128,1,1,4,3,512]{5,3,4,2,1,0:T(4,128)}, u32[]{:S(2)}, u32[]{:S(2)}) async-start(f32[128,1,1,4,3,512]{5,3,4,2,1,0:T(4,128)} %copy.1258), calls=%async_computation.2 | async-start | bytes 6291456 | tf_op jit(solution)/shard_map/all_to_all | solution.py:62
  260.5 3.8 %copy.1124 = f32[64,2,1,1,4,3,512]{6,5,4,1,0,3,2:T(4,128)S(1)} copy(f32[64,2,1,1,4,3,512]{6,4,5,1,0,3,2:T(4,128)} %bitcast.173) | data formatting | bytes 6291456 | tf_op jit(solution)/shard_map/reshape | solution.py:63
  264.3 3.1 copy.1403
  267.5 7.2 %scatter_custom_fusion.2 = f32[129,1536]{1,0:T(8,128)S(1)} fusion(s32[512]{0:T(512)} %reshape.777, f32[512,1536]{1,0:T(8,128)} %bitcast.2874, f32[]{:T(128)} %constant.320.clone.1), kind=kCustom, calls=%fused_computation.309 | custom fusion | flops 786432 | bytes 793088 | tf_op jit(solution)/shard_map/scatter-add | solution.py:295
  280.7 7.0 %collective-permute-start.27 = (f32[2,8,8,128]{3,1,2,0:T(8,128)S(1)}, f32[2,8,8,128]{3,1,2,0:T(8,128)S(1)}, u32[]{:S(2)}, u32[]{:S(2)}) collective-permute-start(f32[2,8,8,128]{3,1,2,0:T(8,128)S(1)} %pad_maximum_fusion.67), channel_id=1, source_target_pairs={{0,127},{1,0},{2,1},{3,2},{4,3},{5,4},{6,5},{7,6},{8,7},{9,8},{10,... | collective-permute-start | bytes 196616 | tf_op jit(solution)/shard_map/ppermute | solution.py:41
  288.8 4.1 %collective-permute-done.27 = f32[2,8,8,128]{3,1,2,0:T(8,128)S(1)} collective-permute-done((f32[2,8,8,128]{3,1,2,0:T(8,128)S(1)}, f32[2,8,8,128]{3,1,2,0:T(8,128)S(1)}, u32[]{:S(2)}, u32[]{:S(2)}) %collective-permute-start.27) | collective-permute-done | bytes 65568 | tf_op jit(solution)/shard_map/ppermute | solution.py:41
  292.9 9.4 %collective-permute-done.26 = f32[2,8,8,128]{3,1,2,0:T(8,128)S(1)} collective-permute-done((f32[2,8,8,128]{3,1,2,0:T(8,128)S(1)}, f32[2,8,8,128]{3,1,2,0:T(8,128)S(1)}, u32[]{:S(2)}, u32[]{:S(2)}) %collective-permute-start.26) | collective-permute-done | bytes 65568 | tf_op jit(solution)/shard_map/ppermute | solution.py:41
  308.6 7.3 %collective-permute-done.28 = f32[2,8,8,128]{3,2,1,0:T(8,128)S(1)} collective-permute-done((f32[2,8,8,128]{3,2,1,0:T(8,128)S(1)}, f32[2,8,8,128]{3,2,1,0:T(8,128)S(1)}, u32[]{:S(2)}, u32[]{:S(2)}) %collective-permute-start.28) | collective-permute-done | bytes 65568 | tf_op jit(solution)/shard_map/ppermute | solution.py:41
  322.2 5.5 %collective-permute-done.30 = f32[2,8,8,128]{3,1,2,0:T(8,128)S(1)} collective-permute-done((f32[2,8,8,128]{3,1,2,0:T(8,128)S(1)}, f32[2,8,8,128]{3,1,2,0:T(8,128)S(1)}, u32[]{:S(2)}, u32[]{:S(2)}) %collective-permute-start.30) | collective-permute-done | bytes 65568 | tf_op jit(solution)/shard_map/ppermute | solution.py:41
  328.9 3.8 %copy.1259 = f32[64,2,1,1,4,3,512]{6,5,4,1,0,3,2:T(4,128)S(1)} copy(f32[64,2,1,1,4,3,512]{6,4,5,1,0,3,2:T(4,128)} %bitcast.384) | data formatting | bytes 6291456 | tf_op jit(solution)/shard_map/reshape | solution.py:63
  332.7 3.1 copy.1404
  335.8 7.2 %scatter_custom_fusion.4 = f32[129,1536]{1,0:T(8,128)S(1)} fusion(s32[512]{0:T(512)} %reshape.777, f32[512,1536]{1,0:T(8,128)} %bitcast.2873, f32[]{:T(128)} %constant.320.clone.1), kind=kCustom, calls=%fused_computation.307 | custom fusion | flops 786432 | bytes 793088 | tf_op jit(solution)/shard_map/scatter-add | solution.py:295
  353.5 7.3 %collective-permute-done.32 = f32[2,8,8,128]{3,2,1,0:T(8,128)S(1)} collective-permute-done((f32[2,8,8,128]{3,2,1,0:T(8,128)S(1)}, f32[2,8,8,128]{3,2,1,0:T(8,128)S(1)}, u32[]{:S(2)}, u32[]{:S(2)}) %collective-permute-start.32) | collective-permute-done | bytes 65568 | tf_op jit(solution)/shard_map/ppermute | solution.py:41
  367.0 7.6 %collective-permute-done.34 = f32[2,8,8,128]{3,2,1,0:T(8,128)S(1)} collective-permute-done((f32[2,8,8,128]{3,2,1,0:T(8,128)S(1)}, f32[2,8,8,128]{3,2,1,0:T(8,128)S(1)}, u32[]{:S(2)}, u32[]{:S(2)}) %collective-permute-start.34) | collective-permute-done | bytes 65568 | tf_op jit(solution)/shard_map/ppermute | solution.py:41
  (699 shorter events, 104.4 us)
Async XLA Ops:
  5.2 46.9 %collective-permute-start = (f32[5,1,16,256]{3,2,1,0:T(8,128)}, f32[5,1,16,256]{3,2,1,0:T(8,128)S(1)}, u32[]{:S(2)}, u32[]{:S(2)}) collective-permute-start(f32[5,1,16,256]{3,2,1,0:T(8,128)} %get-tuple-element.467), channel_id=1, source_target_pairs={{0,2},{2,4},{4,6},{6,8},{8,10},{10,12},{12,14},{14,16},{16,18},{18... | collective-permute-start | bytes 245768 | tf_op jit(solution)/shard_map/ppermute | solution.py:27
  7.2 44.9 %collective-permute-start.1 = (f32[5,1,16,256]{3,2,1,0:T(8,128)}, f32[5,1,16,256]{3,2,1,0:T(8,128)S(1)}, u32[]{:S(2)}, u32[]{:S(2)}) collective-permute-start(f32[5,1,16,256]{3,2,1,0:T(8,128)} %get-tuple-element.468), channel_id=1, source_target_pairs={{2,0},{4,2},{6,4},{8,6},{10,8},{12,10},{14,12},{16,14},{18,16},{20... | collective-permute-start | bytes 245768 | tf_op jit(solution)/shard_map/ppermute | solution.py:28
  14.6 23.1 %collective-permute-start.2 = (f32[5,4,1,256]{3,2,1,0:T(1,128)}, f32[5,4,1,256]{3,2,1,0:T(1,128)}, u32[]{:S(2)}, u32[]{:S(2)}) collective-permute-start(f32[5,4,1,256]{3,2,1,0:T(1,128)} %get-tuple-element.466), channel_id=1, source_target_pairs={{0,1},{1,0},{2,3},{3,2},{4,5},{5,4},{6,7},{7,6},{8,9},{9,8},{10,11... | collective-permute-start | bytes 61448 | tf_op jit(solution)/shard_map/ppermute | solution.py:27
  14.6 31.5 %collective-permute-start.3 = (f32[5,4,1,256]{3,2,1,0:T(1,128)}, f32[5,4,1,256]{3,2,1,0:T(1,128)}, u32[]{:S(2)}, u32[]{:S(2)}) collective-permute-start(f32[5,4,1,256]{3,2,1,0:T(1,128)} %get-tuple-element.465), channel_id=1, source_target_pairs={{1,0},{0,1},{3,2},{2,3},{5,4},{4,5},{7,6},{6,7},{9,8},{8,9},{11,10... | collective-permute-start | bytes 61448 | tf_op jit(solution)/shard_map/ppermute | solution.py:28
  19.5 17.5 %all-to-all-start = ((s32[128,1,1,4]{3,2,1,0:T(1,128)}), s32[128,1,1,4]{3,2,1,0:T(1,128)S(1)}, u32[]{:S(2)}, u32[]{:S(2)}) async-start(s32[128,1,1,4]{3,2,1,0:T(1,128)} %bitcast.158), calls=%async_computation | async-start | bytes 131072 | tf_op jit(solution)/shard_map/all_to_all | solution.py:62
  26.9 20.0 %collective-permute-start.24 = (f32[2,8,8,128]{3,1,2,0:T(8,128)}, f32[2,8,8,128]{3,1,2,0:T(8,128)}, u32[]{:S(2)}, u32[]{:S(2)}) collective-permute-start(f32[2,8,8,128]{3,1,2,0:T(8,128)} %pad_maximum_fusion.64), channel_id=1, source_target_pairs={{0,1},{1,2},{2,3},{3,4},{4,5},{5,6},{6,7},{7,8},{8,9},{9,10},{10,1... | collective-permute-start | bytes 196616 | tf_op jit(solution)/shard_map/ppermute | solution.py:41
  37.7 10.0 %collective-permute-start.25 = (f32[2,8,8,128]{3,1,2,0:T(8,128)S(1)}, f32[2,8,8,128]{3,1,2,0:T(8,128)S(1)}, u32[]{:S(2)}, u32[]{:S(2)}) collective-permute-start(f32[2,8,8,128]{3,1,2,0:T(8,128)S(1)} %pad_maximum_fusion.65), channel_id=1, source_target_pairs={{0,127},{1,0},{2,1},{3,2},{4,3},{5,4},{6,5},{7,6},{8,7},{9,8},{10,... | collective-permute-start | bytes 196616 | tf_op jit(solution)/shard_map/ppermute | solution.py:41
  102.7 148.0 %all-to-all-start.1 = ((f32[128,1,1,4,3,512]{5,3,4,2,1,0:T(4,128)}), f32[128,1,1,4,3,512]{5,3,4,2,1,0:T(4,128)}, u32[]{:S(2)}, u32[]{:S(2)}) async-start(f32[128,1,1,4,3,512]{5,3,4,2,1,0:T(4,128)} %copy.1123), calls=%async_computation.1 | async-start | bytes 6291456 | tf_op jit(solution)/shard_map/all_to_all | solution.py:62
  112.8 42.0 %collective-permute-start.4 = (f32[5,1,16,256]{3,2,1,0:T(8,128)S(1)}, f32[5,1,16,256]{3,2,1,0:T(8,128)S(1)}, u32[]{:S(2)}, u32[]{:S(2)}) collective-permute-start(f32[5,1,16,256]{3,2,1,0:T(8,128)S(1)} %copy-done.21), channel_id=1, source_target_pairs={{0,2},{2,4},{4,6},{6,8},{8,10},{10,12},{12,14},{14,16},{16,18},{18... | collective-permute-start | bytes 245768 | tf_op jit(solution)/shard_map/ppermute | solution.py:27
  113.8 40.9 %collective-permute-start.5 = (f32[5,1,16,256]{3,2,1,0:T(8,128)S(1)}, f32[5,1,16,256]{3,2,1,0:T(8,128)S(1)}, u32[]{:S(2)}, u32[]{:S(2)}) collective-permute-start(f32[5,1,16,256]{3,2,1,0:T(8,128)S(1)} %copy-done.20), channel_id=1, source_target_pairs={{2,0},{4,2},{6,4},{8,6},{10,8},{12,10},{14,12},{16,14},{18,16},{20... | collective-permute-start | bytes 245768 | tf_op jit(solution)/shard_map/ppermute | solution.py:28
  157.3 9.9 %collective-permute-start.8 = (f32[5,1,16,256]{3,2,1,0:T(8,128)S(1)}, f32[5,1,16,256]{3,2,1,0:T(8,128)S(1)}, u32[]{:S(2)}, u32[]{:S(2)}) collective-permute-start(f32[5,1,16,256]{3,2,1,0:T(8,128)S(1)} %get-tuple-element.449), channel_id=1, source_target_pairs={{0,2},{2,4},{4,6},{6,8},{8,10},{10,12},{12,14},{14,16},{16,18},{18... | collective-permute-start | bytes 245768 | tf_op jit(solution)/shard_map/ppermute | solution.py:27
  157.4 9.9 %collective-permute-start.9 = (f32[5,1,16,256]{3,2,1,0:T(8,128)S(1)}, f32[5,1,16,256]{3,2,1,0:T(8,128)S(1)}, u32[]{:S(2)}, u32[]{:S(2)}) collective-permute-start(f32[5,1,16,256]{3,2,1,0:T(8,128)S(1)} %get-tuple-element.450), channel_id=1, source_target_pairs={{2,0},{4,2},{6,4},{8,6},{10,8},{12,10},{14,12},{16,14},{18,16},{20... | collective-permute-start | bytes 245768 | tf_op jit(solution)/shard_map/ppermute | solution.py:28
  169.4 9.9 %collective-permute-start.12 = (f32[5,1,16,256]{3,2,1,0:T(8,128)S(1)}, f32[5,1,16,256]{3,2,1,0:T(8,128)S(1)}, u32[]{:S(2)}, u32[]{:S(2)}) collective-permute-start(f32[5,1,16,256]{3,2,1,0:T(8,128)S(1)} %get-tuple-element.437), channel_id=1, source_target_pairs={{0,2},{2,4},{4,6},{6,8},{8,10},{10,12},{12,14},{14,16},{16,18},{18... | collective-permute-start | bytes 245768 | tf_op jit(solution)/shard_map/ppermute | solution.py:27
  169.4 9.9 %collective-permute-start.13 = (f32[5,1,16,256]{3,2,1,0:T(8,128)S(1)}, f32[5,1,16,256]{3,2,1,0:T(8,128)S(1)}, u32[]{:S(2)}, u32[]{:S(2)}) collective-permute-start(f32[5,1,16,256]{3,2,1,0:T(8,128)S(1)} %get-tuple-element.438), channel_id=1, source_target_pairs={{2,0},{4,2},{6,4},{8,6},{10,8},{12,10},{14,12},{16,14},{18,16},{20... | collective-permute-start | bytes 245768 | tf_op jit(solution)/shard_map/ppermute | solution.py:28
  182.8 53.0 %collective-permute-start.16 = (f32[5,1,16,256]{3,2,1,0:T(8,128)}, f32[5,1,16,256]{3,2,1,0:T(8,128)S(1)}, u32[]{:S(2)}, u32[]{:S(2)}) collective-permute-start(f32[5,1,16,256]{3,2,1,0:T(8,128)} %get-tuple-element.425), channel_id=1, source_target_pairs={{0,2},{2,4},{4,6},{6,8},{8,10},{10,12},{12,14},{14,16},{16,18},{18... | collective-permute-start | bytes 245768 | tf_op jit(solution)/shard_map/ppermute | solution.py:27
  182.9 52.9 %collective-permute-start.17 = (f32[5,1,16,256]{3,2,1,0:T(8,128)}, f32[5,1,16,256]{3,2,1,0:T(8,128)S(1)}, u32[]{:S(2)}, u32[]{:S(2)}) collective-permute-start(f32[5,1,16,256]{3,2,1,0:T(8,128)} %get-tuple-element.426), channel_id=1, source_target_pairs={{2,0},{4,2},{6,4},{8,6},{10,8},{12,10},{14,12},{16,14},{18,16},{20... | collective-permute-start | bytes 245768 | tf_op jit(solution)/shard_map/ppermute | solution.py:28
  190.5 45.3 %collective-permute-start.18 = (f32[5,4,1,256]{3,2,1,0:T(1,128)S(1)}, f32[5,4,1,256]{3,2,1,0:T(1,128)S(1)}, u32[]{:S(2)}, u32[]{:S(2)}) collective-permute-start(f32[5,4,1,256]{3,2,1,0:T(1,128)S(1)} %get-tuple-element.424), channel_id=1, source_target_pairs={{0,1},{1,0},{2,3},{3,2},{4,5},{5,4},{6,7},{7,6},{8,9},{9,8},{10,11... | collective-permute-start | bytes 61448 | tf_op jit(solution)/shard_map/ppermute | solution.py:27
  190.5 45.3 %collective-permute-start.19 = (f32[5,4,1,256]{3,2,1,0:T(1,128)S(1)}, f32[5,4,1,256]{3,2,1,0:T(1,128)S(1)}, u32[]{:S(2)}, u32[]{:S(2)}) collective-permute-start(f32[5,4,1,256]{3,2,1,0:T(1,128)S(1)} %get-tuple-element.423), channel_id=1, source_target_pairs={{1,0},{0,1},{3,2},{2,3},{5,4},{4,5},{7,6},{6,7},{9,8},{8,9},{11,10... | collective-permute-start | bytes 61448 | tf_op jit(solution)/shard_map/ppermute | solution.py:28
  238.4 9.9 %collective-permute-start.20 = (f32[5,1,16,256]{3,2,1,0:T(8,128)S(1)}, f32[5,1,16,256]{3,2,1,0:T(8,128)S(1)}, u32[]{:S(2)}, u32[]{:S(2)}) collective-permute-start(f32[5,1,16,256]{3,2,1,0:T(8,128)S(1)} %get-tuple-element.413), channel_id=1, source_target_pairs={{0,2},{2,4},{4,6},{6,8},{8,10},{10,12},{12,14},{14,16},{16,18},{18... | collective-permute-start | bytes 245768 | tf_op jit(solution)/shard_map/ppermute | solution.py:27
  238.5 9.9 %collective-permute-start.21 = (f32[5,1,16,256]{3,2,1,0:T(8,128)S(1)}, f32[5,1,16,256]{3,2,1,0:T(8,128)S(1)}, u32[]{:S(2)}, u32[]{:S(2)}) collective-permute-start(f32[5,1,16,256]{3,2,1,0:T(8,128)S(1)} %get-tuple-element.414), channel_id=1, source_target_pairs={{2,0},{4,2},{6,4},{8,6},{10,8},{12,10},{14,12},{16,14},{18,16},{20... | collective-permute-start | bytes 245768 | tf_op jit(solution)/shard_map/ppermute | solution.py:28
  245.9 1.7 collective-permute-start.23
  250.7 78.2 %all-to-all-start.2 = ((f32[128,1,1,4,3,512]{5,3,4,2,1,0:T(4,128)}), f32[128,1,1,4,3,512]{5,3,4,2,1,0:T(4,128)}, u32[]{:S(2)}, u32[]{:S(2)}) async-start(f32[128,1,1,4,3,512]{5,3,4,2,1,0:T(4,128)} %copy.1258), calls=%async_computation.2 | async-start | bytes 6291456 | tf_op jit(solution)/shard_map/all_to_all | solution.py:62
  280.7 12.2 %collective-permute-start.27 = (f32[2,8,8,128]{3,1,2,0:T(8,128)S(1)}, f32[2,8,8,128]{3,1,2,0:T(8,128)S(1)}, u32[]{:S(2)}, u32[]{:S(2)}) collective-permute-start(f32[2,8,8,128]{3,1,2,0:T(8,128)S(1)} %pad_maximum_fusion.67), channel_id=1, source_target_pairs={{0,127},{1,0},{2,1},{3,2},{4,3},{5,4},{6,5},{7,6},{8,7},{9,8},{10,... | collective-permute-start | bytes 196616 | tf_op jit(solution)/shard_map/ppermute | solution.py:41
  287.7 14.6 %collective-permute-start.26 = (f32[2,8,8,128]{3,1,2,0:T(8,128)S(1)}, f32[2,8,8,128]{3,1,2,0:T(8,128)S(1)}, u32[]{:S(2)}, u32[]{:S(2)}) collective-permute-start(f32[2,8,8,128]{3,1,2,0:T(8,128)S(1)} %pad_maximum_fusion.66), channel_id=1, source_target_pairs={{0,1},{1,2},{2,3},{3,4},{4,5},{5,6},{6,7},{7,8},{8,9},{9,10},{10,1... | collective-permute-start | bytes 196616 | tf_op jit(solution)/shard_map/ppermute | solution.py:41
  306.6 2.0 collective-permute-start.29
  306.7 9.2 %collective-permute-start.28 = (f32[2,8,8,128]{3,2,1,0:T(8,128)S(1)}, f32[2,8,8,128]{3,2,1,0:T(8,128)S(1)}, u32[]{:S(2)}, u32[]{:S(2)}) collective-permute-start(f32[2,8,8,128]{3,2,1,0:T(8,128)S(1)} %pad_maximum_fusion.68), channel_id=1, source_target_pairs={{0,1},{1,2},{2,3},{3,4},{4,5},{5,6},{6,7},{7,8},{8,9},{9,10},{10,1... | collective-permute-start | bytes 196616 | tf_op jit(solution)/shard_map/ppermute | solution.py:41
  318.2 4.0 %collective-permute-start.31 = (f32[2,8,8,128]{3,1,2,0:T(8,128)S(1)}, f32[2,8,8,128]{3,1,2,0:T(8,128)S(1)}, u32[]{:S(2)}, u32[]{:S(2)}) collective-permute-start(f32[2,8,8,128]{3,1,2,0:T(8,128)S(1)} %pad_maximum_fusion.71), channel_id=1, source_target_pairs={{0,127},{1,0},{2,1},{3,2},{4,3},{5,4},{6,5},{7,6},{8,7},{9,8},{10,... | collective-permute-start | bytes 196616 | tf_op jit(solution)/shard_map/ppermute | solution.py:41
  318.5 9.2 %collective-permute-start.30 = (f32[2,8,8,128]{3,1,2,0:T(8,128)S(1)}, f32[2,8,8,128]{3,1,2,0:T(8,128)S(1)}, u32[]{:S(2)}, u32[]{:S(2)}) collective-permute-start(f32[2,8,8,128]{3,1,2,0:T(8,128)S(1)} %pad_maximum_fusion.70), channel_id=1, source_target_pairs={{0,1},{1,2},{2,3},{3,4},{4,5},{5,6},{6,7},{7,8},{8,9},{9,10},{10,1... | collective-permute-start | bytes 196616 | tf_op jit(solution)/shard_map/ppermute | solution.py:41
  350.3 3.2 collective-permute-start.33
  351.6 9.2 %collective-permute-start.32 = (f32[2,8,8,128]{3,2,1,0:T(8,128)S(1)}, f32[2,8,8,128]{3,2,1,0:T(8,128)S(1)}, u32[]{:S(2)}, u32[]{:S(2)}) collective-permute-start(f32[2,8,8,128]{3,2,1,0:T(8,128)S(1)} %pad_maximum_fusion.72), channel_id=1, source_target_pairs={{0,1},{1,2},{2,3},{3,4},{4,5},{5,6},{6,7},{7,8},{8,9},{9,10},{10,1... | collective-permute-start | bytes 196616 | tf_op jit(solution)/shard_map/ppermute | solution.py:41
  365.0 2.0 collective-permute-start.35
  365.1 9.5 %collective-permute-start.34 = (f32[2,8,8,128]{3,2,1,0:T(8,128)S(1)}, f32[2,8,8,128]{3,2,1,0:T(8,128)S(1)}, u32[]{:S(2)}, u32[]{:S(2)}) collective-permute-start(f32[2,8,8,128]{3,2,1,0:T(8,128)S(1)} %pad_maximum_fusion.74), channel_id=1, source_target_pairs={{0,1},{1,2},{2,3},{3,4},{4,5},{5,6},{6,7},{7,8},{8,9},{9,10},{10,1... | collective-permute-start | bytes 196616 | tf_op jit(solution)/shard_map/ppermute | solution.py:41
  (41 other events, 273.8 us)
where the time goes:
time: 386 us; the launch traced here: 378 us
  local copies, waits for them, and re-layouts  120 us (31%)
  starting transfers between devices  92.4 us (24%)
  waiting for transfers between devices  79.3 us (21%)
  other arithmetic  52.3 us (14%)
  matrix products  29.5 us (8%)
  between operations  4.97 us (1%)
    scatter x2, local copies, waits for them, and re-layouts, pack_partials(): jnp.zeros((devices * CAP, 3, node_count), jnp.float32).at[slot_index]  59.7 us
    ppermute x12, starting transfers between devices, with_halo(): lax.ppermute(initial, axis, [(b, a) for a, b in up])  47 us
    ppermute x12, waiting for transfers between devices, from_behind(): lax.ppermute(value, axis, [(i, (i + by) % length) for i in range(length)])  42.2 us
    ppermute x12, waiting for transfers between devices, with_halo(): lax.ppermute(last, axis, up)  36 us
    all_to_all x3, starting transfers between devices, joined_exchange(): parts = lax.all_to_all(parts, axis, split_axis=0, concat_axis=0, tiled=True)  23.7 us
    dot_general x36, matrix products, derivative(): jnp.einsum(forms[direction], derive, values, precision=MAXIMUM_DEGREE)  22.3 us
    ppermute x12, starting transfers between devices, from_behind(): lax.ppermute(value, axis, [(i, (i + by) % length) for i in range(length)])  18.4 us
    scatter-add x2, other arithmetic, gather_sources(): jax.ops.segment_sum(flat_rows, row_targets, num_segments=local_count + 1)  14.5 us
  transfers between devices with their start and end apart: 39, of which 17 were waited for; matrix products, arithmetic and copies ran while one was open for 31% of the time, Pallas kernels for 0%

commit v1 on v0

v1 whole, which is shorter than its diff:
```python
import jax
import jax.numpy as jnp
import numpy as np
from jax import lax
from jax.experimental import pallas as pl
from jax.experimental.pallas import tpu as pltpu
from jax.sharding import PartitionSpec as P


NP = 8
EZ = 16
CAP = 4
GAMMA = 1.4
DT_FLOW = 0.08
DT_WAVE = 0.01
F32 = jnp.float32
BF16 = jnp.bfloat16
AXES = ("flow", "group")
VMEM_LIMIT = 26 * 2**20
WHOLE_VMEM = 58 * 2**20


def legendre_pair(nodes, degree):
    previous = np.ones(nodes.shape[0])
    current = nodes * 1.0
    for order in range(2, degree + 1):
        previous, current = (
            current,
            ((2 * order - 1) * nodes * current - (order - 1) * previous) / order,
        )
    return (previous, current)


def lobatto(point_count):
    degree = point_count - 1
    nodes = -np.cos(np.pi * np.arange(point_count) / degree)
    for _ in range(60):
        previous, current = legendre_pair(nodes, degree)
        nodes = nodes - (nodes * current - previous) / (point_count * current)
    previous, values = legendre_pair(nodes, degree)
    weights = 2.0 / (degree * (degree + 1) * values**2)
    identity = np.eye(point_count)
    differ = nodes[:, None] - nodes[None, :] + identity
    matrix = values[:, None] / values[None, :] / differ * (1.0 - identity)
    matrix[0, 0] = -degree * (degree + 1) / 4.0
    matrix[-1, -1] = degree * (degree + 1) / 4.0
    return (matrix.astype(np.float32), float(weights[0]))


MATRIX, END_WEIGHT = lobatto(NP)
LIFT = 0.5 / END_WEIGHT


def sds(*shape, dtype=F32):
    return jax.ShapeDtypeStruct(shape, dtype)


def call(body, out_shape, flops, scratch=(), specs=None, out_specs=None, limit=VMEM_LIMIT):
    kinds = {"s": pltpu.SMEM, "v": pltpu.VMEM, "h": pltpu.HBM}
    extra = {}
    if specs is not None:
        extra["in_specs"] = [pl.BlockSpec(memory_space=kinds[k]) for k in specs]
    if out_specs is not None:
        extra["out_specs"] = pl.BlockSpec(memory_space=kinds[out_specs])
    return pl.pallas_call(
        body,
        out_shape=out_shape,
        scratch_shapes=list(scratch),
        cost_estimate=pl.CostEstimate(flops=flops, bytes_accessed=4_000_000, transcendentals=0),
        compiler_params=pltpu.CompilerParams(vmem_limit_bytes=limit),
        **extra,
    )


def halves(value):
    high = value.astype(BF16)
    return high, (value - high.astype(F32)).astype(BF16)


def dot(left, right, dims=((1,), (0,))):
    return lax.dot_general(left, right, (dims, ((), ())), preferred_element_type=F32)


def fields_body(rho_ref, vel_ref, pre_ref, f_ref):
    rho = rho_ref[...]
    v = [vel_ref[d] for d in range(3)]
    kinetic = v[0] * v[0] + v[1] * v[1] + v[2] * v[2]
    f_ref[0] = rho
    for d in range(3):
        f_ref[1 + d] = rho * v[d]
    f_ref[4] = pre_ref[...] / (GAMMA - 1.0) + 0.5 * rho * kinetic


def slots_body(me_ref, mb_ref, mt_ref, sel_ref, lab_ref, *, blocks):
    entries = me_ref.shape[1]
    devices = lab_ref.shape[0]
    shape = (devices, entries)
    owner = me_ref[...] >> 7
    place = (me_ref[...] & 127).astype(F32)
    lane = lax.broadcasted_iota(jnp.int32, shape, 0)
    owned = (lane == owner).astype(F32)
    before = lax.broadcasted_iota(jnp.int32, (entries, entries), 0) < lax.broadcasted_iota(
        jnp.int32, (entries, entries), 1
    )
    ahead = dot(owned.astype(BF16), before.astype(F32).astype(BF16))
    rank = jnp.sum(owned * ahead, axis=0, keepdims=True)
    combo = (lane == mt_ref[...] * blocks + mb_ref[...]).astype(F32).astype(BF16)
    for s in range(CAP):
        mine = jnp.where(rank == float(s), owned, 0.0).astype(BF16)
        pick = dot(mine, combo, ((1,), (1,))).astype(BF16)
        half = devices // 2
        for h in range(2):
            at = (h * CAP + s) * half
            for side in range(2):
                sel_ref[at : at + half, side * 128 : (side + 1) * 128] = pick[
                    h * half : (h + 1) * half
                ]
    spread = jnp.where(lane.astype(F32) == rank, place + 1.0, 0.0).astype(BF16)
    lab_ref[...] = dot(owned.astype(BF16), spread, ((1,), (1,)))


def pack_body(
    flag,
    own_ref,
    part_ref,
    even_ref,
    odd_ref,
    tab_hbm,
    sel_ref,
    lab_ref,
    out_hbm,
    src,
    mp,
    tab,
    out,
    sems,
):
    planes, rows, width = own_ref.shape[1:]
    tables, nodes = tab.shape[0], tab.shape[1]
    blocks = 128 // tables
    loads = [pltpu.make_async_copy(tab_hbm.at[t], tab.at[t], sems.at[t]) for t in range(tables)]
    for load in loads:
        load.start()
    low_flow = flag[0] == 0

    def turn(value, by):
        return pltpu.roll(value, by % width, 1)

    for x in range(planes):
        v = [own_ref[d, x] for d in range(3)]

        def along_x(d):
            if x == 0:
                below = jnp.where(low_flow, odd_ref[d, 0], even_ref[d, 0])
            else:
                below = own_ref[d, x - 1]
            if x == planes - 1:
                above = jnp.where(low_flow, even_ref[d, 0], odd_ref[d, 0])
            else:
                above = own_ref[d, x + 1]
            return 0.5 * (above - below)

        def along_y(d):
            both = jnp.concatenate([v[d], part_ref[d, x]], axis=0)
            up = pltpu.roll(both, 2 * rows - 1, 0)[:rows]
            down = pltpu.roll(both, 1, 0)[:rows]
            return 0.5 * (up - down)

        def along_z(d):
            return 0.5 * (turn(v[d], -1) - turn(v[d], 1))

        curl = (
            along_y(2) - along_z(1),
            along_z(0) - along_x(2),
            along_x(1) - along_y(0),
        )
        for c in range(3):
            a, b = (c + 1) % 3, (c + 2) % 3
            base = (c * planes + x) * rows
            lamb = curl[a] * v[b] - curl[b] * v[a]
            src[0, base : base + rows, :] = lamb[:, :128]
            src[1, base : base + rows, :] = lamb[:, 128:]
    count = 3 * blocks
    split = [
        halves(src[half, pl.ds(start, count, stride=2), :])
        for start in range(2)
        for half in range(2)
    ]
    left = jnp.concatenate(
        [
            jnp.concatenate([h for h, _ in split], axis=1),
            jnp.concatenate([l for _, l in split], axis=1),
        ],
        axis=0,
    )
    for t in range(tables):
        loads[t].wait()
        high, low = halves(tab[t])
        wide = dot(left, high)
        mapped = wide[:count] + wide[count:] + dot(left[:count], low)
        for c in range(3):
            high, low = halves(mapped[c * blocks : (c + 1) * blocks])
            mp[c, t * blocks : (t + 1) * blocks, :] = high
            mp[c, 128 + t * blocks : 128 + (t + 1) * blocks, :] = low
    devices = lab_ref.shape[0]
    half = devices // 2
    groups = nodes // 128
    stride = 3 * groups * CAP + 1
    out[pl.ds(stride - 1, devices, stride=stride), :] = lab_ref[...]
    stores = []
    for h in range(2):
        for c in range(3):
            filled = dot(sel_ref[h * CAP * half : (h + 1) * CAP * half, :], mp[c])
            for s in range(CAP):
                for m in range(groups):
                    row = h * half * stride + CAP * (c * groups + m) + s
                    out[pl.ds(row, half, stride=stride), :] = filled[
                        s * half : (s + 1) * half, m * 128 : (m + 1) * 128
                    ]
        part = pl.ds(h * half * stride, half * stride)
        store = pltpu.make_async_copy(out.at[part], out_hbm.at[part], sems.at[tables + h])
        store.start()
        stores.append(store)
    for store in stores:
        store.wait()


def primitives(s):
    inverse = 1.0 / s[0]
    v = [s[1 + d] * inverse for d in range(3)]
    kinetic = v[0] * v[0] + v[1] * v[1] + v[2] * v[2]
    p = (GAMMA - 1.0) * (s[4] - 0.5 * s[0] * kinetic)
    return v, p, jnp.sqrt(GAMMA * p * inverse)


def flux_of(s, v, p, d, k):
    if k == 0:
        return s[1 + d]
    if k == 4:
        return (s[4] + p) * v
    product = s[k] * v
    return product + p if k == 1 + d else product


def flow_stage(src, base, dst, prim, first, last, weights, shift=0, rows=None):
    a_weight, b_weight = weights

    def prepare(x, carry):
        v, p, sound = primitives([src[k, x] for k in range(5)])
        for d in range(3):
            prim[d, x] = v[d]
        prim[3, x] = p
        prim[4, x] = sound
        return carry

    lax.fori_loop(first - 1, last + 1, prepare, 0)

    def advance(x, carry):
        s = [src[k, x] for k in range(5)]
        total = []
        sound = prim[4, x]
        p = prim[3, x]
        up = [src[k, x + 1] for k in range(5)]
        down = [src[k, x - 1] for k in range(5)]
        v, vu, vd = prim[0, x], prim[0, x + 1], prim[0, x - 1]
        speed = jnp.abs(v) + sound
        fast_u = jnp.maximum(speed, jnp.abs(vu) + prim[4, x + 1])
        fast_d = jnp.maximum(speed, jnp.abs(vd) + prim[4, x - 1])
        pu, pd = prim[3, x + 1], prim[3, x - 1]
        for k in range(5):
            jump = fast_u * (up[k] - s[k]) - fast_d * (s[k] - down[k])
            total.append(flux_of(up, vu, pu, 0, k) - flux_of(down, vd, pd, 0, k) - jump)
        for d, axis in ((1, 0), (2, 1)):
            size = s[0].shape[axis]
            v = prim[d, x]
            speed = jnp.abs(v) + sound
            fast = jnp.maximum(speed, pltpu.roll(speed, size - 1, axis))
            for k in range(5):
                flux = flux_of(s, v, p, d, k)
                face = flux + pltpu.roll(flux, size - 1, axis)
                face = face - fast * (pltpu.roll(s[k], size - 1, axis) - s[k])
                total[k] = total[k] + (face - pltpu.roll(face, 1, axis))
        for k in range(5):
            value = b_weight * s[k] - (0.5 * DT_FLOW * b_weight) * total[k]
            if a_weight is not None:
                value = value + a_weight * base[k, x]
            if rows is not None:
                value = value[:rows]
            dst[k, x - shift] = value
        return carry

    lax.fori_loop(first, last, advance, 0)


STAGES = ((None, 1.0), (0.75, 0.25), (1.0 / 3.0, 2.0 / 3.0))


def assemble(flag, mine, other, s0):
    own, _, _ = mine
    planes, rows = own.shape[1], own.shape[2]
    above = jnp.where(flag[0] == 0, 2 * planes, 0)
    starts = (planes, above, 2 * planes - above)
    for start, a, b in zip(starts, mine, other):
        for i in range(planes):
            for k in range(5):
                s0[k, start + i, :rows] = a[k, i]
                s0[k, start + i, rows:] = b[k, i]


def first_flow_body(flag, *refs):
    mine, other = refs[:3], refs[3:6]
    new_own, new_part, own_ref, part_ref, lo_ref, hi_ref = refs[6:12]
    s0, s1, s2, prim = refs[12:]
    planes, rows = mine[0].shape[1], mine[0].shape[2]
    assemble(flag, mine, other, s0)
    wide = 3 * planes
    flow_stage(s0, None, s1, prim, 1, wide - 1, STAGES[0])
    flow_stage(s1, s0, s2, prim, 2, wide - 2, STAGES[1])
    flow_stage(s2, s0, s1, prim, 3, wide - 3, STAGES[2])
    for i in range(-1, planes + 1):
        x = planes + i
        inverse = 1.0 / s1[0, x]
        v = [s1[1 + d, x] * inverse for d in range(3)]
        for d in range(3):
            if i == -1:
                lo_ref[d, 0] = v[d][:rows]
            elif i == planes:
                hi_ref[d, 0] = v[d][:rows]
            else:
                own_ref[d, i] = v[d][:rows]
                part_ref[d, i] = v[d][rows:]
        if 0 <= i < planes:
            for k in range(5):
                new_own[k, i] = s1[k, x, :rows]
                new_part[k, i] = s1[k, x, rows:]


def last_flow_body(flag, *refs):
    mine, other, out_ref = refs[:3], refs[3:6], refs[6]
    s0, s1, s2, prim = refs[7:]
    planes, rows = mine[0].shape[1], mine[0].shape[2]
    assemble(flag, mine, other, s0)
    wide = 3 * planes
    flow_stage(s0, None, s1, prim, 2, wide - 2, STAGES[0])
    flow_stage(s1, s0, s2, prim, 3, wide - 3, STAGES[1])
    flow_stage(s2, s0, out_ref, prim, planes, 2 * planes, STAGES[2], shift=planes, rows=rows)


def derive(values):
    half = NP // 2
    even = [values[i] + values[NP - 1 - i] for i in range(half)]
    odd = [values[i] - values[NP - 1 - i] for i in range(half)]
    tops, bottoms = [], []
    for a in range(half):
        plus = minus = None
        for i in range(half):
            ce = 0.5 * float(MATRIX[a, i] + MATRIX[a, NP - 1 - i])
            co = 0.5 * float(MATRIX[a, i] - MATRIX[a, NP - 1 - i])
            te, to = ce * even[i], co * odd[i]
            plus = te if plus is None else plus + te
            minus = to if minus is None else minus + to
        tops.append(plus + minus)
        bottoms.append(minus - plus)
    return tops + bottoms[::-1]


def along_middle(ps, us, lanes):
    p = derive(ps)
    below, above = (ps[-1], -ps[0]) if us is None else (ps[-1] + us[-1], us[0] - ps[0])
    own_low, own_high = (ps[0], -ps[-1]) if us is None else (ps[0] + us[0], us[-1] - ps[-1])
    low = LIFT * (pltpu.roll(below, EZ, 1) - own_low)
    high = LIFT * (pltpu.roll(above, lanes - EZ, 1) - own_high)
    dp = [None] * NP if us is None else [-u for u in derive(us)]
    du = [-value for value in p]
    dp[0] = low if dp[0] is None else dp[0] + low
    dp[-1] = -high if dp[-1] is None else dp[-1] - high
    du[0] = du[0] + low
    du[-1] = du[-1] + high
    return dp, du


def inner_maker(coef, lanes):
    lane = lax.broadcasted_iota(jnp.int32, (NP, lanes), 1)
    row = lax.broadcasted_iota(jnp.int32, (NP, lanes), 0)
    firsts = (lane & (EZ - 1)) == 0
    lasts = (lane & (EZ - 1)) == EZ - 1
    is_low = row == 0
    lift_u = jnp.where(is_low | (row == NP - 1), LIFT, 0.0)
    lift_p = jnp.where(is_low, LIFT, jnp.where(row == NP - 1, -LIFT, 0.0))

    def slope(value):
        total = coef[0] * value
        for k in range(1, NP):
            total = total + coef[k] * pltpu.roll(value, NP - k, 0)
        return total

    def jump_of(p, u):
        up, down = (p, -p) if u is None else (u + p, u - p)
        edge = jnp.where(is_low, pltpu.roll(up, 1, 0), pltpu.roll(down, NP - 1, 0))
        from_low = jnp.where(firsts, pltpu.roll(edge, lanes + 1 - EZ, 1), pltpu.roll(edge, 1, 1))
        from_high = jnp.where(
            lasts, pltpu.roll(edge, EZ - 1, 1), pltpu.roll(edge, lanes - 1, 1)
        )
        return jnp.where(is_low, from_low - up, from_high - down)

    def both(p, u, want_u=True):
        jump = jump_of(p, u)
        dp = lift_p * jump if u is None else lift_p * jump - slope(u)
        return dp, (lift_u * jump - slope(p)) if want_u else None

    return both


def local_rate(s, r, coef, forcing=None):
    lanes = s.shape[-1]

    def first(j, carry):
        p = derive([s[0, i, j] for i in range(NP)])
        u = derive([s[1, i, j] for i in range(NP)])
        for i in range(NP):
            r[0, i, j] = -u[i]
            r[1, i, j] = -p[i] if forcing is None else forcing[0, i, j] - p[i]
        return carry

    lax.fori_loop(0, NP, first, 0)
    inner = inner_maker(coef, lanes)

    def second(i, carry):
        ps = [s[0, i, j] for j in range(NP)]
        dp, du = along_middle(ps, [s[2, i, j] for j in range(NP)], lanes)
        for j in range(NP):
            dq, dw = inner(ps[j], s[3, i, j])
            r[0, i, j] = r[0, i, j] + (dp[j] + dq)
            r[2, i, j] = du[j] if forcing is None else forcing[1, i, j] + du[j]
            r[3, i, j] = dw if forcing is None else forcing[2, i, j] + dw
        return carry

    lax.fori_loop(0, NP, second, 0)


def each(function):
    def body(i, carry):
        function(i)
        return carry

    lax.fori_loop(0, NP, body, 0)


def lifts(s, j, flag, even, odd):
    low_core = flag[1] == 0
    from_low = jnp.where(low_core, odd[j], even[j])
    from_high = jnp.where(low_core, even[j], odd[j])
    low = LIFT * (from_low - (s[1, 0, j] + s[0, 0, j]))
    high = LIFT * (from_high - (s[1, NP - 1, j] - s[0, NP - 1, j]))
    return low, high


def put_ends(flag, up, down, even, odd):
    low_core = flag[1] == 0
    even[...] = jnp.where(low_core, up, down)
    odd[...] = jnp.where(low_core, down, up)


def ends_body(flag, w, even, odd):
    put_ends(flag, w[0, NP - 1] + w[1, NP - 1], w[1, 0] - w[0, 0], even, odd)


def inner_body(w, coef, r):
    local_rate(w, r, coef)


def unpack_body(arrived, f, wide):
    groups = f.shape[0] // 128
    stride = groups * CAP + 1
    devices = arrived.shape[0] // stride
    elements = f.shape[-1]
    labels = arrived[pl.ds(stride - 1, devices, stride=stride), :].T
    row = lax.broadcasted_iota(jnp.int32, (elements, devices), 0).astype(F32)
    pick = jnp.concatenate(
        [(row == labels[s : s + 1] - 1.0).astype(F32).astype(BF16) for s in range(CAP)], axis=1
    )
    for g in range(groups):
        for s in range(CAP):
            part = arrived[pl.ds(CAP * g + s, devices, stride=stride), :]
            high, low = halves(part)
            wide[g % 2, s * devices : (s + 1) * devices, 0:128] = high
            wide[g % 2, s * devices : (s + 1) * devices, 128:256] = low
        both = dot(pick, wide[g % 2])
        f[g * 128 : (g + 1) * 128, :] = (both[:, :128] + both[:, 128:]).T


def first_stage_body(flag, w, r0, f, q_even, q_odd, coef, s1, even, odd):
    lanes = w.shape[-1]

    def add(i):
        for k in range(4):
            rate = r0[k, i] if k == 0 else r0[k, i] + f[k - 1, i]
            s1[k, i] = w[k, i] + DT_WAVE * rate

    each(add)

    def lift(j):
        low, high = lifts(w, j, flag, q_even, q_odd)
        low, high = DT_WAVE * low, DT_WAVE * high
        last = NP - 1
        s1[0, 0, j] = s1[0, 0, j] + low
        s1[1, 0, j] = s1[1, 0, j] + low
        s1[0, last, j] = s1[0, last, j] - high
        s1[1, last, j] = s1[1, last, j] + high

    each(lift)
    inner = inner_maker(coef, lanes)
    low_core = flag[1] == 0
    now, then = [], []
    for i, sign in ((NP - 1, 1.0), (0, -1.0)):
        ps = [s1[0, i, j] for j in range(NP)]
        dp, _ = along_middle(ps, [s1[2, i, j] for j in range(NP)], lanes)
        now_rows, then_rows = [], []
        for j in range(NP):
            dq, _ = inner(ps[j], s1[3, i, j], want_u=False)
            rate_p = dp[j] + dq
            rate_u = f[0, i, j]
            for m in range(NP):
                c = float(MATRIX[i, m])
                if c != 0.0:
                    rate_p = rate_p - c * s1[1, m, j]
                    rate_u = rate_u - c * s1[0, m, j]
            u = s1[1, i, j]
            next_p = 0.75 * w[0, i, j] + 0.25 * (ps[j] + DT_WAVE * rate_p)
            next_u = 0.75 * w[1, i, j] + 0.25 * (u + DT_WAVE * rate_u)
            now_rows.append(u + sign * ps[j])
            then_rows.append(next_u + sign * next_p)
        now.append(now_rows)
        then.append(then_rows)
    for j in range(NP):
        for slot, (up, down) in enumerate((now, then)):
            even[slot, j] = jnp.where(low_core, up[j], down[j])
            odd[slot, j] = jnp.where(low_core, down[j], up[j])


def middle_stage_body(w, s1, f, coef, s2, r2, r1):
    local_rate(s1, r1, coef, f)

    def add(i):
        for k in range(4):
            s2[k, i] = 0.75 * w[k, i] + 0.25 * (s1[k, i] + DT_WAVE * r1[k, i])

    each(add)
    local_rate(s2, r2, coef, f)


def last_stage_body(flag, w, s1, s2, r2, q_even, q_odd, coef, out, even, odd, s, r):
    lanes = w.shape[-1]
    last = NP - 1

    def first(j):
        low, high = lifts(s1, j, flag, q_even.at[0], q_odd.at[0])
        low, high = (0.25 * DT_WAVE) * low, (0.25 * DT_WAVE) * high
        s[0, j] = low
        s[1, j] = -high
        new = (s2[0, 0, j] + low, s2[1, 0, j] + low, s2[0, last, j] - high, s2[1, last, j] + high)
        low_core = flag[1] == 0
        from_low = jnp.where(low_core, q_odd[1, j], q_even[1, j])
        from_high = jnp.where(low_core, q_even[1, j], q_odd[1, j])
        lift_low = LIFT * (from_low - (new[1] + new[0]))
        lift_high = LIFT * (from_high - (new[3] - new[2]))
        for i in range(NP):
            a, b = float(MATRIX[i, 0]), float(MATRIX[i, last])
            p = r2[0, i, j] - a * low - b * high
            u = r2[1, i, j] - a * low + b * high
            if i == 0:
                p, u = p + lift_low, u + lift_low
            if i == last:
                p, u = p - lift_high, u + lift_high
            r[0, i, j] = p
            r[1, i, j] = u

    each(first)
    third = 1.0 / 3.0

    def close(k, i, j, state, rate):
        out[k, i, j] = w[k, i, j] * third + (2.0 * third) * (state + DT_WAVE * rate)

    def inside(i, carry):
        for j in range(NP):
            for k in range(4):
                rate = r[k, i, j] if k < 2 else r2[k, i, j]
                close(k, i, j, s2[k, i, j], rate)
        return carry

    lax.fori_loop(1, last, inside, 0)
    inner = inner_maker(coef, lanes)
    for side, i in ((0, 0), (1, last)):
        ps = [s[side, j] for j in range(NP)]
        dp, du = along_middle(ps, None, lanes)
        for j in range(NP):
            dq, dw = inner(ps[j], None)
            rate = r[0, i, j] + dq
            if dp[j] is not None:
                rate = rate + dp[j]
            close(0, i, j, s2[0, i, j] + ps[j], rate)
            change = ps[j] if side == 0 else -ps[j]
            close(1, i, j, s2[1, i, j] + change, r[1, i, j])
            close(2, i, j, s2[2, i, j], r2[2, i, j] + du[j])
            close(3, i, j, s2[3, i, j], r2[3, i, j] + dw)
    put_ends(flag, out[0, last] + out[1, last], out[1, 0] - out[0, 0], even, odd)


def trade(value, axis, odd):
    size = lax.axis_size(axis)
    pairs = []
    for i in range(odd, size + odd, 2):
        a, b = i % size, (i + 1) % size
        pairs += [(a, b), (b, a)]
    return lax.ppermute(value, axis, pairs)


def exchange_all(value):
    return lax.all_to_all(value, AXES, split_axis=0, concat_axis=0, tiled=True)


def advance(density, velocity, pressure, wave, tables, margin_element, margin_block, margin_table):
    planes, rows, width = density.shape
    lanes = wave.shape[-1]
    devices = lax.axis_size("flow") * lax.axis_size("group")
    kinds, nodes = tables.shape[:2]
    stride = 3 * CAP * nodes // 128 + 1
    blocks = planes * rows * width // nodes

    coef = np.stack([MATRIX[np.arange(NP), (np.arange(NP) + k) % NP] for k in range(NP)])
    coef = jnp.asarray(np.broadcast_to(coef[:, :, None], (NP, NP, lanes)).copy())
    odd_flow = lax.axis_index("flow") & 1
    flag = jnp.stack([odd_flow, lax.axis_index("group")]).astype(jnp.int32)
    first_flag = jnp.zeros((2,), jnp.int32)

    inward = (planes - 1) * (1 - odd_flow)
    v_even = trade(lax.dynamic_slice_in_dim(velocity, inward, 1, 1), "flow", 0)
    v_odd = trade(lax.dynamic_slice_in_dim(velocity, planes - 1 - inward, 1, 1), "flow", 1)
    v_part = trade(velocity, "group", 0)

    block = sds(5, planes, rows, width)
    fields = call(fields_body, block, 1_000_000, limit=WHOLE_VMEM)(density, velocity, pressure)

    def surround(own):
        even = trade(own, "flow", 0)
        return (own, even, trade(own, "flow", 1))

    def swap_rows(pieces):
        return [trade(p, "group", 0) for p in pieces]

    pieces = surround(fields)
    others = swap_rows(pieces)

    select, labels = call(
        lambda *refs: slots_body(*refs, blocks=blocks),
        (sds(CAP * devices, 256, dtype=BF16), sds(devices, 128)),
        1_000_000,
        limit=WHOLE_VMEM,
    )(margin_element, margin_block, margin_table)

    pack = call(
        pack_body,
        sds(devices * stride, 128),
        8_000_000,
        scratch=(
            pltpu.VMEM((2, 3 * planes * rows, 128), F32),
            pltpu.VMEM((3, 256, nodes), BF16),
            pltpu.VMEM(tables.shape, F32),
            pltpu.VMEM((devices * stride, 128), F32),
            pltpu.SemaphoreType.DMA((kinds + 2,)),
        ),
        specs="svvvvhvv",
        limit=WHOLE_VMEM,
        out_specs="h",
    )

    def send(which, *speeds):
        sent = pack(which, *speeds, tables, select, labels)
        sent = exchange_all(sent.reshape(devices, 1, stride * 128))
        return sent.reshape(devices * stride, 128)

    arrived_1 = send(flag, velocity, v_part, v_even, v_odd)

    speed = sds(3, planes, rows, width)
    thin = sds(3, 1, rows, width)
    wide = pltpu.VMEM((5, 3 * planes, 2 * rows, width), F32)
    new_own, new_part, own, part, low, high = call(
        first_flow_body,
        (block, block, speed, speed, thin, thin),
        60_000_000,
        scratch=[wide] * 4,
        specs="s" + 6 * "v",
    )(flag, *pieces, *others)
    arrived_2 = send(first_flag, own, part, high, low)
    pieces = surround(new_own)

    def finish_flow(pieces):
        return call(
            last_flow_body, block, 30_000_000, scratch=[wide] * 4, specs="s" + 6 * "v"
        )(flag, *pieces, new_part, *swap_rows(pieces[1:]))

    state = sds(*wave.shape)
    hold = pltpu.VMEM(wave.shape, F32)
    face = sds(NP, NP, lanes)
    pair = sds(2, NP, NP, lanes)
    inner = call(inner_body, state, 8_000_000)
    unpack = call(
        unpack_body,
        sds(3 * nodes, lanes),
        8_000_000,
        scratch=[pltpu.VMEM((2, CAP * devices, 256), BF16)],
    )
    first_stage = call(first_stage_body, (state, pair, pair), 4_000_000, specs="svvvvvv")
    middle_stage = call(middle_stage_body, (state, state), 16_000_000, scratch=[hold])
    last_stage = call(
        last_stage_body,
        (state, face, face),
        6_000_000,
        scratch=[pltpu.VMEM((2, NP, NP, lanes), F32), pltpu.VMEM((2,) + wave.shape[1:], F32)],
        specs="svvvvvvv",
    )

    def around(even, odd):
        return (trade(even, "group", 0), trade(odd, AXES, 1))

    ends = call(ends_body, (face, face), 100_000, specs="sv")(flag, wave)
    for turn, arrived in enumerate((arrived_1, arrived_2)):
        faces = around(*ends)
        rate = inner(wave, coef)
        forcing = unpack(arrived).reshape(3, *wave.shape[1:])
        s1, *ends = first_stage(flag, wave, rate, forcing, *faces, coef)
        faces = around(*ends)
        if turn == 0:
            pieces, _ = lax.optimization_barrier((pieces, ends))
            flow_state = finish_flow(pieces)
        s2, r2 = middle_stage(wave, s1, forcing, coef)
        wave, *ends = last_stage(flag, wave, s1, s2, r2, *faces, coef)
    return (flow_state, wave, forcing)


def solution(mesh):
    in_specs = (
        P("flow", "group", None),
        P(None, "flow", "group", None),
        P("flow", "group", None),
        P(None, None, None, None, AXES),
        P(),
        P(AXES, None),
        P(AXES, None),
        P(AXES, None),
    )
    out_specs = (
        P(None, "flow", "group", None),
        P(None, None, None, None, AXES),
        P(None, None, None, None, AXES),
    )
    return jax.shard_map(advance, mesh=mesh, in_specs=in_specs, out_specs=out_specs, check_vma=False)
```

time: 386 us -> 198 us (0.51); the launches traced: 378 us -> 197 us
  local copies, waits for them, and re-layouts: 120 us -> 12.5 us
  other arithmetic: 52.3 us -> 0.66 us
  Pallas kernels: 0 us -> 50.6 us
  starting transfers between devices: 92.4 us -> 46.1 us
  matrix products: 29.5 us -> 0 us
  waiting for transfers between devices: 79.3 us -> 86.4 us
  between operations: 4.97 us -> 0.92 us
    scatter x3 -> x0, local copies, waits for them, and re-layouts: 61.1 us -> none  [the longest x2 59.7 us: pack_partials(): jnp.zeros((devices * CAP, 3, node_count), jnp.float32).at[slot_index]]
    pallas_call x0 -> x17, Pallas kernels: none -> 50.6 us  [the longest x2 11.8 us: send(): sent = pack(which, *speeds, tables, select, labels)]
    ppermute x36 -> x20, starting transfers between devices: 68.8 us -> 31.3 us  [trade(): return lax.ppermute(value, axis, pairs)]
    dot_general x38 -> x0, matrix products: 29.5 us -> none  [the longest x36 22.3 us: derivative(): jnp.einsum(forms[direction], derive, values, precision=MAXIMUM_DEGREE)]
    another operation x58 -> x1, local copies, waits for them, and re-layouts: 17.8 us -> 0.52 us  [the longest x3 11.6 us: joined_exchange(): parts = parts.reshape(-1, *inside)]
    scatter-add x2 -> x0, other arithmetic: 14.5 us -> none  [gather_sources(): jax.ops.segment_sum(flat_rows, row_targets, num_segments=local_count + 1)]
    all_to_all x3 -> x2, starting transfers between devices: 23.7 us -> 14.9 us  [exchange_all(): return lax.all_to_all(value, AXES, split_axis=0, concat_axis=0, tiled=True)]
    slice x38 -> x0, local copies, waits for them, and re-layouts: 8.69 us -> none  [the longest x4 2.63 us: gather_sources(): jax.ops.segment_sum(flat_rows, row_targets, num_segments=local_count + 1)]
  transfers between devices with their start and end apart: 39 -> 22, of which waited for: 17 -> 6; matrix products, arithmetic and copies ran while one was open for 31% -> 1% of each run, Pallas kernels for 0% -> 22%
where the time goes in v1:
time: 198 us; the launch traced here: 197 us
  waiting for transfers between devices  86.4 us (44%)
  Pallas kernels  50.6 us (26%)
  starting transfers between devices  46.1 us (23%)
  local copies, waits for them, and re-layouts  12.5 us (6%)
    ppermute x20, waiting for transfers between devices, trade(): return lax.ppermute(value, axis, pairs)  86.4 us
    ppermute x20, starting transfers between devices, trade(): return lax.ppermute(value, axis, pairs)  31.3 us
    all_to_all x2, starting transfers between devices, exchange_all(): return lax.all_to_all(value, AXES, split_axis=0, concat_axis=0, tiled=True)  14.9 us
    pallas_call x2, Pallas kernels, send(): sent = pack(which, *speeds, tables, select, labels)  11.8 us
    unnamed x38, local copies, waits for them, and re-layouts  11.1 us
    pallas_call x1, Pallas kernels, advance(): call(first_flow_body, (block, block, speed, speed, thin, thin), 60000000,...  8.66 us
    pallas_call x1, Pallas kernels, finish_flow(): call(last_flow_body, block, 30000000, scratch=[wide] * 4, specs='s' + 6 *...  7.76 us
    pallas_call x2, Pallas kernels, advance(): s2, r2 = middle_stage(wave, s1, forcing, coef)  5.05 us
  transfers between devices with their start and end apart: 22, of which 6 were waited for; matrix products, arithmetic and copies ran while one was open for 1% of the time, Pallas kernels for 22%

profile of v1, /device:TPU:0, one launch (start us, length us, event | category | flops | bytes accessed | tf_op | source)
XLA Modules:
  0.0 197.2 jit_solution(3403290675144069772)
XLA Ops:
  1.6 2.1 %collective-permute-start.8 = (f32[3,1,16,256]{3,2,1,0:T(8,128)S(1)}, f32[3,1,16,256]{3,2,1,0:T(8,128)S(1)}, u32[]{:S(2)}, u32[]{:S(2)}) collective-permute-start(f32[3,1,16,256]{3,2,1,0:T(8,128)S(1)} %get-tuple-element.58), channel_id=1, source_target_pairs={{0,2},{2,0},{4,6},{6,4},{8,10},{10,8},{12,14},{14,12},{16,18},{18,... | collective-permute-start | bytes 147464 | tf_op jit(solution)/shard_map/ppermute | solution.py:615
  3.7 7.2 %collective-permute-start.9 = (f32[3,1,16,256]{3,2,1,0:T(8,128)S(1)}, f32[3,1,16,256]{3,2,1,0:T(8,128)S(1)}, u32[]{:S(2)}, u32[]{:S(2)}) collective-permute-start(f32[3,1,16,256]{3,2,1,0:T(8,128)S(1)} %get-tuple-element.57), channel_id=1, source_target_pairs={{2,4},{4,2},{6,8},{8,6},{10,12},{12,10},{14,16},{16,14},{18,20},{2... | collective-permute-start | bytes 147464 | tf_op jit(solution)/shard_map/ppermute | solution.py:615
  11.5 1.8 shard_map.115
  14.0 5.9 %shard_map.116 = f32[6272,128]{1,0:T(8,128)} custom-call(s32[2]{0:T(128)} %pad_add_fusion.flag, f32[3,4,16,256]{3,2,1,0:T(8,128)} %own_ref.1, f32[3,4,16,256]{3,2,1,0:T(8,128)} %copy-done.16, f32[3,1,16,256]{3,2,1,0:T(8,128)} %copy-done.17, f32[3,1,16,256]{3,2,1,0:T(8,128)} %copy-done.18, f32[4,512,512]{2,1,0:T(8,128)} %tab_hbm.3, ...), custom_call_target="tpu_custom_call" | custom-call | flops 8000000 | bytes 4000000 | tf_op jit(solution)/shard_map/pallas_call | solution.py:678
  20.0 9.0 %all-to-all-start = ((f32[128,1,6272]{2,1,0:T(1,128)}), f32[128,1,6272]{2,1,0:T(1,128)S(1)}, u32[]{:S(2)}, u32[]{:S(2)}) async-start(f32[128,1,6272]{2,1,0:T(1,128)} %bitcast.15), calls=%async_computation | async-start | bytes 6422528 | tf_op jit(solution)/shard_map/all_to_all | solution.py:619
  28.9 1.7 shard_map.112.refs_0_
  31.7 6.8 %collective-permute-start.1 = (f32[5,4,16,256]{3,2,1,0:T(8,128)}, f32[5,4,16,256]{3,2,1,0:T(8,128)S(1)}, u32[]{:S(2)}, u32[]{:S(2)}) collective-permute-start(f32[5,4,16,256]{3,2,1,0:T(8,128)} %shard_map.112.refs_0_), channel_id=1, source_target_pairs={{2,4},{4,2},{6,8},{8,6},{10,12},{12,10},{14,16},{16,14},{18,20},{2... | collective-permute-start | bytes 983048 | tf_op jit(solution)/shard_map/ppermute | solution.py:615
  38.6 33.6 %collective-permute-done.refs_1_ = f32[5,4,16,256]{3,2,1,0:T(8,128)S(1)} collective-permute-done((f32[5,4,16,256]{3,2,1,0:T(8,128)}, f32[5,4,16,256]{3,2,1,0:T(8,128)S(1)}, u32[]{:S(2)}, u32[]{:S(2)}) %collective-permute-start) | collective-permute-done | bytes 327712 | tf_op jit(solution)/shard_map/ppermute | solution.py:615
  72.2 6.1 %collective-permute-done.1.refs_2_ = f32[5,4,16,256]{3,2,1,0:T(8,128)S(1)} collective-permute-done((f32[5,4,16,256]{3,2,1,0:T(8,128)}, f32[5,4,16,256]{3,2,1,0:T(8,128)S(1)}, u32[]{:S(2)}, u32[]{:S(2)}) %collective-permute-start.1) | collective-permute-done | bytes 327712 | tf_op jit(solution)/shard_map/ppermute | solution.py:615
  78.3 1.6 collective-permute-done.4.refs_5_
  80.8 8.7 %shard_map.113 = (f32[5,4,16,256]{3,2,1,0:T(8,128)S(1)}, f32[5,4,16,256]{3,2,1,0:T(8,128)S(1)}, f32[3,4,16,256]{3,2,1,0:T(8,128)S(1)}, f32[3,4,16,256]{3,2,1,0:T...) custom-call(s32[2]{0:T(128)S(1)} %copy-done.15, f32[5,4,16,256]{3,2,1,0:T(8,128)S(1)} %copy-done.6, ...), custom_call_target="tpu_custom_call" | custom-call | flops 60000000 | bytes 4000000 | tf_op jit(solution)/shard_map/pallas_call | solution.py:687
  93.3 5.9 %shard_map.124 = f32[6272,128]{1,0:T(8,128)} custom-call(s32[2]{0:T(128)} %broadcast_1_flag.2.flag, f32[3,4,16,256]{3,2,1,0:T(8,128)} %copy-done.9, f32[3,4,16,256]{3,2,1,0:T(8,128)} %copy-done.10, f32[3,1,16,256]{3,2,1,0:T(8,128)} %copy-done.12, f32[3,1,16,256]{3,2,1,0:T(8,128)} %copy-done.11, f32[4,512,512]{2,1,0:T(8,128)} %tab_hbm.3, ...), custom_call_target="tpu_custom_call" | custom-call | flops 8000000 | bytes 4000000 | tf_op jit(solution)/shard_map/pallas_call | solution.py:678
  99.2 1.7 copy-done.1
  101.0 5.9 %all-to-all-start.1 = ((f32[128,1,6272]{2,1,0:T(1,128)}), f32[128,1,6272]{2,1,0:T(1,128)}, u32[]{:S(2)}, u32[]{:S(2)}) async-start(f32[128,1,6272]{2,1,0:T(1,128)} %bitcast.14), calls=%async_computation.1 | async-start | bytes 6422528 | tf_op jit(solution)/shard_map/all_to_all | solution.py:619
  106.9 1.1 collective-permute-start.5
  108.0 6.8 %collective-permute-start.6 = (f32[5,4,16,256]{3,2,1,0:T(8,128)S(1)}, f32[5,4,16,256]{3,2,1,0:T(8,128)}, u32[]{:S(2)}, u32[]{:S(2)}) collective-permute-start(f32[5,4,16,256]{3,2,1,0:T(8,128)S(1)} %get-tuple-element.37.refs_0_), channel_id=1, source_target_pairs={{2,4},{4,2},{6,8},{8,6},{10,12},{12,10},{14,16},{16,14},{18,20},{2... | collective-permute-start | bytes 983048 | tf_op jit(solution)/shard_map/ppermute | solution.py:615
  116.2 1.1 shard_map.114.r0
  117.3 1.9 copy-done.2
  119.2 1.1 shard_map.117
  120.3 35.7 %collective-permute-done.11.q_odd = f32[8,8,128]{2,1,0:T(8,128)S(1)} collective-permute-done((f32[8,8,128]{2,1,0:T(8,128)S(1)}, f32[8,8,128]{2,1,0:T(8,128)S(1)}, u32[]{:S(2)}, u32[]{:S(2)}) %collective-permute-start.11) | collective-permute-done | bytes 32800 | tf_op jit(solution)/shard_map/ppermute | solution.py:615
  156.0 1.1 shard_map.119
  158.4 2.5 %shard_map.121 = (f32[4,8,8,8,128]{4,3,2,1,0:T(8,128)S(1)}, f32[4,8,8,8,128]{4,3,2,1,0:T(8,128)S(1)}) custom-call(f32[4,8,8,8,128]{4,3,2,1,0:T(8,128)S(1)} %copy-done, f32[4,8,8,8,128]{4,3,2,1,0:T(8,128)S(1)} %get-tuple-element.41.s1, f32[3,8,8,8,128]{4,3,2,1,0:T(8,128)S(1)} %bitcast.13, f32[8,8,128]{2,1,0:T(8,128)S(1)} %copy-done.5), custom_call_target="tpu_custom_call" | custom-call | flops 16000000 | bytes 4000000 | tf_op jit(solution)/shard_map/pallas_call | solution.py:736
  161.0 6.0 %collective-permute-done.15.q_odd = f32[2,8,8,128]{3,2,1,0:T(8,128)S(1)} collective-permute-done((f32[2,8,8,128]{3,2,1,0:T(8,128)S(1)}, f32[2,8,8,128]{3,2,1,0:T(8,128)S(1)}, u32[]{:S(2)}, u32[]{:S(2)}) %collective-permute-start.15) | collective-permute-done | bytes 65568 | tf_op jit(solution)/shard_map/ppermute | solution.py:615
  167.0 1.7 shard_map.122
  169.3 1.1 shard_map.123.r0
  170.5 3.9 %shard_map.125 = f32[1536,128]{1,0:T(8,128)} custom-call(f32[6272,128]{1,0:T(8,128)} %bitcast.6.arrived), custom_call_target="tpu_custom_call" | custom-call | flops 8000000 | bytes 4000000 | tf_op jit(solution)/shard_map/pallas_call | solution.py:730
  174.4 3.3 %collective-permute-done.17.q_odd = f32[8,8,128]{2,1,0:T(8,128)S(1)} collective-permute-done((f32[8,8,128]{2,1,0:T(8,128)}, f32[8,8,128]{2,1,0:T(8,128)S(1)}, u32[]{:S(2)}, u32[]{:S(2)}) %collective-permute-start.17) | collective-permute-done | bytes 32800 | tf_op jit(solution)/shard_map/ppermute | solution.py:615
  178.3 1.1 copy-done.3
  181.4 3.4 %collective-permute-start.19 = (f32[2,8,8,128]{3,2,1,0:T(8,128)S(1)}, f32[2,8,8,128]{3,2,1,0:T(8,128)S(1)}, u32[]{:S(2)}, u32[]{:S(2)}) collective-permute-start(f32[2,8,8,128]{3,2,1,0:T(8,128)S(1)} %get-tuple-element.55), channel_id=1, source_target_pairs={{1,2},{2,1},{3,4},{4,3},{5,6},{6,5},{7,8},{8,7},{9,10},{10,9},{11,... | collective-permute-start | bytes 196616 | tf_op jit(solution)/shard_map/ppermute | solution.py:615
  184.8 7.8 %shard_map.120 = f32[5,4,16,256]{3,2,1,0:T(8,128)} custom-call(s32[2]{0:T(128)S(1)} %copy-done.15, f32[5,4,16,256]{3,2,1,0:T(8,128)S(1)} %get-tuple-element.37.refs_0_, f32[5,4,16,256]{3,2,1,0:T(8,128)} %collective-permute-done.5.refs_1_, f32[5,4,16,256]{3,2,1,0:T(8,128)} %collective-permute-done.6.refs_2_, f32[5,4,16,256]{3,2,1,0:T(8,128)S(1)} %copy-done.8, ...), custom_call_target="tpu_custom_call" | custom-call | flops 30000000 | bytes 4000000 | tf_op jit(solution)/shard_map/pallas_call | solution.py:698
  192.5 2.5 %shard_map.127 = (f32[4,8,8,8,128]{4,3,2,1,0:T(8,128)S(1)}, f32[4,8,8,8,128]{4,3,2,1,0:T(8,128)S(1)}) custom-call(f32[4,8,8,8,128]{4,3,2,1,0:T(8,128)S(1)} %get-tuple-element.44.w, f32[4,8,8,8,128]{4,3,2,1,0:T(8,128)S(1)} %get-tuple-element.51.s1, f32[3,8,8,8,128]{4,3,2,1,0:T(8,128)S(1)} %bitcast.11, f32[8,8,128]{2,1,0:T(8,128)S(1)} %copy-done.5), custom_call_target="tpu_custom_call" | custom-call | flops 16000000 | bytes 4000000 | tf_op jit(solution)/shard_map/pallas_call | solution.py:736
  195.1 2.1 %shard_map.128 = (f32[4,8,8,8,128]{4,3,2,1,0:T(8,128)}, f32[8,8,128]{2,1,0:T(8,128)}, f32[8,8,128]{2,1,0:T(8,128)}) custom-call(s32[2]{0:T(128)S(1)} %copy-done.15, f32[4,8,8,8,128]{4,3,2,1,0:T(8,128)S(1)} %get-tuple-element.44.w, f32[4,8,8,8,128]{4,3,2,1,0:T(8,128)S(1)} %get-tuple-element.51.s1, f32[4,8,8,8,128]{4,3,2,1,0:T(8,128)S(1)} %get-tuple-element.52.s2, ...), custom_call_target="tpu_custom_call" | custom-call | flops 6000000 | bytes 4000000 | tf_op jit(solution)/shard_map/pallas_call | solution.py:737
  (70 shorter events, 14.0 us)
Async XLA Ops:
  0.6 12.7 %collective-permute-start.7 = (f32[3,4,16,256]{3,2,1,0:T(8,128)}, f32[3,4,16,256]{3,2,1,0:T(8,128)S(1)}, u32[]{:S(2)}, u32[]{:S(2)}) collective-permute-start(f32[3,4,16,256]{3,2,1,0:T(8,128)} %own_ref.1), channel_id=1, source_target_pairs={{0,1},{1,0},{2,3},{3,2},{4,5},{5,4},{6,7},{7,6},{8,9},{9,8},{10,11... | collective-permute-start | bytes 589832 | tf_op jit(solution)/shard_map/ppermute | solution.py:615
  1.6 11.7 %collective-permute-start.8 = (f32[3,1,16,256]{3,2,1,0:T(8,128)S(1)}, f32[3,1,16,256]{3,2,1,0:T(8,128)S(1)}, u32[]{:S(2)}, u32[]{:S(2)}) collective-permute-start(f32[3,1,16,256]{3,2,1,0:T(8,128)S(1)} %get-tuple-element.58), channel_id=1, source_target_pairs={{0,2},{2,0},{4,6},{6,4},{8,10},{10,8},{12,14},{14,12},{16,18},{18,... | collective-permute-start | bytes 147464 | tf_op jit(solution)/shard_map/ppermute | solution.py:615
  3.7 9.7 %collective-permute-start.9 = (f32[3,1,16,256]{3,2,1,0:T(8,128)S(1)}, f32[3,1,16,256]{3,2,1,0:T(8,128)S(1)}, u32[]{:S(2)}, u32[]{:S(2)}) collective-permute-start(f32[3,1,16,256]{3,2,1,0:T(8,128)S(1)} %get-tuple-element.57), channel_id=1, source_target_pairs={{2,4},{4,2},{6,8},{8,6},{10,12},{12,10},{14,16},{16,14},{18,20},{2... | collective-permute-start | bytes 147464 | tf_op jit(solution)/shard_map/ppermute | solution.py:615
  19.9 59.9 %copy-start.15 = (s32[2]{0:T(128)S(1)}, s32[2]{0:T(128)}, u32[]{:S(2)}) copy-start(s32[2]{0:T(128)} %pad_add_fusion.flag) | copy-start | bytes 28
  20.0 79.3 %all-to-all-start = ((f32[128,1,6272]{2,1,0:T(1,128)}), f32[128,1,6272]{2,1,0:T(1,128)S(1)}, u32[]{:S(2)}, u32[]{:S(2)}) async-start(f32[128,1,6272]{2,1,0:T(1,128)} %bitcast.15), calls=%async_computation | async-start | bytes 6422528 | tf_op jit(solution)/shard_map/all_to_all | solution.py:619
  30.7 41.5 %collective-permute-start = (f32[5,4,16,256]{3,2,1,0:T(8,128)}, f32[5,4,16,256]{3,2,1,0:T(8,128)S(1)}, u32[]{:S(2)}, u32[]{:S(2)}) collective-permute-start(f32[5,4,16,256]{3,2,1,0:T(8,128)} %shard_map.112.refs_0_), channel_id=1, source_target_pairs={{0,2},{2,0},{4,6},{6,4},{8,10},{10,8},{12,14},{14,12},{16,18},{18,... | collective-permute-start | bytes 983048 | tf_op jit(solution)/shard_map/ppermute | solution.py:615
  31.7 46.5 %collective-permute-start.1 = (f32[5,4,16,256]{3,2,1,0:T(8,128)}, f32[5,4,16,256]{3,2,1,0:T(8,128)S(1)}, u32[]{:S(2)}, u32[]{:S(2)}) collective-permute-start(f32[5,4,16,256]{3,2,1,0:T(8,128)} %shard_map.112.refs_0_), channel_id=1, source_target_pairs={{2,4},{4,2},{6,8},{8,6},{10,12},{12,10},{14,16},{16,14},{18,20},{2... | collective-permute-start | bytes 983048 | tf_op jit(solution)/shard_map/ppermute | solution.py:615
  38.6 39.7 %collective-permute-start.2 = (f32[5,4,16,256]{3,2,1,0:T(8,128)}, f32[5,4,16,256]{3,2,1,0:T(8,128)S(1)}, u32[]{:S(2)}, u32[]{:S(2)}) collective-permute-start(f32[5,4,16,256]{3,2,1,0:T(8,128)} %shard_map.112.refs_0_), channel_id=1, source_target_pairs={{0,1},{1,0},{2,3},{3,2},{4,5},{5,4},{6,7},{7,6},{8,9},{9,8},{10,11... | collective-permute-start | bytes 983048 | tf_op jit(solution)/shard_map/ppermute | solution.py:615
  72.1 6.1 %collective-permute-start.3 = (f32[5,4,16,256]{3,2,1,0:T(8,128)S(1)}, f32[5,4,16,256]{3,2,1,0:T(8,128)S(1)}, u32[]{:S(2)}, u32[]{:S(2)}) collective-permute-start(f32[5,4,16,256]{3,2,1,0:T(8,128)S(1)} %collective-permute-done.refs_1_), channel_id=1, source_target_pairs={{0,1},{1,0},{2,3},{3,2},{4,5},{5,4},{6,7},{7,6},{8,9},{9,8},{10,11... | collective-permute-start | bytes 983048 | tf_op jit(solution)/shard_map/ppermute | solution.py:615
  78.2 1.6 collective-permute-start.4
  79.9 1.0 copy-start.6
  99.2 1.7 copy-start.1
  101.0 13.8 %copy-start = (f32[4,8,8,8,128]{4,3,2,1,0:T(8,128)S(1)}, f32[4,8,8,8,128]{4,3,2,1,0:T(8,128)}, u32[]{:S(2)}) copy-start(f32[4,8,8,8,128]{4,3,2,1,0:T(8,128)} %w.9) | copy-start | bytes 3145732
  101.0 15.2 %copy-start.5 = (f32[8,8,128]{2,1,0:T(8,128)S(1)}, f32[8,8,128]{2,1,0:T(8,128)}, u32[]{:S(2)}) copy-start(f32[8,8,128]{2,1,0:T(8,128)} %constant.21.clone.coef) | copy-start | bytes 98308
  101.0 69.5 %all-to-all-start.1 = ((f32[128,1,6272]{2,1,0:T(1,128)}), f32[128,1,6272]{2,1,0:T(1,128)}, u32[]{:S(2)}, u32[]{:S(2)}) async-start(f32[128,1,6272]{2,1,0:T(1,128)} %bitcast.14), calls=%async_computation.1 | async-start | bytes 6422528 | tf_op jit(solution)/shard_map/all_to_all | solution.py:619
  106.9 50.3 %collective-permute-start.5 = (f32[5,4,16,256]{3,2,1,0:T(8,128)S(1)}, f32[5,4,16,256]{3,2,1,0:T(8,128)}, u32[]{:S(2)}, u32[]{:S(2)}) collective-permute-start(f32[5,4,16,256]{3,2,1,0:T(8,128)S(1)} %get-tuple-element.37.refs_0_), channel_id=1, source_target_pairs={{0,2},{2,0},{4,6},{6,4},{8,10},{10,8},{12,14},{14,12},{16,18},{18,... | collective-permute-start | bytes 983048 | tf_op jit(solution)/shard_map/ppermute | solution.py:615
  108.0 49.2 %collective-permute-start.6 = (f32[5,4,16,256]{3,2,1,0:T(8,128)S(1)}, f32[5,4,16,256]{3,2,1,0:T(8,128)}, u32[]{:S(2)}, u32[]{:S(2)}) collective-permute-start(f32[5,4,16,256]{3,2,1,0:T(8,128)S(1)} %get-tuple-element.37.refs_0_), channel_id=1, source_target_pairs={{2,4},{4,2},{6,8},{8,6},{10,12},{12,10},{14,16},{16,14},{18,20},{2... | collective-permute-start | bytes 983048 | tf_op jit(solution)/shard_map/ppermute | solution.py:615
  115.3 5.0 %collective-permute-start.10 = (f32[8,8,128]{2,1,0:T(8,128)S(1)}, f32[8,8,128]{2,1,0:T(8,128)S(1)}, u32[]{:S(2)}, u32[]{:S(2)}) collective-permute-start(f32[8,8,128]{2,1,0:T(8,128)S(1)} %get-tuple-element.33), channel_id=1, source_target_pairs={{0,1},{1,0},{2,3},{3,2},{4,5},{5,4},{6,7},{7,6},{8,9},{9,8},{10,11... | collective-permute-start | bytes 98312 | tf_op jit(solution)/shard_map/ppermute | solution.py:615
  115.4 40.6 %collective-permute-start.11 = (f32[8,8,128]{2,1,0:T(8,128)S(1)}, f32[8,8,128]{2,1,0:T(8,128)S(1)}, u32[]{:S(2)}, u32[]{:S(2)}) collective-permute-start(f32[8,8,128]{2,1,0:T(8,128)S(1)} %get-tuple-element.34), channel_id=1, source_target_pairs={{1,2},{2,1},{3,4},{4,3},{5,6},{6,5},{7,8},{8,7},{9,10},{10,9},{11,... | collective-permute-start | bytes 98312 | tf_op jit(solution)/shard_map/ppermute | solution.py:615
  117.3 1.9 copy-start.2
  157.2 27.6 %collective-permute-start.12 = (f32[5,4,16,256]{3,2,1,0:T(8,128)}, f32[5,4,16,256]{3,2,1,0:T(8,128)}, u32[]{:S(2)}, u32[]{:S(2)}) collective-permute-start(f32[5,4,16,256]{3,2,1,0:T(8,128)} %collective-permute-done.5.refs_1_), channel_id=1, source_target_pairs={{0,1},{1,0},{2,3},{3,2},{4,5},{5,4},{6,7},{7,6},{8,9},{9,8},{10,11... | collective-permute-start | bytes 983048 | tf_op jit(solution)/shard_map/ppermute | solution.py:615
  157.3 27.5 %collective-permute-start.13 = (f32[5,4,16,256]{3,2,1,0:T(8,128)}, f32[5,4,16,256]{3,2,1,0:T(8,128)}, u32[]{:S(2)}, u32[]{:S(2)}) collective-permute-start(f32[5,4,16,256]{3,2,1,0:T(8,128)} %collective-permute-done.6.refs_2_), channel_id=1, source_target_pairs={{0,1},{1,0},{2,3},{3,2},{4,5},{5,4},{6,7},{7,6},{8,9},{9,8},{10,11... | collective-permute-start | bytes 983048 | tf_op jit(solution)/shard_map/ppermute | solution.py:615
  157.8 3.2 %collective-permute-start.14 = (f32[2,8,8,128]{3,2,1,0:T(8,128)S(1)}, f32[2,8,8,128]{3,2,1,0:T(8,128)S(1)}, u32[]{:S(2)}, u32[]{:S(2)}) collective-permute-start(f32[2,8,8,128]{3,2,1,0:T(8,128)S(1)} %get-tuple-element.35), channel_id=1, source_target_pairs={{0,1},{1,0},{2,3},{3,2},{4,5},{5,4},{6,7},{7,6},{8,9},{9,8},{10,11... | collective-permute-start | bytes 196616 | tf_op jit(solution)/shard_map/ppermute | solution.py:615
  157.9 9.1 %collective-permute-start.15 = (f32[2,8,8,128]{3,2,1,0:T(8,128)S(1)}, f32[2,8,8,128]{3,2,1,0:T(8,128)S(1)}, u32[]{:S(2)}, u32[]{:S(2)}) collective-permute-start(f32[2,8,8,128]{3,2,1,0:T(8,128)S(1)} %get-tuple-element.36), channel_id=1, source_target_pairs={{1,2},{2,1},{3,4},{4,3},{5,6},{6,5},{7,8},{8,7},{9,10},{10,9},{11,... | collective-permute-start | bytes 196616 | tf_op jit(solution)/shard_map/ppermute | solution.py:615
  168.7 5.7 %collective-permute-start.16 = (f32[8,8,128]{2,1,0:T(8,128)}, f32[8,8,128]{2,1,0:T(8,128)S(1)}, u32[]{:S(2)}, u32[]{:S(2)}) collective-permute-start(f32[8,8,128]{2,1,0:T(8,128)} %get-tuple-element.49), channel_id=1, source_target_pairs={{0,1},{1,0},{2,3},{3,2},{4,5},{5,4},{6,7},{7,6},{8,9},{9,8},{10,11... | collective-permute-start | bytes 98312 | tf_op jit(solution)/shard_map/ppermute | solution.py:615
  168.7 9.0 %collective-permute-start.17 = (f32[8,8,128]{2,1,0:T(8,128)}, f32[8,8,128]{2,1,0:T(8,128)S(1)}, u32[]{:S(2)}, u32[]{:S(2)}) collective-permute-start(f32[8,8,128]{2,1,0:T(8,128)} %get-tuple-element.50), channel_id=1, source_target_pairs={{1,2},{2,1},{3,4},{4,3},{5,6},{6,5},{7,8},{8,7},{9,10},{10,9},{11,... | collective-permute-start | bytes 98312 | tf_op jit(solution)/shard_map/ppermute | solution.py:615
  170.5 14.3 %copy-start.8 = (f32[5,4,16,256]{3,2,1,0:T(8,128)S(1)}, f32[5,4,16,256]{3,2,1,0:T(8,128)}, u32[]{:S(2)}) copy-start(f32[5,4,16,256]{3,2,1,0:T(8,128)} %copy-done.7) | copy-start | bytes 983044
  178.3 1.1 copy-start.3
  179.4 0.8 copy-start.14
  180.2 12.3 %copy-start.4 = (f32[1536,128]{1,0:T(8,128)S(1)}, f32[1536,128]{1,0:T(8,128)}, u32[]{:S(2)}) copy-start(f32[1536,128]{1,0:T(8,128)} %shard_map.125) | copy-start | bytes 2359300
  181.3 13.8 %collective-permute-start.18 = (f32[2,8,8,128]{3,2,1,0:T(8,128)S(1)}, f32[2,8,8,128]{3,2,1,0:T(8,128)S(1)}, u32[]{:S(2)}, u32[]{:S(2)}) collective-permute-start(f32[2,8,8,128]{3,2,1,0:T(8,128)S(1)} %get-tuple-element.54), channel_id=1, source_target_pairs={{0,1},{1,0},{2,3},{3,2},{4,5},{5,4},{6,7},{7,6},{8,9},{9,8},{10,11... | collective-permute-start | bytes 196616 | tf_op jit(solution)/shard_map/ppermute | solution.py:615
  181.4 13.7 %collective-permute-start.19 = (f32[2,8,8,128]{3,2,1,0:T(8,128)S(1)}, f32[2,8,8,128]{3,2,1,0:T(8,128)S(1)}, u32[]{:S(2)}, u32[]{:S(2)}) collective-permute-start(f32[2,8,8,128]{3,2,1,0:T(8,128)S(1)} %get-tuple-element.55), channel_id=1, source_target_pairs={{1,2},{2,1},{3,4},{4,3},{5,6},{6,5},{7,8},{8,7},{9,10},{10,9},{11,... | collective-permute-start | bytes 196616 | tf_op jit(solution)/shard_map/ppermute | solution.py:615
  (9 other events, 5.9 us)

commit v2 on v1

--- a/solution.py
+++ b/solution.py
@@ -70,6 +70,10 @@
         compiler_params=pltpu.CompilerParams(vmem_limit_bytes=limit),
         **extra,
     )
+
+
+def flags():
+    return lax.axis_index("flow") & 1, lax.axis_index("group")
 
 
 def halves(value):
@@ -120,7 +124,6 @@
 
 
 def pack_body(
-    flag,
     own_ref,
     part_ref,
     even_ref,
@@ -134,6 +137,8 @@
     tab,
     out,
     sems,
+    *,
+    paired,
 ):
     planes, rows, width = own_ref.shape[1:]
     tables, nodes = tab.shape[0], tab.shape[1]
@@ -141,7 +146,10 @@
     loads = [pltpu.make_async_copy(tab_hbm.at[t], tab.at[t], sems.at[t]) for t in range(tables)]
     for load in loads:
         load.start()
-    low_flow = flag[0] == 0
+    low_flow = flags()[0] == 0
+
+    def pick(when, other):
+        return jnp.where(low_flow, when, other) if paired else when
 
     def turn(value, by):
         return pltpu.roll(value, by % width, 1)
@@ -151,11 +159,11 @@
 
         def along_x(d):
             if x == 0:
-                below = jnp.where(low_flow, odd_ref[d, 0], even_ref[d, 0])
+                below = pick(odd_ref[d, 0], even_ref[d, 0])
             else:
                 below = own_ref[d, x - 1]
             if x == planes - 1:
-                above = jnp.where(low_flow, even_ref[d, 0], odd_ref[d, 0])
+                above = pick(even_ref[d, 0], odd_ref[d, 0])
             else:
                 above = own_ref[d, x + 1]
             return 0.5 * (above - below)
@@ -295,24 +303,27 @@
 STAGES = ((None, 1.0), (0.75, 0.25), (1.0 / 3.0, 2.0 / 3.0))
 
 
-def assemble(flag, mine, other, s0):
-    own, _, _ = mine
-    planes, rows = own.shape[1], own.shape[2]
-    above = jnp.where(flag[0] == 0, 2 * planes, 0)
-    starts = (planes, above, 2 * planes - above)
-    for start, a, b in zip(starts, mine, other):
-        for i in range(planes):
-            for k in range(5):
-                s0[k, start + i, :rows] = a[k, i]
-                s0[k, start + i, rows:] = b[k, i]
-
-
-def first_flow_body(flag, *refs):
+def place(s0, start, mine, other, first=0):
+    rows = mine.shape[2]
+    for i in range(mine.shape[1]):
+        for k in range(5):
+            s0[k, start + first + i, :rows] = mine[k, i]
+            s0[k, start + first + i, rows:] = other[k, i]
+
+
+def around_own(planes):
+    above = jnp.where(flags()[0] == 0, 2 * planes, 0)
+    return above, 2 * planes - above
+
+
+def first_flow_body(*refs):
     mine, other = refs[:3], refs[3:6]
-    new_own, new_part, own_ref, part_ref, lo_ref, hi_ref = refs[6:12]
-    s0, s1, s2, prim = refs[12:]
+    new_own, new_part, mid, low, high = refs[6:11]
+    own_ref, part_ref, lo_ref, hi_ref = refs[11:15]
+    s0, s1, s2, prim = refs[15:]
     planes, rows = mine[0].shape[1], mine[0].shape[2]
-    assemble(flag, mine, other, s0)
+    for start, a, b in zip((planes, *around_own(planes)), mine, other):
+        place(s0, start, a, b)
     wide = 3 * planes
     flow_stage(s0, None, s1, prim, 1, wide - 1, STAGES[0])
     flow_stage(s1, s0, s2, prim, 2, wide - 2, STAGES[1])
@@ -329,18 +340,31 @@
             else:
                 own_ref[d, i] = v[d][:rows]
                 part_ref[d, i] = v[d][rows:]
-        if 0 <= i < planes:
-            for k in range(5):
+        for k in range(5):
+            if i == -1:
+                low[k, 0] = s1[k, x]
+            elif i == planes:
+                high[k, 0] = s1[k, x]
+            else:
                 new_own[k, i] = s1[k, x, :rows]
                 new_part[k, i] = s1[k, x, rows:]
-
-
-def last_flow_body(flag, *refs):
-    mine, other, out_ref = refs[:3], refs[3:6], refs[6]
-    s0, s1, s2, prim = refs[7:]
-    planes, rows = mine[0].shape[1], mine[0].shape[2]
-    assemble(flag, mine, other, s0)
+                if 0 < i < planes - 1:
+                    mid[k, i - 1] = s1[k, x, :rows]
+
+
+def last_flow_body(*refs):
+    own, part, low, high = refs[:4]
+    even, odd, even_part, odd_part, out_ref = refs[4:9]
+    s0, s1, s2, prim = refs[9:]
+    planes, rows = own.shape[1], own.shape[2]
+    place(s0, planes, own, part)
+    even_at, odd_at = around_own(planes)
+    place(s0, even_at, even, even_part, first=1)
+    place(s0, odd_at, odd, odd_part, first=1)
     wide = 3 * planes
+    for k in range(5):
+        s0[k, planes - 1] = low[k, 0]
+        s0[k, 2 * planes] = high[k, 0]
     flow_stage(s0, None, s1, prim, 2, wide - 2, STAGES[0])
     flow_stage(s1, s0, s2, prim, 3, wide - 3, STAGES[1])
     flow_stage(s2, s0, out_ref, prim, planes, 2 * planes, STAGES[2], shift=planes, rows=rows)
@@ -446,51 +470,81 @@
     lax.fori_loop(0, NP, body, 0)
 
 
-def lifts(s, j, flag, even, odd):
-    low_core = flag[1] == 0
-    from_low = jnp.where(low_core, odd[j], even[j])
-    from_high = jnp.where(low_core, even[j], odd[j])
-    low = LIFT * (from_low - (s[1, 0, j] + s[0, 0, j]))
-    high = LIFT * (from_high - (s[1, NP - 1, j] - s[0, NP - 1, j]))
-    return low, high
-
-
-def put_ends(flag, up, down, even, odd):
-    low_core = flag[1] == 0
-    even[...] = jnp.where(low_core, up, down)
-    odd[...] = jnp.where(low_core, down, up)
-
-
-def ends_body(flag, w, even, odd):
-    put_ends(flag, w[0, NP - 1] + w[1, NP - 1], w[1, 0] - w[0, 0], even, odd)
-
-
-def inner_body(w, coef, r):
+LAST = NP - 1
+
+
+def chosen(low, when_low, when_high):
+    return jnp.where(low, when_low, when_high)
+
+
+def add_lifts(s, r, incoming=None):
+    def lift(j):
+        from_low, from_high = (0.0, 0.0) if incoming is None else incoming(j)
+        low = LIFT * (from_low - (s[1, 0, j] + s[0, 0, j]))
+        high = LIFT * (from_high - (s[1, LAST, j] - s[0, LAST, j]))
+        r[0, 0, j] = r[0, 0, j] + low
+        r[1, 0, j] = r[1, 0, j] + low
+        r[0, LAST, j] = r[0, LAST, j] - high
+        r[1, LAST, j] = r[1, LAST, j] + high
+
+    each(lift)
+
+
+def ends_body(w, even, odd):
+    low_core = flags()[1] == 0
+    up, down = w[0, LAST] + w[1, LAST], w[1, 0] - w[0, 0]
+    even[...] = chosen(low_core, up, down)
+    odd[...] = chosen(low_core, down, up)
+
+
+def rate_body(w, even, odd, coef, r):
+    low_core = flags()[1] == 0
     local_rate(w, r, coef)
-
-
-def unpack_body(arrived, f, wide):
-    groups = f.shape[0] // 128
+    add_lifts(
+        w,
+        r,
+        lambda j: (
+            chosen(low_core, odd[j], even[j]),
+            chosen(low_core, even[j], odd[j]),
+        ),
+    )
+
+
+def unpack_body(w, r0, arrived_hbm, coef, f, s1, even, odd, arrived, wide, sums, sems):
+    lanes = w.shape[-1]
+    groups = sums.shape[0]
     stride = groups * CAP + 1
-    devices = arrived.shape[0] // stride
-    elements = f.shape[-1]
-    labels = arrived[pl.ds(stride - 1, devices, stride=stride), :].T
-    row = lax.broadcasted_iota(jnp.int32, (elements, devices), 0).astype(F32)
-    pick = jnp.concatenate(
-        [(row == labels[s : s + 1] - 1.0).astype(F32).astype(BF16) for s in range(CAP)], axis=1
-    )
-    for g in range(groups):
-        for s in range(CAP):
-            part = arrived[pl.ds(CAP * g + s, devices, stride=stride), :]
-            high, low = halves(part)
-            wide[g % 2, s * devices : (s + 1) * devices, 0:128] = high
-            wide[g % 2, s * devices : (s + 1) * devices, 128:256] = low
-        both = dot(pick, wide[g % 2])
-        f[g * 128 : (g + 1) * 128, :] = (both[:, :128] + both[:, 128:]).T
-
-
-def first_stage_body(flag, w, r0, f, q_even, q_odd, coef, s1, even, odd):
-    lanes = w.shape[-1]
+    half = arrived.shape[0] // stride // 2
+    loads = []
+    for h in range(2):
+        part = pl.ds(h * half * stride, half * stride)
+        loads.append(pltpu.make_async_copy(arrived_hbm.at[part], arrived.at[part], sems.at[h]))
+        loads[-1].start()
+    row = lax.broadcasted_iota(jnp.int32, (lanes, half), 0).astype(F32)
+    for h in range(2):
+        loads[h].wait()
+        base = h * half * stride
+        labels = arrived[pl.ds(base + stride - 1, half, stride=stride), :].T
+        pick = jnp.concatenate(
+            [(row == labels[s : s + 1] - 1.0).astype(F32).astype(BF16) for s in range(CAP)],
+            axis=1,
+        )
+        for g in range(groups):
+            for s in range(CAP):
+                part = arrived[pl.ds(base + CAP * g + s, half, stride=stride), :]
+                high, low = halves(part)
+                wide[g % 2, s * half : (s + 1) * half, 0:128] = high
+                wide[g % 2, s * half : (s + 1) * half, 128:256] = low
+            both = dot(pick, wide[g % 2])
+            if h == 0:
+                sums[g] = both
+                continue
+            both = both + sums[g]
+            nodes = (both[:, :128] + both[:, 128:]).T
+            for row_of in range(128 // NP):
+                at = g * 128 // NP + row_of
+                c, i, j = at // (NP * NP), at // NP % NP, at % NP
+                f[c, i, j] = nodes[row_of * NP : (row_of + 1) * NP, :]
 
     def add(i):
         for k in range(4):
@@ -498,21 +552,10 @@
             s1[k, i] = w[k, i] + DT_WAVE * rate
 
     each(add)
-
-    def lift(j):
-        low, high = lifts(w, j, flag, q_even, q_odd)
-        low, high = DT_WAVE * low, DT_WAVE * high
-        last = NP - 1
-        s1[0, 0, j] = s1[0, 0, j] + low
-        s1[1, 0, j] = s1[1, 0, j] + low
-        s1[0, last, j] = s1[0, last, j] - high
-        s1[1, last, j] = s1[1, last, j] + high
-
-    each(lift)
     inner = inner_maker(coef, lanes)
-    low_core = flag[1] == 0
+    low_core = flags()[1] == 0
     now, then = [], []
-    for i, sign in ((NP - 1, 1.0), (0, -1.0)):
+    for i, sign in ((LAST, 1.0), (0, -1.0)):
         ps = [s1[0, i, j] for j in range(NP)]
         dp, _ = along_middle(ps, [s1[2, i, j] for j in range(NP)], lanes)
         now_rows, then_rows = [], []
@@ -534,12 +577,13 @@
         then.append(then_rows)
     for j in range(NP):
         for slot, (up, down) in enumerate((now, then)):
-            even[slot, j] = jnp.where(low_core, up[j], down[j])
-            odd[slot, j] = jnp.where(low_core, down[j], up[j])
-
-
-def middle_stage_body(w, s1, f, coef, s2, r2, r1):
+            even[slot, j] = chosen(low_core, up[j], down[j])
+            odd[slot, j] = chosen(low_core, down[j], up[j])
+
+
+def middle_body(w, s1, f, coef, s2, r2, r1):
     local_rate(s1, r1, coef, f)
+    add_lifts(s1, r1)
 
     def add(i):
         for k in range(4):
@@ -547,30 +591,50 @@
 
     each(add)
     local_rate(s2, r2, coef, f)
-
-
-def last_stage_body(flag, w, s1, s2, r2, q_even, q_odd, coef, out, even, odd, s, r):
+    add_lifts(s2, r2)
+
+
+def relay_body(w, s1, f, coef, even, odd, s2, r2, even3, odd3, far_even, far_odd, r1):
+    middle_body(w, s1, f, coef, s2, r2, r1)
+    low_flow, low_core = flags()[0] == 0, flags()[1] == 0
+
+    def third(k, i, j):
+        return w[k, i, j] * (1.0 / 3.0) + (2.0 / 3.0) * (s2[k, i, j] + DT_WAVE * r2[k, i, j])
+
+    def send(j):
+        for slot in range(2):
+            even3[slot, j] = even[slot, j]
+            odd3[slot, j] = odd[slot, j]
+        up = third(1, LAST, j) + third(0, LAST, j)
+        down = third(1, 0, j) - third(0, 0, j)
+        even3[2, j] = chosen(low_core, up, down)
+        odd3[2, j] = chosen(low_core, down, up)
+        up = chosen(low_core, even[0, j], odd[0, j])
+        down = chosen(low_core, odd[0, j], even[0, j])
+        far_even[j] = chosen(low_flow, up, down)
+        far_odd[j] = chosen(low_flow, down, up)
+
+    each(send)
+
+
+def close_step(w, s2, r2, even, odd, coef, out, s, r):
     lanes = w.shape[-1]
-    last = NP - 1
+    low_core = flags()[1] == 0
 
     def first(j):
-        low, high = lifts(s1, j, flag, q_even.at[0], q_odd.at[0])
-        low, high = (0.25 * DT_WAVE) * low, (0.25 * DT_WAVE) * high
+        low = (0.25 * DT_WAVE * LIFT) * chosen(low_core, odd[0, j], even[0, j])
+        high = (0.25 * DT_WAVE * LIFT) * chosen(low_core, even[0, j], odd[0, j])
         s[0, j] = low
         s[1, j] = -high
-        new = (s2[0, 0, j] + low, s2[1, 0, j] + low, s2[0, last, j] - high, s2[1, last, j] + high)
-        low_core = flag[1] == 0
-        from_low = jnp.where(low_core, q_odd[1, j], q_even[1, j])
-        from_high = jnp.where(low_core, q_even[1, j], q_odd[1, j])
-        lift_low = LIFT * (from_low - (new[1] + new[0]))
-        lift_high = LIFT * (from_high - (new[3] - new[2]))
+        lift_low = LIFT * (chosen(low_core, odd[1, j], even[1, j]) - 2.0 * low)
+        lift_high = LIFT * (chosen(low_core, even[1, j], odd[1, j]) - 2.0 * high)
         for i in range(NP):
-            a, b = float(MATRIX[i, 0]), float(MATRIX[i, last])
+            a, b = float(MATRIX[i, 0]), float(MATRIX[i, LAST])
             p = r2[0, i, j] - a * low - b * high
             u = r2[1, i, j] - a * low + b * high
             if i == 0:
                 p, u = p + lift_low, u + lift_low
-            if i == last:
+            if i == LAST:
                 p, u = p - lift_high, u + lift_high
             r[0, i, j] = p
             r[1, i, j] = u
@@ -588,9 +652,9 @@
                 close(k, i, j, s2[k, i, j], rate)
         return carry
 
-    lax.fori_loop(1, last, inside, 0)
+    lax.fori_loop(1, LAST, inside, 0)
     inner = inner_maker(coef, lanes)
-    for side, i in ((0, 0), (1, last)):
+    for side, i in ((0, 0), (1, LAST)):
         ps = [s[side, j] for j in range(NP)]
         dp, du = along_middle(ps, None, lanes)
         for j in range(NP):
@@ -603,7 +667,37 @@
             close(1, i, j, s2[1, i, j] + change, r[1, i, j])
             close(2, i, j, s2[2, i, j], r2[2, i, j] + du[j])
             close(3, i, j, s2[3, i, j], r2[3, i, j] + dw)
-    put_ends(flag, out[0, last] + out[1, last], out[1, 0] - out[0, 0], even, odd)
+
+
+def turn_body(
+    w, s2, r2, even, odd, far_even, far_odd, own_even, own_odd, coef, out, r0, s, r, q
+):
+    close_step(w, s2, r2, even, odd, coef, out, s, r)
+    lanes = w.shape[-1]
+    low_flow, low_core = flags()[0] == 0, flags()[1] == 0
+    inner = inner_maker(coef, lanes)
+    weight = 0.25 * DT_WAVE * LIFT
+
+    def spill(values):
+        dp, _ = along_middle(values, None, lanes)
+        found = []
+        for j in range(NP):
+            dq, _ = inner(values[j], None, want_u=False)
+            found.append(dq if dp[j] is None else dp[j] + dq)
+        return found
+
+    ups = [weight * chosen(low_core, own_even[0, j], own_odd[0, j]) for j in range(NP)]
+    downs = [weight * chosen(low_core, own_odd[0, j], own_even[0, j]) for j in range(NP)]
+    step = 2.0 / 3.0 * DT_WAVE
+    for j, (a, b) in enumerate(zip(spill([-d for d in downs]), spill(ups))):
+        far_low = chosen(low_flow, far_odd[j], far_even[j])
+        far_high = chosen(low_flow, far_even[j], far_odd[j])
+        a = a - (2.0 * float(MATRIX[LAST, 0]) * weight) * far_low
+        b = (2.0 * float(MATRIX[0, LAST]) * weight) * far_high - b
+        q[0, j] = chosen(low_core, odd[2, j], even[2, j]) + step * a
+        q[1, j] = chosen(low_core, even[2, j], odd[2, j]) + step * b
+    local_rate(out, r0, coef)
+    add_lifts(out, r0, lambda j: (q[0, j], q[1, j]))
 
 
 def trade(value, axis, odd):
@@ -630,8 +724,6 @@
     coef = np.stack([MATRIX[np.arange(NP), (np.arange(NP) + k) % NP] for k in range(NP)])
     coef = jnp.asarray(np.broadcast_to(coef[:, :, None], (NP, NP, lanes)).copy())
     odd_flow = lax.axis_index("flow") & 1
-    flag = jnp.stack([odd_flow, lax.axis_index("group")]).astype(jnp.int32)
-    first_flag = jnp.zeros((2,), jnp.int32)
 
     inward = (planes - 1) * (1 - odd_flow)
     v_even = trade(lax.dynamic_slice_in_dim(velocity, inward, 1, 1), "flow", 0)
@@ -658,83 +750,88 @@
         limit=WHOLE_VMEM,
     )(margin_element, margin_block, margin_table)
 
-    pack = call(
-        pack_body,
-        sds(devices * stride, 128),
-        8_000_000,
-        scratch=(
-            pltpu.VMEM((2, 3 * planes * rows, 128), F32),
-            pltpu.VMEM((3, 256, nodes), BF16),
-            pltpu.VMEM(tables.shape, F32),
-            pltpu.VMEM((devices * stride, 128), F32),
-            pltpu.SemaphoreType.DMA((kinds + 2,)),
-        ),
-        specs="svvvvhvv",
-        limit=WHOLE_VMEM,
-        out_specs="h",
-    )
-
-    def send(which, *speeds):
-        sent = pack(which, *speeds, tables, select, labels)
+    def send(paired, *speeds):
+        sent = call(
+            lambda *refs: pack_body(*refs, paired=paired),
+            sds(devices * stride, 128),
+            8_000_000,
+            scratch=(
+                pltpu.VMEM((2, 3 * planes * rows, 128), F32),
+                pltpu.VMEM((3, 256, nodes), BF16),
+                pltpu.VMEM(tables.shape, F32),
+                pltpu.VMEM((devices * stride, 128), F32),
+                pltpu.SemaphoreType.DMA((kinds + 2,)),
+            ),
+            specs="vvvvhvv",
+            out_specs="h",
+            limit=WHOLE_VMEM,
+        )(*speeds, tables, select, labels)
         sent = exchange_all(sent.reshape(devices, 1, stride * 128))
         return sent.reshape(devices * stride, 128)
 
-    arrived_1 = send(flag, velocity, v_part, v_even, v_odd)
+    arrived_1 = send(True, velocity, v_part, v_even, v_odd)
 
     speed = sds(3, planes, rows, width)
     thin = sds(3, 1, rows, width)
+    edge = sds(5, 1, 2 * rows, width)
     wide = pltpu.VMEM((5, 3 * planes, 2 * rows, width), F32)
-    new_own, new_part, own, part, low, high = call(
+    new_own, new_part, mid, low_edge, high_edge, own, part, low, high = call(
         first_flow_body,
-        (block, block, speed, speed, thin, thin),
+        (block, block, sds(5, planes - 2, rows, width), edge, edge, speed, speed, thin, thin),
         60_000_000,
         scratch=[wide] * 4,
-        specs="s" + 6 * "v",
-    )(flag, *pieces, *others)
-    arrived_2 = send(first_flag, own, part, high, low)
-    pieces = surround(new_own)
-
-    def finish_flow(pieces):
-        return call(
-            last_flow_body, block, 30_000_000, scratch=[wide] * 4, specs="s" + 6 * "v"
-        )(flag, *pieces, new_part, *swap_rows(pieces[1:]))
+    )(*pieces, *others)
+    arrived_2 = send(False, own, part, high, low)
+    mids = surround(mid)[1:]
+
+    def finish_flow(mids):
+        return call(last_flow_body, block, 30_000_000, scratch=[wide] * 4)(
+            new_own, new_part, low_edge, high_edge, *mids, *swap_rows(mids)
+        )
 
     state = sds(*wave.shape)
+    force = sds(3, *wave.shape[1:])
     hold = pltpu.VMEM(wave.shape, F32)
     face = sds(NP, NP, lanes)
     pair = sds(2, NP, NP, lanes)
-    inner = call(inner_body, state, 8_000_000)
+    triple = sds(3, NP, NP, lanes)
+    sides = pltpu.VMEM((2, NP, NP, lanes), F32)
+    couple = pltpu.VMEM((2,) + wave.shape[1:], F32)
     unpack = call(
         unpack_body,
-        sds(3 * nodes, lanes),
-        8_000_000,
-        scratch=[pltpu.VMEM((2, CAP * devices, 256), BF16)],
-    )
-    first_stage = call(first_stage_body, (state, pair, pair), 4_000_000, specs="svvvvvv")
-    middle_stage = call(middle_stage_body, (state, state), 16_000_000, scratch=[hold])
-    last_stage = call(
-        last_stage_body,
-        (state, face, face),
-        6_000_000,
-        scratch=[pltpu.VMEM((2, NP, NP, lanes), F32), pltpu.VMEM((2,) + wave.shape[1:], F32)],
-        specs="svvvvvvv",
+        (force, state, pair, pair),
+        12_000_000,
+        scratch=[
+            pltpu.VMEM((devices * stride, 128), F32),
+            pltpu.VMEM((2, CAP * devices // 2, 256), BF16),
+            pltpu.VMEM((3 * nodes // 128, lanes, 256), F32),
+            pltpu.SemaphoreType.DMA((2,)),
+        ],
+        specs="vvhv",
     )
 
     def around(even, odd):
         return (trade(even, "group", 0), trade(odd, AXES, 1))
 
-    ends = call(ends_body, (face, face), 100_000, specs="sv")(flag, wave)
-    for turn, arrived in enumerate((arrived_1, arrived_2)):
-        faces = around(*ends)
-        rate = inner(wave, coef)
-        forcing = unpack(arrived).reshape(3, *wave.shape[1:])
-        s1, *ends = first_stage(flag, wave, rate, forcing, *faces, coef)
-        faces = around(*ends)
-        if turn == 0:
-            pieces, _ = lax.optimization_barrier((pieces, ends))
-            flow_state = finish_flow(pieces)
-        s2, r2 = middle_stage(wave, s1, forcing, coef)
-        wave, *ends = last_stage(flag, wave, s1, s2, r2, *faces, coef)
+    ends = call(ends_body, (face, face), 100_000)(wave)
+    faces = around(*ends)
+    rate = call(rate_body, state, 8_000_000)(wave, *faces, coef)
+    forcing, s1, *ends = unpack(wave, rate, arrived_1, coef)
+    s2, r2, even, odd, far_even, far_odd = call(
+        relay_body, (state, state, triple, triple, face, face), 16_000_000, scratch=[hold]
+    )(wave, s1, forcing, coef, *ends)
+    faces = around(even, odd)
+    far = (trade(far_even, "flow", 0), trade(far_odd, "flow", 1))
+    mids, _ = lax.optimization_barrier((mids, far_even))
+    flow_state = finish_flow(mids)
+    wave, rate = call(
+        turn_body, (state, state), 14_000_000, scratch=[sides, couple, sides]
+    )(wave, s2, r2, *faces, *far, *ends, coef)
+
+    forcing, s1, *ends = unpack(wave, rate, arrived_2, coef)
+    faces = around(*ends)
+    s2, r2 = call(middle_body, (state, state), 16_000_000, scratch=[hold])(wave, s1, forcing, coef)
+    wave = call(close_step, state, 6_000_000, scratch=[sides, couple])(wave, s2, r2, *faces, coef)
     return (flow_state, wave, forcing)
 
 

time: 198 us -> 197 us (level)
  waiting for transfers between devices: 86.4 us -> 94.1 us
  Pallas kernels: 50.6 us -> 46.5 us
    ppermute x20, waiting for transfers between devices: 86.4 us -> 94.1 us  [trade(): return lax.ppermute(value, axis, pairs)]
    pallas_call x15 -> x12, Pallas kernels: 47.1 us -> 43 us  [the longest x2 11.8 us: send(): call(lambda *refs: pack_body(*refs, paired=paired), sds(devices * stride,...]
    unnamed x38 -> x42, local copies, waits for them, and re-layouts: 11.1 us -> 9.84 us
  transfers between devices with their start and end apart: 22 -> 22, of which waited for: 6 -> 9; matrix products, arithmetic and copies ran while one was open for 1% -> 0% of each run, Pallas kernels for 22% -> 20%
where the time goes in v2:
time: 197 us
  waiting for transfers between devices  94.1 us (48%)
  Pallas kernels  46.5 us (24%)
  starting transfers between devices  44.7 us (23%)
  local copies, waits for them, and re-layouts  10.7 us (5%)
    ppermute x20, waiting for transfers between devices, trade(): return lax.ppermute(value, axis, pairs)  94.1 us
    ppermute x20, starting transfers between devices, trade(): return lax.ppermute(value, axis, pairs)  31.4 us
    all_to_all x2, starting transfers between devices, exchange_all(): return lax.all_to_all(value, AXES, split_axis=0, concat_axis=0, tiled=True)  13.3 us
    pallas_call x2, Pallas kernels, send(): call(lambda *refs: pack_body(*refs, paired=paired), sds(devices * stride,...  11.8 us
    unnamed x42, local copies, waits for them, and re-layouts  9.84 us
    pallas_call x1, Pallas kernels, advance(): call(first_flow_body, (block, block, sds(5, planes - 2, rows, width), edg...  8.16 us
    pallas_call x1, Pallas kernels, finish_flow(): call(last_flow_body, block, 30000000, scratch=[wide] * 4)  7.61 us
  transfers between devices with their start and end apart: 22, of which 9 were waited for; matrix products, arithmetic and copies ran while one was open for 0% of the time, Pallas kernels for 20%

profile of v2, /device:TPU:0, one launch (start us, length us, event | category | flops | bytes accessed | tf_op | source)
XLA Modules:
  0.0 196.9 jit_solution(9395710937908632432)
XLA Ops:
  0.7 0.8 constant_dynamic-slice_fusion
  1.6 8.9 %collective-permute-start.11 = (f32[3,1,16,256]{3,2,1,0:T(8,128)S(1)}, f32[3,1,16,256]{3,2,1,0:T(8,128)S(1)}, u32[]{:S(2)}, u32[]{:S(2)}) collective-permute-start(f32[3,1,16,256]{3,2,1,0:T(8,128)S(1)} %get-tuple-element.69), channel_id=1, source_target_pairs={{2,4},{4,2},{6,8},{8,6},{10,12},{12,10},{14,16},{16,14},{18,20},{2... | collective-permute-start | bytes 147464 | tf_op jit(solution)/shard_map/ppermute | solution.py:709
  10.4 1.8 shard_map.116
  12.8 1.7 collective-permute-done.10.refs_2_
  15.2 5.9 %shard_map.117 = f32[6272,128]{1,0:T(8,128)} custom-call(f32[3,4,16,256]{3,2,1,0:T(8,128)} %refs_0_.3, f32[3,4,16,256]{3,2,1,0:T(8,128)} %copy-done.18, f32[3,1,16,256]{3,2,1,0:T(8,128)} %copy-done.20, f32[3,1,16,256]{3,2,1,0:T(8,128)} %copy-done.19, f32[4,512,512]{2,1,0:T(8,128)} %refs_4_.3, bf16[512,256]{1,0:T(8,128)(2,1)} %get-tuple-element.43.refs_5_, ...), custom_call_target="tpu_custom_call" | custom-call | flops 8000000 | bytes 4000000 | tf_op jit(solution)/shard_map/pallas_call | solution.py:754
  21.1 7.4 %all-to-all-start = ((f32[128,1,6272]{2,1,0:T(1,128)}), f32[128,1,6272]{2,1,0:T(1,128)S(1)}, u32[]{:S(2)}, u32[]{:S(2)}) async-start(f32[128,1,6272]{2,1,0:T(1,128)} %bitcast.6), calls=%async_computation | async-start | bytes 6422528 | tf_op jit(solution)/shard_map/all_to_all | solution.py:713
  28.6 1.7 shard_map.112.refs_0_
  30.3 7.3 %collective-permute-start.1 = (f32[5,4,16,256]{3,2,1,0:T(8,128)}, f32[5,4,16,256]{3,2,1,0:T(8,128)S(1)}, u32[]{:S(2)}, u32[]{:S(2)}) collective-permute-start(f32[5,4,16,256]{3,2,1,0:T(8,128)} %shard_map.112.refs_0_), channel_id=1, source_target_pairs={{2,4},{4,2},{6,8},{8,6},{10,12},{12,10},{14,16},{16,14},{18,20},{2... | collective-permute-start | bytes 983048 | tf_op jit(solution)/shard_map/ppermute | solution.py:709
  37.6 40.3 %collective-permute-done.1.refs_2_ = f32[5,4,16,256]{3,2,1,0:T(8,128)S(1)} collective-permute-done((f32[5,4,16,256]{3,2,1,0:T(8,128)}, f32[5,4,16,256]{3,2,1,0:T(8,128)S(1)}, u32[]{:S(2)}, u32[]{:S(2)}) %collective-permute-start.1) | collective-permute-done | bytes 327712 | tf_op jit(solution)/shard_map/ppermute | solution.py:709
  78.4 1.1 collective-permute-done.4.refs_5_
  80.0 1.0 copy-done.4
  81.0 8.2 %shard_map.113 = (f32[5,4,16,256]{3,2,1,0:T(8,128)S(1)}, f32[5,4,16,256]{3,2,1,0:T(8,128)S(1)}, f32[5,2,16,256]{3,2,1,0:T(8,128)S(1)}, f32[5,1,32,256]{3,2,1,0:T...) custom-call(f32[5,4,16,256]{3,2,1,0:T(8,128)S(1)} %copy-done.4, ...), custom_call_target="tpu_custom_call" | custom-call | flops 60000000 | bytes 4000000 | tf_op jit(solution)/shard_map/pallas_call | solution.py:778
  89.1 0.7 copy-done.6
  94.4 5.9 %shard_map.122 = f32[6272,128]{1,0:T(8,128)} custom-call(f32[3,4,16,256]{3,2,1,0:T(8,128)} %copy-done.8, f32[3,4,16,256]{3,2,1,0:T(8,128)} %copy-done.9, f32[3,1,16,256]{3,2,1,0:T(8,128)} %copy-done.15, f32[3,1,16,256]{3,2,1,0:T(8,128)} %copy-done.14, f32[4,512,512]{2,1,0:T(8,128)} %refs_4_.3, bf16[512,256]{1,0:T(8,128)(2,1)} %get-tuple-element.43.refs_5_, ...), custom_call_target="tpu_custom_call" | custom-call | flops 8000000 | bytes 4000000 | tf_op jit(solution)/shard_map/pallas_call | solution.py:754
  100.3 1.7 copy-done.1
  102.1 5.9 %all-to-all-start.1 = ((f32[128,1,6272]{2,1,0:T(1,128)}), f32[128,1,6272]{2,1,0:T(1,128)}, u32[]{:S(2)}, u32[]{:S(2)}) async-start(f32[128,1,6272]{2,1,0:T(1,128)} %bitcast.5), calls=%async_computation.1 | async-start | bytes 6422528 | tf_op jit(solution)/shard_map/all_to_all | solution.py:713
  108.0 7.3 %collective-permute-start.6 = (f32[5,2,16,256]{3,2,1,0:T(8,128)S(1)}, f32[5,2,16,256]{3,2,1,0:T(8,128)}, u32[]{:S(2)}, u32[]{:S(2)}) collective-permute-start(f32[5,2,16,256]{3,2,1,0:T(8,128)S(1)} %copy-done.17), channel_id=1, source_target_pairs={{2,4},{4,2},{6,8},{8,6},{10,12},{12,10},{14,16},{16,14},{18,20},{2... | collective-permute-start | bytes 491528 | tf_op jit(solution)/shard_map/ppermute | solution.py:709
  115.4 1.0 collective-permute-start.8
  116.6 37.0 %collective-permute-done.8.odd = f32[8,8,128]{2,1,0:T(8,128)S(1)} collective-permute-done((f32[8,8,128]{2,1,0:T(8,128)S(1)}, f32[8,8,128]{2,1,0:T(8,128)S(1)}, u32[]{:S(2)}, u32[]{:S(2)}) %collective-permute-start.8) | collective-permute-done | bytes 32800 | tf_op jit(solution)/shard_map/ppermute | solution.py:709
  153.6 1.2 shard_map.115.r0
  154.8 1.9 shard_map.118
  156.7 2.7 %shard_map.119 = (f32[4,8,8,8,128]{4,3,2,1,0:T(8,128)S(1)}, f32[4,8,8,8,128]{4,3,2,1,0:T(8,128)S(1)}, f32[3,8,8,128]{3,2,1,0:T(8,128)S(1)}, f32[3,8,8,128]{3,2,1...) custom-call(f32[4,8,8,8,128]{4,3,2,1,0:T(8,128)S(1)} %copy-done, ...), custom_call_target="tpu_custom_call" | custom-call | flops 16000000 | bytes 4000000 | tf_op jit(solution)/shard_map/pallas_call | solution.py:820
  160.7 0.8 collective-permute-start.17
  161.5 8.8 %collective-permute-done.17.far_odd = f32[8,8,128]{2,1,0:T(8,128)S(1)} collective-permute-done((f32[8,8,128]{2,1,0:T(8,128)S(1)}, f32[8,8,128]{2,1,0:T(8,128)S(1)}, u32[]{:S(2)}, u32[]{:S(2)}) %collective-permute-start.17) | collective-permute-done | bytes 32800 | tf_op jit(solution)/shard_map/ppermute | solution.py:709
  170.4 3.9 %collective-permute-done.16.far_even = f32[8,8,128]{2,1,0:T(8,128)S(1)} collective-permute-done((f32[8,8,128]{2,1,0:T(8,128)S(1)}, f32[8,8,128]{2,1,0:T(8,128)S(1)}, u32[]{:S(2)}, u32[]{:S(2)}) %collective-permute-start.16) | collective-permute-done | bytes 32800 | tf_op jit(solution)/shard_map/ppermute | solution.py:709
  174.3 1.8 shard_map.121
  176.1 3.8 %shard_map.123 = (f32[3,8,8,8,128]{4,3,2,1,0:T(8,128)}, f32[4,8,8,8,128]{4,3,2,1,0:T(8,128)S(1)}, f32[2,8,8,128]{3,2,1,0:T(8,128)S(1)}, f32[2,8,8,128]{3,2,1,0:T(8,128)S(1)}) custom-call(f32[4,8,8,8,128]{4,3,2,1,0:T(8,128)S(1)} %get-tuple-element.57.w, f32[4,8,8,8,128]{4,3,2,1,0:T(8,128)S(1)} %get-tuple-element.58.r0, f32[6272,128]{1,0:T(8,128)} %bitcast.3.arrived_hbm, ...), custom_call_target="tpu_custom_call" | custom-call | flops 12000000 | bytes 4000000 | tf_op jit(solution)/shard_map/pallas_call | solution.py:831
  179.9 4.1 %collective-permute-start.19 = (f32[2,8,8,128]{3,2,1,0:T(8,128)S(1)}, f32[2,8,8,128]{3,2,1,0:T(8,128)S(1)}, u32[]{:S(2)}, u32[]{:S(2)}) collective-permute-start(f32[2,8,8,128]{3,2,1,0:T(8,128)S(1)} %get-tuple-element.68), channel_id=1, source_target_pairs={{1,2},{2,1},{3,4},{4,3},{5,6},{6,5},{7,8},{8,7},{9,10},{10,9},{11,... | collective-permute-start | bytes 196616 | tf_op jit(solution)/shard_map/ppermute | solution.py:709
  184.1 7.6 %shard_map.120 = f32[5,4,16,256]{3,2,1,0:T(8,128)} custom-call(f32[5,4,16,256]{3,2,1,0:T(8,128)S(1)} %get-tuple-element.36.refs_0_, f32[5,4,16,256]{3,2,1,0:T(8,128)S(1)} %copy-done.7, f32[5,1,32,256]{3,2,1,0:T(8,128)S(1)} %copy-done.11, f32[5,1,32,256]{3,2,1,0:T(8,128)S(1)} %copy-done.13, f32[5,2,16,256]{3,2,1,0:T(8,128)} %collective-permute-done.5.refs_4_, ...), custom_call_target="tpu_custom_call" | custom-call | flops 30000000 | bytes 4000000 | tf_op jit(solution)/shard_map/pallas_call | solution.py:788
  191.7 1.1 copy-done.5
  192.9 2.6 %shard_map.124 = (f32[4,8,8,8,128]{4,3,2,1,0:T(8,128)S(1)}, f32[4,8,8,8,128]{4,3,2,1,0:T(8,128)S(1)}) custom-call(f32[4,8,8,8,128]{4,3,2,1,0:T(8,128)S(1)} %get-tuple-element.57.w, f32[4,8,8,8,128]{4,3,2,1,0:T(8,128)S(1)} %get-tuple-element.63.s1, f32[3,8,8,8,128]{4,3,2,1,0:T(8,128)S(1)} %copy-done.5, f32[8,8,128]{2,1,0:T(8,128)S(1)} %copy-done.3), custom_call_target="tpu_custom_call" | custom-call | flops 16000000 | bytes 4000000 | tf_op jit(solution)/shard_map/pallas_call | solution.py:833
  195.5 1.5 shard_map.125
  (69 shorter events, 8.6 us)
Async XLA Ops:
  0.6 13.9 %collective-permute-start.9 = (f32[3,4,16,256]{3,2,1,0:T(8,128)}, f32[3,4,16,256]{3,2,1,0:T(8,128)S(1)}, u32[]{:S(2)}, u32[]{:S(2)}) collective-permute-start(f32[3,4,16,256]{3,2,1,0:T(8,128)} %refs_0_.3), channel_id=1, source_target_pairs={{0,1},{1,0},{2,3},{3,2},{4,5},{5,4},{6,7},{7,6},{8,9},{9,8},{10,11... | collective-permute-start | bytes 589832 | tf_op jit(solution)/shard_map/ppermute | solution.py:709
  1.6 11.2 %collective-permute-start.11 = (f32[3,1,16,256]{3,2,1,0:T(8,128)S(1)}, f32[3,1,16,256]{3,2,1,0:T(8,128)S(1)}, u32[]{:S(2)}, u32[]{:S(2)}) collective-permute-start(f32[3,1,16,256]{3,2,1,0:T(8,128)S(1)} %get-tuple-element.69), channel_id=1, source_target_pairs={{2,4},{4,2},{6,8},{8,6},{10,12},{12,10},{14,16},{16,14},{18,20},{2... | collective-permute-start | bytes 147464 | tf_op jit(solution)/shard_map/ppermute | solution.py:709
  10.4 4.1 %collective-permute-start.10 = (f32[3,1,16,256]{3,2,1,0:T(8,128)S(1)}, f32[3,1,16,256]{3,2,1,0:T(8,128)S(1)}, u32[]{:S(2)}, u32[]{:S(2)}) collective-permute-start(f32[3,1,16,256]{3,2,1,0:T(8,128)S(1)} %get-tuple-element.70), channel_id=1, source_target_pairs={{0,2},{2,0},{4,6},{6,4},{8,10},{10,8},{12,14},{14,12},{16,18},{18,... | collective-permute-start | bytes 147464 | tf_op jit(solution)/shard_map/ppermute | solution.py:709
  12.8 1.7 copy-start.19
  21.1 79.2 %all-to-all-start = ((f32[128,1,6272]{2,1,0:T(1,128)}), f32[128,1,6272]{2,1,0:T(1,128)S(1)}, u32[]{:S(2)}, u32[]{:S(2)}) async-start(f32[128,1,6272]{2,1,0:T(1,128)} %bitcast.6), calls=%async_computation | async-start | bytes 6422528 | tf_op jit(solution)/shard_map/all_to_all | solution.py:713
  30.3 47.6 %collective-permute-start.1 = (f32[5,4,16,256]{3,2,1,0:T(8,128)}, f32[5,4,16,256]{3,2,1,0:T(8,128)S(1)}, u32[]{:S(2)}, u32[]{:S(2)}) collective-permute-start(f32[5,4,16,256]{3,2,1,0:T(8,128)} %shard_map.112.refs_0_), channel_id=1, source_target_pairs={{2,4},{4,2},{6,8},{8,6},{10,12},{12,10},{14,16},{16,14},{18,20},{2... | collective-permute-start | bytes 983048 | tf_op jit(solution)/shard_map/ppermute | solution.py:709
  37.6 40.3 %collective-permute-start = (f32[5,4,16,256]{3,2,1,0:T(8,128)}, f32[5,4,16,256]{3,2,1,0:T(8,128)S(1)}, u32[]{:S(2)}, u32[]{:S(2)}) collective-permute-start(f32[5,4,16,256]{3,2,1,0:T(8,128)} %shard_map.112.refs_0_), channel_id=1, source_target_pairs={{0,2},{2,0},{4,6},{6,4},{8,10},{10,8},{12,14},{14,12},{16,18},{18,... | collective-permute-start | bytes 983048 | tf_op jit(solution)/shard_map/ppermute | solution.py:709
  37.6 40.8 %collective-permute-start.2 = (f32[5,4,16,256]{3,2,1,0:T(8,128)}, f32[5,4,16,256]{3,2,1,0:T(8,128)S(1)}, u32[]{:S(2)}, u32[]{:S(2)}) collective-permute-start(f32[5,4,16,256]{3,2,1,0:T(8,128)} %shard_map.112.refs_0_), channel_id=1, source_target_pairs={{0,1},{1,0},{2,3},{3,2},{4,5},{5,4},{6,7},{7,6},{8,9},{9,8},{10,11... | collective-permute-start | bytes 983048 | tf_op jit(solution)/shard_map/ppermute | solution.py:709
  77.9 1.6 collective-permute-start.4
  77.9 2.1 %collective-permute-start.3 = (f32[5,4,16,256]{3,2,1,0:T(8,128)S(1)}, f32[5,4,16,256]{3,2,1,0:T(8,128)S(1)}, u32[]{:S(2)}, u32[]{:S(2)}) collective-permute-start(f32[5,4,16,256]{3,2,1,0:T(8,128)S(1)} %collective-permute-done.refs_1_), channel_id=1, source_target_pairs={{0,1},{1,0},{2,3},{3,2},{4,5},{5,4},{6,7},{7,6},{8,9},{9,8},{10,11... | collective-permute-start | bytes 983048 | tf_op jit(solution)/shard_map/ppermute | solution.py:709
  100.3 1.7 copy-start.1
  102.0 5.9 %copy-start.17 = (f32[5,2,16,256]{3,2,1,0:T(8,128)S(1)}, f32[5,2,16,256]{3,2,1,0:T(8,128)}, u32[]{:S(2)}) copy-start(f32[5,2,16,256]{3,2,1,0:T(8,128)} %copy-done.16) | copy-start | bytes 491524
  102.0 13.2 %copy-start = (f32[4,8,8,8,128]{4,3,2,1,0:T(8,128)S(1)}, f32[4,8,8,8,128]{4,3,2,1,0:T(8,128)}, u32[]{:S(2)}) copy-start(f32[4,8,8,8,128]{4,3,2,1,0:T(8,128)} %w.9) | copy-start | bytes 3145732
  102.1 51.5 %copy-start.3 = (f32[8,8,128]{2,1,0:T(8,128)S(1)}, f32[8,8,128]{2,1,0:T(8,128)}, u32[]{:S(2)}) copy-start(f32[8,8,128]{2,1,0:T(8,128)} %constant.18.clone.coef) | copy-start | bytes 98308
  102.1 74.0 %all-to-all-start.1 = ((f32[128,1,6272]{2,1,0:T(1,128)}), f32[128,1,6272]{2,1,0:T(1,128)}, u32[]{:S(2)}, u32[]{:S(2)}) async-start(f32[128,1,6272]{2,1,0:T(1,128)} %bitcast.5), calls=%async_computation.1 | async-start | bytes 6422528 | tf_op jit(solution)/shard_map/all_to_all | solution.py:713
  107.9 46.9 %copy-start.2 = (f32[128,1,6272]{2,1,0:T(1,128)S(1)}, f32[128,1,6272]{2,1,0:T(1,128)}, u32[]{:S(2)}) copy-start(f32[128,1,6272]{2,1,0:T(1,128)} %copy-done.1) | copy-start | bytes 9633796
  108.0 51.5 %collective-permute-start.6 = (f32[5,2,16,256]{3,2,1,0:T(8,128)S(1)}, f32[5,2,16,256]{3,2,1,0:T(8,128)}, u32[]{:S(2)}, u32[]{:S(2)}) collective-permute-start(f32[5,2,16,256]{3,2,1,0:T(8,128)S(1)} %copy-done.17), channel_id=1, source_target_pairs={{2,4},{4,2},{6,8},{8,6},{10,12},{12,10},{14,16},{16,14},{18,20},{2... | collective-permute-start | bytes 491528 | tf_op jit(solution)/shard_map/ppermute | solution.py:709
  115.3 44.2 %collective-permute-start.5 = (f32[5,2,16,256]{3,2,1,0:T(8,128)S(1)}, f32[5,2,16,256]{3,2,1,0:T(8,128)}, u32[]{:S(2)}, u32[]{:S(2)}) collective-permute-start(f32[5,2,16,256]{3,2,1,0:T(8,128)S(1)} %copy-done.17), channel_id=1, source_target_pairs={{0,2},{2,0},{4,6},{6,4},{8,10},{10,8},{12,14},{14,12},{16,18},{18,... | collective-permute-start | bytes 491528 | tf_op jit(solution)/shard_map/ppermute | solution.py:709
  115.3 1.3 collective-permute-start.7
  115.4 38.2 %collective-permute-start.8 = (f32[8,8,128]{2,1,0:T(8,128)S(1)}, f32[8,8,128]{2,1,0:T(8,128)S(1)}, u32[]{:S(2)}, u32[]{:S(2)}) collective-permute-start(f32[8,8,128]{2,1,0:T(8,128)S(1)} %get-tuple-element.42), channel_id=1, source_target_pairs={{1,2},{2,1},{3,4},{4,3},{5,6},{6,5},{7,8},{8,7},{9,10},{10,9},{11,... | collective-permute-start | bytes 98312 | tf_op jit(solution)/shard_map/ppermute | solution.py:709
  159.5 24.6 %collective-permute-start.12 = (f32[5,2,16,256]{3,2,1,0:T(8,128)}, f32[5,2,16,256]{3,2,1,0:T(8,128)}, u32[]{:S(2)}, u32[]{:S(2)}) collective-permute-start(f32[5,2,16,256]{3,2,1,0:T(8,128)} %collective-permute-done.5.refs_4_), channel_id=1, source_target_pairs={{0,1},{1,0},{2,3},{3,2},{4,5},{5,4},{6,7},{7,6},{8,9},{9,8},{10,11... | collective-permute-start | bytes 491528 | tf_op jit(solution)/shard_map/ppermute | solution.py:709
  159.6 24.5 %collective-permute-start.13 = (f32[5,2,16,256]{3,2,1,0:T(8,128)}, f32[5,2,16,256]{3,2,1,0:T(8,128)}, u32[]{:S(2)}, u32[]{:S(2)}) collective-permute-start(f32[5,2,16,256]{3,2,1,0:T(8,128)} %collective-permute-done.6.refs_5_), channel_id=1, source_target_pairs={{0,1},{1,0},{2,3},{3,2},{4,5},{5,4},{6,7},{7,6},{8,9},{9,8},{10,11... | collective-permute-start | bytes 491528 | tf_op jit(solution)/shard_map/ppermute | solution.py:709
  160.1 14.2 %collective-permute-start.14 = (f32[3,8,8,128]{3,2,1,0:T(8,128)S(1)}, f32[3,8,8,128]{3,2,1,0:T(8,128)S(1)}, u32[]{:S(2)}, u32[]{:S(2)}) collective-permute-start(f32[3,8,8,128]{3,2,1,0:T(8,128)S(1)} %get-tuple-element.54), channel_id=1, source_target_pairs={{0,1},{1,0},{2,3},{3,2},{4,5},{5,4},{6,7},{7,6},{8,9},{9,8},{10,11... | collective-permute-start | bytes 294920 | tf_op jit(solution)/shard_map/ppermute | solution.py:709
  160.2 14.1 %collective-permute-start.15 = (f32[3,8,8,128]{3,2,1,0:T(8,128)S(1)}, f32[3,8,8,128]{3,2,1,0:T(8,128)S(1)}, u32[]{:S(2)}, u32[]{:S(2)}) collective-permute-start(f32[3,8,8,128]{3,2,1,0:T(8,128)S(1)} %get-tuple-element.55), channel_id=1, source_target_pairs={{1,2},{2,1},{3,4},{4,3},{5,6},{6,5},{7,8},{8,7},{9,10},{10,9},{11,... | collective-permute-start | bytes 294920 | tf_op jit(solution)/shard_map/ppermute | solution.py:709
  160.7 9.6 %collective-permute-start.17 = (f32[8,8,128]{2,1,0:T(8,128)S(1)}, f32[8,8,128]{2,1,0:T(8,128)S(1)}, u32[]{:S(2)}, u32[]{:S(2)}) collective-permute-start(f32[8,8,128]{2,1,0:T(8,128)S(1)} %get-tuple-element.56), channel_id=1, source_target_pairs={{2,4},{4,2},{6,8},{8,6},{10,12},{12,10},{14,16},{16,14},{18,20},{2... | collective-permute-start | bytes 98312 | tf_op jit(solution)/shard_map/ppermute | solution.py:709
  170.4 3.9 %collective-permute-start.16 = (f32[8,8,128]{2,1,0:T(8,128)S(1)}, f32[8,8,128]{2,1,0:T(8,128)S(1)}, u32[]{:S(2)}, u32[]{:S(2)}) collective-permute-start(f32[8,8,128]{2,1,0:T(8,128)S(1)} %get-tuple-element.49), channel_id=1, source_target_pairs={{0,2},{2,0},{4,6},{6,4},{8,10},{10,8},{12,14},{14,12},{16,18},{18,... | collective-permute-start | bytes 98312 | tf_op jit(solution)/shard_map/ppermute | solution.py:709
  176.0 8.0 %copy-start.7 = (f32[5,4,16,256]{3,2,1,0:T(8,128)S(1)}, f32[5,4,16,256]{3,2,1,0:T(8,128)}, u32[]{:S(2)}) copy-start(f32[5,4,16,256]{3,2,1,0:T(8,128)} %copy-done.6) | copy-start | bytes 983044
  176.1 8.0 %copy-start.11 = (f32[5,1,32,256]{3,2,1,0:T(8,128)S(1)}, f32[5,1,32,256]{3,2,1,0:T(8,128)}, u32[]{:S(2)}) copy-start(f32[5,1,32,256]{3,2,1,0:T(8,128)} %copy-done.10) | copy-start | bytes 491524
  176.1 8.0 %copy-start.13 = (f32[5,1,32,256]{3,2,1,0:T(8,128)S(1)}, f32[5,1,32,256]{3,2,1,0:T(8,128)}, u32[]{:S(2)}) copy-start(f32[5,1,32,256]{3,2,1,0:T(8,128)} %copy-done.12) | copy-start | bytes 491524
  179.9 15.6 %collective-permute-start.18 = (f32[2,8,8,128]{3,2,1,0:T(8,128)S(1)}, f32[2,8,8,128]{3,2,1,0:T(8,128)S(1)}, u32[]{:S(2)}, u32[]{:S(2)}) collective-permute-start(f32[2,8,8,128]{3,2,1,0:T(8,128)S(1)} %get-tuple-element.67), channel_id=1, source_target_pairs={{0,1},{1,0},{2,3},{3,2},{4,5},{5,4},{6,7},{7,6},{8,9},{9,8},{10,11... | collective-permute-start | bytes 196616 | tf_op jit(solution)/shard_map/ppermute | solution.py:709
  179.9 15.5 %collective-permute-start.19 = (f32[2,8,8,128]{3,2,1,0:T(8,128)S(1)}, f32[2,8,8,128]{3,2,1,0:T(8,128)S(1)}, u32[]{:S(2)}, u32[]{:S(2)}) collective-permute-start(f32[2,8,8,128]{3,2,1,0:T(8,128)S(1)} %get-tuple-element.68), channel_id=1, source_target_pairs={{1,2},{2,1},{3,4},{4,3},{5,6},{6,5},{7,8},{8,7},{9,10},{10,9},{11,... | collective-permute-start | bytes 196616 | tf_op jit(solution)/shard_map/ppermute | solution.py:709
  191.7 1.1 copy-start.5
  (11 other events, 7.6 us)

commit v3 on v2

--- a/solution.py
+++ b/solution.py
@@ -17,7 +17,8 @@
 BF16 = jnp.bfloat16
 AXES = ("flow", "group")
 VMEM_LIMIT = 26 * 2**20
-WHOLE_VMEM = 58 * 2**20
+WHOLE_VMEM = 63_050_000
+PACK_VMEM = 55_000_000
 
 
 def legendre_pair(nodes, degree):
@@ -61,7 +62,8 @@
     if specs is not None:
         extra["in_specs"] = [pl.BlockSpec(memory_space=kinds[k]) for k in specs]
     if out_specs is not None:
-        extra["out_specs"] = pl.BlockSpec(memory_space=kinds[out_specs])
+        places = [pl.BlockSpec(memory_space=kinds[k]) for k in out_specs]
+        extra["out_specs"] = places if len(places) > 1 else places[0]
     return pl.pallas_call(
         body,
         out_shape=out_shape,
@@ -85,7 +87,9 @@
     return lax.dot_general(left, right, (dims, ((), ())), preferred_element_type=F32)
 
 
-def fields_body(rho_ref, vel_ref, pre_ref, f_ref):
+def fields_body(rho_ref, vel_ref, pre_ref, me_ref, mb_ref, mt_ref, f_ref, margin_ref):
+    for row, ref in enumerate((me_ref, mb_ref, mt_ref)):
+        margin_ref[row : row + 1, :] = ref[...]
     rho = rho_ref[...]
     v = [vel_ref[d] for d in range(3)]
     kinetic = v[0] * v[0] + v[1] * v[1] + v[2] * v[2]
@@ -123,29 +127,27 @@
     lab_ref[...] = dot(owned.astype(BF16), spread, ((1,), (1,)))
 
 
-def pack_body(
-    own_ref,
-    part_ref,
-    even_ref,
-    odd_ref,
-    tab_hbm,
-    sel_ref,
-    lab_ref,
-    out_hbm,
-    src,
-    mp,
-    tab,
-    out,
-    sems,
-    *,
-    paired,
-):
+def pack_body(own_ref, part_ref, even_ref, odd_ref, tab_hbm, *refs, paired):
+    if paired:
+        margin_ref, out_hbm, sel_hbm, lab_hbm, sel_ref, lab_ref = refs[:6]
+    else:
+        sel_ref, lab_ref, out_hbm = refs[:3]
+    src, mp, tab, out, sems = refs[-5:]
     planes, rows, width = own_ref.shape[1:]
     tables, nodes = tab.shape[0], tab.shape[1]
     blocks = 128 // tables
     loads = [pltpu.make_async_copy(tab_hbm.at[t], tab.at[t], sems.at[t]) for t in range(tables)]
     for load in loads:
         load.start()
+    if paired:
+        margin = [margin_ref.at[pl.ds(row, 1)] for row in range(3)]
+        slots_body(*margin, sel_ref, lab_ref, blocks=blocks)
+        kept = [
+            pltpu.make_async_copy(sel_ref, sel_hbm, sems.at[tables + 2]),
+            pltpu.make_async_copy(lab_ref, lab_hbm, sems.at[tables + 3]),
+        ]
+        for copy in kept:
+            copy.start()
     low_flow = flags()[0] == 0
 
     def pick(when, other):
@@ -210,10 +212,10 @@
             high, low = halves(mapped[c * blocks : (c + 1) * blocks])
             mp[c, t * blocks : (t + 1) * blocks, :] = high
             mp[c, 128 + t * blocks : 128 + (t + 1) * blocks, :] = low
-    devices = lab_ref.shape[0]
+    devices = sel_ref.shape[0] // CAP
     half = devices // 2
     groups = nodes // 128
-    stride = 3 * groups * CAP + 1
+    stride = out.shape[0] // devices
     out[pl.ds(stride - 1, devices, stride=stride), :] = lab_ref[...]
     stores = []
     for h in range(2):
@@ -229,7 +231,7 @@
         store = pltpu.make_async_copy(out.at[part], out_hbm.at[part], sems.at[tables + h])
         store.start()
         stores.append(store)
-    for store in stores:
+    for store in stores + (kept if paired else []):
         store.wait()
 
 
@@ -718,8 +720,6 @@
     lanes = wave.shape[-1]
     devices = lax.axis_size("flow") * lax.axis_size("group")
     kinds, nodes = tables.shape[:2]
-    stride = 3 * CAP * nodes // 128 + 1
-    blocks = planes * rows * width // nodes
 
     coef = np.stack([MATRIX[np.arange(NP), (np.arange(NP) + k) % NP] for k in range(NP)])
     coef = jnp.asarray(np.broadcast_to(coef[:, :, None], (NP, NP, lanes)).copy())
@@ -731,7 +731,12 @@
     v_part = trade(velocity, "group", 0)
 
     block = sds(5, planes, rows, width)
-    fields = call(fields_body, block, 1_000_000, limit=WHOLE_VMEM)(density, velocity, pressure)
+    fields, margin = call(
+        fields_body,
+        (block, sds(8, margin_element.shape[1], dtype=jnp.int32)),
+        1_000_000,
+        limit=WHOLE_VMEM,
+    )(density, velocity, pressure, margin_element, margin_block, margin_table)
 
     def surround(own):
         even = trade(own, "flow", 0)
@@ -743,33 +748,36 @@
     pieces = surround(fields)
     others = swap_rows(pieces)
 
-    select, labels = call(
-        lambda *refs: slots_body(*refs, blocks=blocks),
-        (sds(CAP * devices, 256, dtype=BF16), sds(devices, 128)),
-        1_000_000,
-        limit=WHOLE_VMEM,
-    )(margin_element, margin_block, margin_table)
-
-    def send(paired, *speeds):
+    def send(speeds, extra, length, out_shape=(), **keys):
+        sent = sds(devices * length, 128)
         sent = call(
-            lambda *refs: pack_body(*refs, paired=paired),
-            sds(devices * stride, 128),
+            lambda *refs: pack_body(*refs, paired=bool(out_shape)),
+            (sent, *out_shape) if out_shape else sent,
             8_000_000,
             scratch=(
+                *(pltpu.VMEM(o.shape, o.dtype) for o in out_shape),
                 pltpu.VMEM((2, 3 * planes * rows, 128), F32),
                 pltpu.VMEM((3, 256, nodes), BF16),
                 pltpu.VMEM(tables.shape, F32),
-                pltpu.VMEM((devices * stride, 128), F32),
-                pltpu.SemaphoreType.DMA((kinds + 2,)),
+                pltpu.VMEM((devices * length, 128), F32),
+                pltpu.SemaphoreType.DMA((kinds + 4,)),
             ),
-            specs="vvvvhvv",
-            out_specs="h",
-            limit=WHOLE_VMEM,
-        )(*speeds, tables, select, labels)
-        sent = exchange_all(sent.reshape(devices, 1, stride * 128))
-        return sent.reshape(devices * stride, 128)
-
-    arrived_1 = send(True, velocity, v_part, v_even, v_odd)
+            limit=PACK_VMEM,
+            **keys,
+        )(*speeds, tables, *extra)
+        sent, *kept = sent if out_shape else (sent,)
+        sent = exchange_all(sent.reshape(devices, 1, length * 128))
+        return sent.reshape(devices * length, 128), kept
+
+    stride = 3 * CAP * nodes // 128 + 1
+    arrived_1, kept = send(
+        (velocity, v_part, v_even, v_odd),
+        (margin,),
+        stride,
+        (sds(CAP * devices, 256, dtype=BF16), sds(devices, 128)),
+        specs="vvvvhv",
+        out_specs="hhh",
+    )
 
     speed = sds(3, planes, rows, width)
     thin = sds(3, 1, rows, width)
@@ -781,7 +789,7 @@
         60_000_000,
         scratch=[wide] * 4,
     )(*pieces, *others)
-    arrived_2 = send(False, own, part, high, low)
+    arrived_2, _ = send((own, part, high, low), kept, stride, specs="vvvvhvv", out_specs="h")
     mids = surround(mid)[1:]
 
     def finish_flow(mids):

time: 197 us -> 197 us (level)
  Pallas kernels: 46.5 us -> 42.4 us
    pallas_call x4 -> x3, Pallas kernels: 15.3 us -> 11.2 us  [the longest x2 9.45 us: send(): call(lambda *refs: pack_body(*refs, paired=bool(out_shape)), (sent, *out_...]
  transfers between devices with their start and end apart: 22 -> 22, of which waited for: 9 -> 9; matrix products, arithmetic and copies ran while one was open for 0% -> 0% of each run, Pallas kernels for 20% -> 18%
where the time goes in v3:
time: 197 us; the launch traced here: 196 us
  waiting for transfers between devices  95.8 us (49%)
  starting transfers between devices  44.7 us (23%)
  Pallas kernels  42.4 us (22%)
  local copies, waits for them, and re-layouts  12.2 us (6%)
    ppermute x20, waiting for transfers between devices, trade(): return lax.ppermute(value, axis, pairs)  95.8 us
    ppermute x20, starting transfers between devices, trade(): return lax.ppermute(value, axis, pairs)  31.5 us
    all_to_all x2, starting transfers between devices, exchange_all(): return lax.all_to_all(value, AXES, split_axis=0, concat_axis=0, tiled=True)  13.3 us
    unnamed x42, local copies, waits for them, and re-layouts  11.3 us
    pallas_call x2, Pallas kernels, send(): call(lambda *refs: pack_body(*refs, paired=bool(out_shape)), (sent, *out_...  9.45 us
    pallas_call x1, Pallas kernels, advance(): call(first_flow_body, (block, block, sds(5, planes - 2, rows, width), edg...  8.16 us
    pallas_call x1, Pallas kernels, finish_flow(): call(last_flow_body, block, 30000000, scratch=[wide] * 4)  7.61 us
  transfers between devices with their start and end apart: 22, of which 9 were waited for; matrix products, arithmetic and copies ran while one was open for 0% of the time, Pallas kernels for 18%

profile of v3, /device:TPU:0, one launch (start us, length us, event | category | flops | bytes accessed | tf_op | source)
XLA Modules:
  0.0 196.1 jit_solution(12906504524276732433)
XLA Ops:
  0.7 0.8 constant_dynamic-slice_fusion
  1.6 8.9 %collective-permute-start.11 = (f32[3,1,16,256]{3,2,1,0:T(8,128)S(1)}, f32[3,1,16,256]{3,2,1,0:T(8,128)S(1)}, u32[]{:S(2)}, u32[]{:S(2)}) collective-permute-start(f32[3,1,16,256]{3,2,1,0:T(8,128)S(1)} %get-tuple-element.75), channel_id=1, source_target_pairs={{2,4},{4,2},{6,8},{8,6},{10,12},{12,10},{14,16},{16,14},{18,20},{2... | collective-permute-start | bytes 147464 | tf_op jit(solution)/shard_map/ppermute | solution.py:711
  10.4 1.7 shard_map.112
  12.8 1.7 collective-permute-done.10.refs_2_
  14.5 0.9 copy-done.4
  16.1 4.8 %shard_map.116 = (f32[6272,128]{1,0:T(8,128)}, bf16[512,256]{1,0:T(8,128)(2,1)S(1)}, f32[128,128]{1,0:T(8,128)S(1)}) custom-call(f32[3,4,16,256]{3,2,1,0:T(8,128)S(1)} %copy-done.4, f32[3,4,16,256]{3,2,1,0:T(8,128)S(1)} %collective-permute-done.9.refs_1_, f32[3,1,16,256]{3,2,1,0:T(8,128)S(1)} %collective-permute-done.10.refs_2_, ...), custom_call_target="tpu_custom_call" | custom-call | flops 8000000 | bytes 4000000 | tf_op jit(solution)/shard_map/pallas_call | solution.py:753
  22.2 7.4 %all-to-all-start = ((f32[128,1,6272]{2,1,0:T(1,128)}), f32[128,1,6272]{2,1,0:T(1,128)S(1)}, u32[]{:S(2)}, u32[]{:S(2)}) async-start(f32[128,1,6272]{2,1,0:T(1,128)} %bitcast.6), calls=%async_computation | async-start | bytes 6422528 | tf_op jit(solution)/shard_map/all_to_all | solution.py:715
  29.7 7.4 %collective-permute-start.1 = (f32[5,4,16,256]{3,2,1,0:T(8,128)S(1)}, f32[5,4,16,256]{3,2,1,0:T(8,128)S(1)}, u32[]{:S(2)}, u32[]{:S(2)}) collective-permute-start(f32[5,4,16,256]{3,2,1,0:T(8,128)S(1)} %copy-done.8), channel_id=1, source_target_pairs={{2,4},{4,2},{6,8},{8,6},{10,12},{12,10},{14,16},{16,14},{18,20},{2... | collective-permute-start | bytes 983048 | tf_op jit(solution)/shard_map/ppermute | solution.py:711
  37.0 41.9 %collective-permute-done.1.refs_2_ = f32[5,4,16,256]{3,2,1,0:T(8,128)S(1)} collective-permute-done((f32[5,4,16,256]{3,2,1,0:T(8,128)S(1)}, f32[5,4,16,256]{3,2,1,0:T(8,128)S(1)}, u32[]{:S(2)}, u32[]{:S(2)}) %collective-permute-start.1) | collective-permute-done | bytes 327712 | tf_op jit(solution)/shard_map/ppermute | solution.py:711
  79.5 1.1 collective-permute-done.4.refs_5_
  81.1 1.0 copy-done.9
  82.0 8.2 %shard_map.113 = (f32[5,4,16,256]{3,2,1,0:T(8,128)S(1)}, f32[5,4,16,256]{3,2,1,0:T(8,128)S(1)}, f32[5,2,16,256]{3,2,1,0:T(8,128)S(1)}, f32[5,1,32,256]{3,2,1,0:T...) custom-call(f32[5,4,16,256]{3,2,1,0:T(8,128)S(1)} %copy-done.9, ...), custom_call_target="tpu_custom_call" | custom-call | flops 60000000 | bytes 4000000 | tf_op jit(solution)/shard_map/pallas_call | solution.py:786
  92.9 0.9 copy-done.11
  93.9 0.8 copy-done.17
  94.7 4.7 %shard_map.121 = f32[6272,128]{1,0:T(8,128)} custom-call(f32[3,4,16,256]{3,2,1,0:T(8,128)S(1)} %get-tuple-element.63.refs_0_, f32[3,4,16,256]{3,2,1,0:T(8,128)S(1)} %get-tuple-element.64.refs_1_, f32[3,1,16,256]{3,2,1,0:T(8,128)S(1)} %get-tuple-element.65.refs_2_, f32[3,1,16,256]{3,2,1,0:T(8,128)S(1)} %get-tuple-element.66.refs_3_, f32[4,512,512]{2,1,0:T(8,128)} %refs_4_.3, ...), custom_call_target="tpu_custom_call" | custom-call | flops 8000000 | bytes 4000000 | tf_op jit(solution)/shard_map/pallas_call | solution.py:753
  99.5 1.7 copy-done.1
  101.2 5.9 %all-to-all-start.1 = ((f32[128,1,6272]{2,1,0:T(1,128)}), f32[128,1,6272]{2,1,0:T(1,128)}, u32[]{:S(2)}, u32[]{:S(2)}) async-start(f32[128,1,6272]{2,1,0:T(1,128)} %bitcast.5), calls=%async_computation.1 | async-start | bytes 6422528 | tf_op jit(solution)/shard_map/all_to_all | solution.py:715
  107.1 7.3 %collective-permute-start.6 = (f32[5,2,16,256]{3,2,1,0:T(8,128)S(1)}, f32[5,2,16,256]{3,2,1,0:T(8,128)}, u32[]{:S(2)}, u32[]{:S(2)}) collective-permute-start(f32[5,2,16,256]{3,2,1,0:T(8,128)S(1)} %copy-done.20), channel_id=1, source_target_pairs={{2,4},{4,2},{6,8},{8,6},{10,12},{12,10},{14,16},{16,14},{18,20},{2... | collective-permute-start | bytes 491528 | tf_op jit(solution)/shard_map/ppermute | solution.py:711
  114.5 1.0 collective-permute-start.8
  115.7 37.0 %collective-permute-done.8.odd = f32[8,8,128]{2,1,0:T(8,128)S(1)} collective-permute-done((f32[8,8,128]{2,1,0:T(8,128)S(1)}, f32[8,8,128]{2,1,0:T(8,128)S(1)}, u32[]{:S(2)}, u32[]{:S(2)}) %collective-permute-start.8) | collective-permute-done | bytes 32800 | tf_op jit(solution)/shard_map/ppermute | solution.py:711
  152.7 1.2 shard_map.115.r0
  153.9 1.9 shard_map.117
  155.9 2.7 %shard_map.118 = (f32[4,8,8,8,128]{4,3,2,1,0:T(8,128)S(1)}, f32[4,8,8,8,128]{4,3,2,1,0:T(8,128)S(1)}, f32[3,8,8,128]{3,2,1,0:T(8,128)S(1)}, f32[3,8,8,128]{3,2,1...) custom-call(f32[4,8,8,8,128]{4,3,2,1,0:T(8,128)S(1)} %copy-done, ...), custom_call_target="tpu_custom_call" | custom-call | flops 16000000 | bytes 4000000 | tf_op jit(solution)/shard_map/pallas_call | solution.py:828
  160.7 8.8 %collective-permute-done.17.far_odd = f32[8,8,128]{2,1,0:T(8,128)S(1)} collective-permute-done((f32[8,8,128]{2,1,0:T(8,128)S(1)}, f32[8,8,128]{2,1,0:T(8,128)S(1)}, u32[]{:S(2)}, u32[]{:S(2)}) %collective-permute-start.17) | collective-permute-done | bytes 32800 | tf_op jit(solution)/shard_map/ppermute | solution.py:711
  169.5 3.9 %collective-permute-done.16.far_even = f32[8,8,128]{2,1,0:T(8,128)S(1)} collective-permute-done((f32[8,8,128]{2,1,0:T(8,128)S(1)}, f32[8,8,128]{2,1,0:T(8,128)S(1)}, u32[]{:S(2)}, u32[]{:S(2)}) %collective-permute-start.16) | collective-permute-done | bytes 32800 | tf_op jit(solution)/shard_map/ppermute | solution.py:711
  173.4 1.8 shard_map.120
  175.2 3.8 %shard_map.122 = (f32[3,8,8,8,128]{4,3,2,1,0:T(8,128)}, f32[4,8,8,8,128]{4,3,2,1,0:T(8,128)S(1)}, f32[2,8,8,128]{3,2,1,0:T(8,128)S(1)}, f32[2,8,8,128]{3,2,1,0:T(8,128)S(1)}) custom-call(f32[4,8,8,8,128]{4,3,2,1,0:T(8,128)S(1)} %get-tuple-element.61.w, f32[4,8,8,8,128]{4,3,2,1,0:T(8,128)S(1)} %get-tuple-element.62.r0, f32[6272,128]{1,0:T(8,128)} %bitcast.3.arrived_hbm, ...), custom_call_target="tpu_custom_call" | custom-call | flops 12000000 | bytes 4000000 | tf_op jit(solution)/shard_map/pallas_call | solution.py:839
  179.1 4.1 %collective-permute-start.19 = (f32[2,8,8,128]{3,2,1,0:T(8,128)S(1)}, f32[2,8,8,128]{3,2,1,0:T(8,128)S(1)}, u32[]{:S(2)}, u32[]{:S(2)}) collective-permute-start(f32[2,8,8,128]{3,2,1,0:T(8,128)S(1)} %get-tuple-element.74), channel_id=1, source_target_pairs={{1,2},{2,1},{3,4},{4,3},{5,6},{6,5},{7,8},{8,7},{9,10},{10,9},{11,... | collective-permute-start | bytes 196616 | tf_op jit(solution)/shard_map/ppermute | solution.py:711
  183.2 7.6 %shard_map.119 = f32[5,4,16,256]{3,2,1,0:T(8,128)} custom-call(f32[5,4,16,256]{3,2,1,0:T(8,128)S(1)} %get-tuple-element.40.refs_0_, f32[5,4,16,256]{3,2,1,0:T(8,128)S(1)} %copy-done.7, f32[5,1,32,256]{3,2,1,0:T(8,128)S(1)} %copy-done.13, f32[5,1,32,256]{3,2,1,0:T(8,128)S(1)} %copy-done.15, f32[5,2,16,256]{3,2,1,0:T(8,128)} %collective-permute-done.5.refs_4_, ...), custom_call_target="tpu_custom_call" | custom-call | flops 30000000 | bytes 4000000 | tf_op jit(solution)/shard_map/pallas_call | solution.py:796
  190.9 1.1 copy-done.5
  192.0 2.6 %shard_map.123 = (f32[4,8,8,8,128]{4,3,2,1,0:T(8,128)S(1)}, f32[4,8,8,8,128]{4,3,2,1,0:T(8,128)S(1)}) custom-call(f32[4,8,8,8,128]{4,3,2,1,0:T(8,128)S(1)} %get-tuple-element.61.w, f32[4,8,8,8,128]{4,3,2,1,0:T(8,128)S(1)} %get-tuple-element.69.s1, f32[3,8,8,8,128]{4,3,2,1,0:T(8,128)S(1)} %copy-done.5, f32[8,8,128]{2,1,0:T(8,128)S(1)} %copy-done.3), custom_call_target="tpu_custom_call" | custom-call | flops 16000000 | bytes 4000000 | tf_op jit(solution)/shard_map/pallas_call | solution.py:841
  194.6 1.5 shard_map.124
  (68 shorter events, 9.0 us)
Async XLA Ops:
  0.6 13.9 %collective-permute-start.9 = (f32[3,4,16,256]{3,2,1,0:T(8,128)}, f32[3,4,16,256]{3,2,1,0:T(8,128)S(1)}, u32[]{:S(2)}, u32[]{:S(2)}) collective-permute-start(f32[3,4,16,256]{3,2,1,0:T(8,128)} %refs_0_.1), channel_id=1, source_target_pairs={{0,1},{1,0},{2,3},{3,2},{4,5},{5,4},{6,7},{7,6},{8,9},{9,8},{10,11... | collective-permute-start | bytes 589832 | tf_op jit(solution)/shard_map/ppermute | solution.py:711
  1.6 11.2 %collective-permute-start.11 = (f32[3,1,16,256]{3,2,1,0:T(8,128)S(1)}, f32[3,1,16,256]{3,2,1,0:T(8,128)S(1)}, u32[]{:S(2)}, u32[]{:S(2)}) collective-permute-start(f32[3,1,16,256]{3,2,1,0:T(8,128)S(1)} %get-tuple-element.75), channel_id=1, source_target_pairs={{2,4},{4,2},{6,8},{8,6},{10,12},{12,10},{14,16},{16,14},{18,20},{2... | collective-permute-start | bytes 147464 | tf_op jit(solution)/shard_map/ppermute | solution.py:711
  10.4 4.1 %collective-permute-start.10 = (f32[3,1,16,256]{3,2,1,0:T(8,128)S(1)}, f32[3,1,16,256]{3,2,1,0:T(8,128)S(1)}, u32[]{:S(2)}, u32[]{:S(2)}) collective-permute-start(f32[3,1,16,256]{3,2,1,0:T(8,128)S(1)} %get-tuple-element.76), channel_id=1, source_target_pairs={{0,2},{2,0},{4,6},{6,4},{8,10},{10,8},{12,14},{14,12},{16,18},{18,... | collective-permute-start | bytes 147464 | tf_op jit(solution)/shard_map/ppermute | solution.py:711
  22.2 7.4 %copy-start.8 = (f32[5,4,16,256]{3,2,1,0:T(8,128)S(1)}, f32[5,4,16,256]{3,2,1,0:T(8,128)}, u32[]{:S(2)}) copy-start(f32[5,4,16,256]{3,2,1,0:T(8,128)} %get-tuple-element.39.refs_0_) | copy-start | bytes 983044
  22.2 77.2 %all-to-all-start = ((f32[128,1,6272]{2,1,0:T(1,128)}), f32[128,1,6272]{2,1,0:T(1,128)S(1)}, u32[]{:S(2)}, u32[]{:S(2)}) async-start(f32[128,1,6272]{2,1,0:T(1,128)} %bitcast.6), calls=%async_computation | async-start | bytes 6422528 | tf_op jit(solution)/shard_map/all_to_all | solution.py:715
  29.7 49.3 %collective-permute-start.1 = (f32[5,4,16,256]{3,2,1,0:T(8,128)S(1)}, f32[5,4,16,256]{3,2,1,0:T(8,128)S(1)}, u32[]{:S(2)}, u32[]{:S(2)}) collective-permute-start(f32[5,4,16,256]{3,2,1,0:T(8,128)S(1)} %copy-done.8), channel_id=1, source_target_pairs={{2,4},{4,2},{6,8},{8,6},{10,12},{12,10},{14,16},{16,14},{18,20},{2... | collective-permute-start | bytes 983048 | tf_op jit(solution)/shard_map/ppermute | solution.py:711
  37.0 41.9 %collective-permute-start = (f32[5,4,16,256]{3,2,1,0:T(8,128)S(1)}, f32[5,4,16,256]{3,2,1,0:T(8,128)S(1)}, u32[]{:S(2)}, u32[]{:S(2)}) collective-permute-start(f32[5,4,16,256]{3,2,1,0:T(8,128)S(1)} %copy-done.8), channel_id=1, source_target_pairs={{0,2},{2,0},{4,6},{6,4},{8,10},{10,8},{12,14},{14,12},{16,18},{18,... | collective-permute-start | bytes 983048 | tf_op jit(solution)/shard_map/ppermute | solution.py:711
  37.0 42.4 %collective-permute-start.2 = (f32[5,4,16,256]{3,2,1,0:T(8,128)S(1)}, f32[5,4,16,256]{3,2,1,0:T(8,128)S(1)}, u32[]{:S(2)}, u32[]{:S(2)}) collective-permute-start(f32[5,4,16,256]{3,2,1,0:T(8,128)S(1)} %copy-done.8), channel_id=1, source_target_pairs={{0,1},{1,0},{2,3},{3,2},{4,5},{5,4},{6,7},{7,6},{8,9},{9,8},{10,11... | collective-permute-start | bytes 983048 | tf_op jit(solution)/shard_map/ppermute | solution.py:711
  79.0 1.6 collective-permute-start.4
  79.0 2.1 %collective-permute-start.3 = (f32[5,4,16,256]{3,2,1,0:T(8,128)S(1)}, f32[5,4,16,256]{3,2,1,0:T(8,128)S(1)}, u32[]{:S(2)}, u32[]{:S(2)}) collective-permute-start(f32[5,4,16,256]{3,2,1,0:T(8,128)S(1)} %collective-permute-done.refs_1_), channel_id=1, source_target_pairs={{0,1},{1,0},{2,3},{3,2},{4,5},{5,4},{6,7},{7,6},{8,9},{9,8},{10,11... | collective-permute-start | bytes 983048 | tf_op jit(solution)/shard_map/ppermute | solution.py:711
  99.4 1.7 copy-start.1
  101.2 5.9 %copy-start.20 = (f32[5,2,16,256]{3,2,1,0:T(8,128)S(1)}, f32[5,2,16,256]{3,2,1,0:T(8,128)}, u32[]{:S(2)}) copy-start(f32[5,2,16,256]{3,2,1,0:T(8,128)} %copy-done.19) | copy-start | bytes 491524
  101.2 13.2 %copy-start = (f32[4,8,8,8,128]{4,3,2,1,0:T(8,128)S(1)}, f32[4,8,8,8,128]{4,3,2,1,0:T(8,128)}, u32[]{:S(2)}) copy-start(f32[4,8,8,8,128]{4,3,2,1,0:T(8,128)} %w.9) | copy-start | bytes 3145732
  101.2 51.5 %copy-start.3 = (f32[8,8,128]{2,1,0:T(8,128)S(1)}, f32[8,8,128]{2,1,0:T(8,128)}, u32[]{:S(2)}) copy-start(f32[8,8,128]{2,1,0:T(8,128)} %constant.18.clone.coef) | copy-start | bytes 98308
  101.2 74.0 %all-to-all-start.1 = ((f32[128,1,6272]{2,1,0:T(1,128)}), f32[128,1,6272]{2,1,0:T(1,128)}, u32[]{:S(2)}, u32[]{:S(2)}) async-start(f32[128,1,6272]{2,1,0:T(1,128)} %bitcast.5), calls=%async_computation.1 | async-start | bytes 6422528 | tf_op jit(solution)/shard_map/all_to_all | solution.py:715
  107.1 46.9 %copy-start.2 = (f32[128,1,6272]{2,1,0:T(1,128)S(1)}, f32[128,1,6272]{2,1,0:T(1,128)}, u32[]{:S(2)}) copy-start(f32[128,1,6272]{2,1,0:T(1,128)} %copy-done.1) | copy-start | bytes 9633796
  107.1 51.5 %collective-permute-start.6 = (f32[5,2,16,256]{3,2,1,0:T(8,128)S(1)}, f32[5,2,16,256]{3,2,1,0:T(8,128)}, u32[]{:S(2)}, u32[]{:S(2)}) collective-permute-start(f32[5,2,16,256]{3,2,1,0:T(8,128)S(1)} %copy-done.20), channel_id=1, source_target_pairs={{2,4},{4,2},{6,8},{8,6},{10,12},{12,10},{14,16},{16,14},{18,20},{2... | collective-permute-start | bytes 491528 | tf_op jit(solution)/shard_map/ppermute | solution.py:711
  114.4 44.2 %collective-permute-start.5 = (f32[5,2,16,256]{3,2,1,0:T(8,128)S(1)}, f32[5,2,16,256]{3,2,1,0:T(8,128)}, u32[]{:S(2)}, u32[]{:S(2)}) collective-permute-start(f32[5,2,16,256]{3,2,1,0:T(8,128)S(1)} %copy-done.20), channel_id=1, source_target_pairs={{0,2},{2,0},{4,6},{6,4},{8,10},{10,8},{12,14},{14,12},{16,18},{18,... | collective-permute-start | bytes 491528 | tf_op jit(solution)/shard_map/ppermute | solution.py:711
  114.4 1.3 collective-permute-start.7
  114.5 38.2 %collective-permute-start.8 = (f32[8,8,128]{2,1,0:T(8,128)S(1)}, f32[8,8,128]{2,1,0:T(8,128)S(1)}, u32[]{:S(2)}, u32[]{:S(2)}) collective-permute-start(f32[8,8,128]{2,1,0:T(8,128)S(1)} %get-tuple-element.46), channel_id=1, source_target_pairs={{1,2},{2,1},{3,4},{4,3},{5,6},{6,5},{7,8},{8,7},{9,10},{10,9},{11,... | collective-permute-start | bytes 98312 | tf_op jit(solution)/shard_map/ppermute | solution.py:711
  158.6 24.6 %collective-permute-start.12 = (f32[5,2,16,256]{3,2,1,0:T(8,128)}, f32[5,2,16,256]{3,2,1,0:T(8,128)}, u32[]{:S(2)}, u32[]{:S(2)}) collective-permute-start(f32[5,2,16,256]{3,2,1,0:T(8,128)} %collective-permute-done.5.refs_4_), channel_id=1, source_target_pairs={{0,1},{1,0},{2,3},{3,2},{4,5},{5,4},{6,7},{7,6},{8,9},{9,8},{10,11... | collective-permute-start | bytes 491528 | tf_op jit(solution)/shard_map/ppermute | solution.py:711
  158.7 24.5 %collective-permute-start.13 = (f32[5,2,16,256]{3,2,1,0:T(8,128)}, f32[5,2,16,256]{3,2,1,0:T(8,128)}, u32[]{:S(2)}, u32[]{:S(2)}) collective-permute-start(f32[5,2,16,256]{3,2,1,0:T(8,128)} %collective-permute-done.6.refs_5_), channel_id=1, source_target_pairs={{0,1},{1,0},{2,3},{3,2},{4,5},{5,4},{6,7},{7,6},{8,9},{9,8},{10,11... | collective-permute-start | bytes 491528 | tf_op jit(solution)/shard_map/ppermute | solution.py:711
  159.2 14.2 %collective-permute-start.14 = (f32[3,8,8,128]{3,2,1,0:T(8,128)S(1)}, f32[3,8,8,128]{3,2,1,0:T(8,128)S(1)}, u32[]{:S(2)}, u32[]{:S(2)}) collective-permute-start(f32[3,8,8,128]{3,2,1,0:T(8,128)S(1)} %get-tuple-element.58), channel_id=1, source_target_pairs={{0,1},{1,0},{2,3},{3,2},{4,5},{5,4},{6,7},{7,6},{8,9},{9,8},{10,11... | collective-permute-start | bytes 294920 | tf_op jit(solution)/shard_map/ppermute | solution.py:711
  159.3 14.1 %collective-permute-start.15 = (f32[3,8,8,128]{3,2,1,0:T(8,128)S(1)}, f32[3,8,8,128]{3,2,1,0:T(8,128)S(1)}, u32[]{:S(2)}, u32[]{:S(2)}) collective-permute-start(f32[3,8,8,128]{3,2,1,0:T(8,128)S(1)} %get-tuple-element.59), channel_id=1, source_target_pairs={{1,2},{2,1},{3,4},{4,3},{5,6},{6,5},{7,8},{8,7},{9,10},{10,9},{11,... | collective-permute-start | bytes 294920 | tf_op jit(solution)/shard_map/ppermute | solution.py:711
  159.9 9.6 %collective-permute-start.17 = (f32[8,8,128]{2,1,0:T(8,128)S(1)}, f32[8,8,128]{2,1,0:T(8,128)S(1)}, u32[]{:S(2)}, u32[]{:S(2)}) collective-permute-start(f32[8,8,128]{2,1,0:T(8,128)S(1)} %get-tuple-element.60), channel_id=1, source_target_pairs={{2,4},{4,2},{6,8},{8,6},{10,12},{12,10},{14,16},{16,14},{18,20},{2... | collective-permute-start | bytes 98312 | tf_op jit(solution)/shard_map/ppermute | solution.py:711
  169.5 3.9 %collective-permute-start.16 = (f32[8,8,128]{2,1,0:T(8,128)S(1)}, f32[8,8,128]{2,1,0:T(8,128)S(1)}, u32[]{:S(2)}, u32[]{:S(2)}) collective-permute-start(f32[8,8,128]{2,1,0:T(8,128)S(1)} %get-tuple-element.53), channel_id=1, source_target_pairs={{0,2},{2,0},{4,6},{6,4},{8,10},{10,8},{12,14},{14,12},{16,18},{18,... | collective-permute-start | bytes 98312 | tf_op jit(solution)/shard_map/ppermute | solution.py:711
  175.2 8.0 %copy-start.7 = (f32[5,4,16,256]{3,2,1,0:T(8,128)S(1)}, f32[5,4,16,256]{3,2,1,0:T(8,128)}, u32[]{:S(2)}) copy-start(f32[5,4,16,256]{3,2,1,0:T(8,128)} %copy-done.6) | copy-start | bytes 983044
  175.2 8.0 %copy-start.13 = (f32[5,1,32,256]{3,2,1,0:T(8,128)S(1)}, f32[5,1,32,256]{3,2,1,0:T(8,128)}, u32[]{:S(2)}) copy-start(f32[5,1,32,256]{3,2,1,0:T(8,128)} %copy-done.12) | copy-start | bytes 491524
  175.2 8.0 %copy-start.15 = (f32[5,1,32,256]{3,2,1,0:T(8,128)S(1)}, f32[5,1,32,256]{3,2,1,0:T(8,128)}, u32[]{:S(2)}) copy-start(f32[5,1,32,256]{3,2,1,0:T(8,128)} %copy-done.14) | copy-start | bytes 491524
  179.0 15.6 %collective-permute-start.18 = (f32[2,8,8,128]{3,2,1,0:T(8,128)S(1)}, f32[2,8,8,128]{3,2,1,0:T(8,128)S(1)}, u32[]{:S(2)}, u32[]{:S(2)}) collective-permute-start(f32[2,8,8,128]{3,2,1,0:T(8,128)S(1)} %get-tuple-element.73), channel_id=1, source_target_pairs={{0,1},{1,0},{2,3},{3,2},{4,5},{5,4},{6,7},{7,6},{8,9},{9,8},{10,11... | collective-permute-start | bytes 196616 | tf_op jit(solution)/shard_map/ppermute | solution.py:711
  179.1 15.5 %collective-permute-start.19 = (f32[2,8,8,128]{3,2,1,0:T(8,128)S(1)}, f32[2,8,8,128]{3,2,1,0:T(8,128)S(1)}, u32[]{:S(2)}, u32[]{:S(2)}) collective-permute-start(f32[2,8,8,128]{3,2,1,0:T(8,128)S(1)} %get-tuple-element.74), channel_id=1, source_target_pairs={{1,2},{2,1},{3,4},{4,3},{5,6},{6,5},{7,8},{8,7},{9,10},{10,9},{11,... | collective-permute-start | bytes 196616 | tf_op jit(solution)/shard_map/ppermute | solution.py:711
  190.9 1.1 copy-start.5
  (11 other events, 8.5 us)

commit v4 on v3

--- a/solution.py
+++ b/solution.py
@@ -512,7 +512,7 @@
     )
 
 
-def unpack_body(w, r0, arrived_hbm, coef, f, s1, even, odd, arrived, wide, sums, sems):
+def unpack_body(w, r0, arrived_hbm, coef, f_out, s1, even, odd, arrived, wide, sums, sems, f):
     lanes = w.shape[-1]
     groups = sums.shape[0]
     stride = groups * CAP + 1
@@ -547,6 +547,8 @@
                 at = g * 128 // NP + row_of
                 c, i, j = at // (NP * NP), at // NP % NP, at % NP
                 f[c, i, j] = nodes[row_of * NP : (row_of + 1) * NP, :]
+    keep = pltpu.make_async_copy(f, f_out, sems.at[2])
+    keep.start()
 
     def add(i):
         for k in range(4):
@@ -581,6 +583,7 @@
         for slot, (up, down) in enumerate((now, then)):
             even[slot, j] = chosen(low_core, up[j], down[j])
             odd[slot, j] = chosen(low_core, down[j], up[j])
+    keep.wait()
 
 
 def middle_body(w, s1, f, coef, s2, r2, r1):
@@ -813,9 +816,11 @@
             pltpu.VMEM((devices * stride, 128), F32),
             pltpu.VMEM((2, CAP * devices // 2, 256), BF16),
             pltpu.VMEM((3 * nodes // 128, lanes, 256), F32),
-            pltpu.SemaphoreType.DMA((2,)),
+            pltpu.SemaphoreType.DMA((3,)),
+            pltpu.VMEM((3, *wave.shape[1:]), F32),
         ],
         specs="vvhv",
+        out_specs="hvvv",
     )
 
     def around(even, odd):

time: 197 us -> 197 us (level)
  no operation moved by 1% of the time
where the time goes in v4:
time: 197 us; the launch traced here: 196 us
  waiting for transfers between devices  95.8 us (49%)
  starting transfers between devices  44.7 us (23%)
  Pallas kernels  42.3 us (21%)
  local copies, waits for them, and re-layouts  12.2 us (6%)
    ppermute x20, waiting for transfers between devices, trade(): return lax.ppermute(value, axis, pairs)  95.8 us
    ppermute x20, starting transfers between devices, trade(): return lax.ppermute(value, axis, pairs)  31.5 us
    all_to_all x2, starting transfers between devices, exchange_all(): return lax.all_to_all(value, AXES, split_axis=0, concat_axis=0, tiled=True)  13.3 us
    unnamed x42, local copies, waits for them, and re-layouts  11.3 us
    pallas_call x2, Pallas kernels, send(): call(lambda *refs: pack_body(*refs, paired=bool(out_shape)), (sent, *out_...  9.45 us
    pallas_call x1, Pallas kernels, advance(): call(first_flow_body, (block, block, sds(5, planes - 2, rows, width), edg...  8.16 us
    pallas_call x1, Pallas kernels, finish_flow(): call(last_flow_body, block, 30000000, scratch=[wide] * 4)  7.61 us
  transfers between devices with their start and end apart: 22, of which 9 were waited for; matrix products, arithmetic and copies ran while one was open for 0% of the time, Pallas kernels for 18%

profile of v4, /device:TPU:0, one launch (start us, length us, event | category | flops | bytes accessed | tf_op | source)
XLA Modules:
  0.0 196.0 jit_solution(16704509004203750566)
XLA Ops:
  0.7 0.8 constant_dynamic-slice_fusion
  1.6 8.9 %collective-permute-start.11 = (f32[3,1,16,256]{3,2,1,0:T(8,128)S(1)}, f32[3,1,16,256]{3,2,1,0:T(8,128)S(1)}, u32[]{:S(2)}, u32[]{:S(2)}) collective-permute-start(f32[3,1,16,256]{3,2,1,0:T(8,128)S(1)} %get-tuple-element.75), channel_id=1, source_target_pairs={{2,4},{4,2},{6,8},{8,6},{10,12},{12,10},{14,16},{16,14},{18,20},{2... | collective-permute-start | bytes 147464 | tf_op jit(solution)/shard_map/ppermute | solution.py:714
  10.4 1.7 shard_map.112
  12.8 1.7 collective-permute-done.10.refs_2_
  14.5 0.9 copy-done.4
  16.1 4.8 %shard_map.116 = (f32[6272,128]{1,0:T(8,128)}, bf16[512,256]{1,0:T(8,128)(2,1)S(1)}, f32[128,128]{1,0:T(8,128)S(1)}) custom-call(f32[3,4,16,256]{3,2,1,0:T(8,128)S(1)} %copy-done.4, f32[3,4,16,256]{3,2,1,0:T(8,128)S(1)} %collective-permute-done.9.refs_1_, f32[3,1,16,256]{3,2,1,0:T(8,128)S(1)} %collective-permute-done.10.refs_2_, ...), custom_call_target="tpu_custom_call" | custom-call | flops 8000000 | bytes 4000000 | tf_op jit(solution)/shard_map/pallas_call | solution.py:756
  22.2 7.4 %all-to-all-start = ((f32[128,1,6272]{2,1,0:T(1,128)}), f32[128,1,6272]{2,1,0:T(1,128)S(1)}, u32[]{:S(2)}, u32[]{:S(2)}) async-start(f32[128,1,6272]{2,1,0:T(1,128)} %bitcast.6), calls=%async_computation | async-start | bytes 6422528 | tf_op jit(solution)/shard_map/all_to_all | solution.py:718
  29.7 7.4 %collective-permute-start.1 = (f32[5,4,16,256]{3,2,1,0:T(8,128)S(1)}, f32[5,4,16,256]{3,2,1,0:T(8,128)S(1)}, u32[]{:S(2)}, u32[]{:S(2)}) collective-permute-start(f32[5,4,16,256]{3,2,1,0:T(8,128)S(1)} %copy-done.8), channel_id=1, source_target_pairs={{2,4},{4,2},{6,8},{8,6},{10,12},{12,10},{14,16},{16,14},{18,20},{2... | collective-permute-start | bytes 983048 | tf_op jit(solution)/shard_map/ppermute | solution.py:714
  37.0 41.9 %collective-permute-done.1.refs_2_ = f32[5,4,16,256]{3,2,1,0:T(8,128)S(1)} collective-permute-done((f32[5,4,16,256]{3,2,1,0:T(8,128)S(1)}, f32[5,4,16,256]{3,2,1,0:T(8,128)S(1)}, u32[]{:S(2)}, u32[]{:S(2)}) %collective-permute-start.1) | collective-permute-done | bytes 327712 | tf_op jit(solution)/shard_map/ppermute | solution.py:714
  79.5 1.1 collective-permute-done.4.refs_5_
  81.1 1.0 copy-done.9
  82.0 8.2 %shard_map.113 = (f32[5,4,16,256]{3,2,1,0:T(8,128)S(1)}, f32[5,4,16,256]{3,2,1,0:T(8,128)S(1)}, f32[5,2,16,256]{3,2,1,0:T(8,128)S(1)}, f32[5,1,32,256]{3,2,1,0:T...) custom-call(f32[5,4,16,256]{3,2,1,0:T(8,128)S(1)} %copy-done.9, ...), custom_call_target="tpu_custom_call" | custom-call | flops 60000000 | bytes 4000000 | tf_op jit(solution)/shard_map/pallas_call | solution.py:789
  92.9 0.9 copy-done.11
  93.9 0.8 copy-done.17
  94.7 4.7 %shard_map.121 = f32[6272,128]{1,0:T(8,128)} custom-call(f32[3,4,16,256]{3,2,1,0:T(8,128)S(1)} %get-tuple-element.63.refs_0_, f32[3,4,16,256]{3,2,1,0:T(8,128)S(1)} %get-tuple-element.64.refs_1_, f32[3,1,16,256]{3,2,1,0:T(8,128)S(1)} %get-tuple-element.65.refs_2_, f32[3,1,16,256]{3,2,1,0:T(8,128)S(1)} %get-tuple-element.66.refs_3_, f32[4,512,512]{2,1,0:T(8,128)} %refs_4_.3, ...), custom_call_target="tpu_custom_call" | custom-call | flops 8000000 | bytes 4000000 | tf_op jit(solution)/shard_map/pallas_call | solution.py:756
  99.5 1.7 copy-done.1
  101.2 5.9 %all-to-all-start.1 = ((f32[128,1,6272]{2,1,0:T(1,128)}), f32[128,1,6272]{2,1,0:T(1,128)}, u32[]{:S(2)}, u32[]{:S(2)}) async-start(f32[128,1,6272]{2,1,0:T(1,128)} %bitcast.5), calls=%async_computation.1 | async-start | bytes 6422528 | tf_op jit(solution)/shard_map/all_to_all | solution.py:718
  107.1 7.3 %collective-permute-start.6 = (f32[5,2,16,256]{3,2,1,0:T(8,128)S(1)}, f32[5,2,16,256]{3,2,1,0:T(8,128)}, u32[]{:S(2)}, u32[]{:S(2)}) collective-permute-start(f32[5,2,16,256]{3,2,1,0:T(8,128)S(1)} %copy-done.20), channel_id=1, source_target_pairs={{2,4},{4,2},{6,8},{8,6},{10,12},{12,10},{14,16},{16,14},{18,20},{2... | collective-permute-start | bytes 491528 | tf_op jit(solution)/shard_map/ppermute | solution.py:714
  114.5 1.0 collective-permute-start.8
  115.7 37.0 %collective-permute-done.8.odd = f32[8,8,128]{2,1,0:T(8,128)S(1)} collective-permute-done((f32[8,8,128]{2,1,0:T(8,128)S(1)}, f32[8,8,128]{2,1,0:T(8,128)S(1)}, u32[]{:S(2)}, u32[]{:S(2)}) %collective-permute-start.8) | collective-permute-done | bytes 32800 | tf_op jit(solution)/shard_map/ppermute | solution.py:714
  152.7 1.2 shard_map.115.r0
  153.9 2.0 %shard_map.117 = (f32[3,8,8,8,128]{4,3,2,1,0:T(8,128)S(1)}, f32[4,8,8,8,128]{4,3,2,1,0:T(8,128)S(1)}, f32[2,8,8,128]{3,2,1,0:T(8,128)S(1)}, f32[2,8,8,128]{3,2,1,0:T(8,128)S(1)}) custom-call(f32[4,8,8,8,128]{4,3,2,1,0:T(8,128)S(1)} %copy-done, f32[4,8,8,8,128]{4,3,2,1,0:T(8,128)S(1)} %shard_map.115.r0, f32[6272,128]{1,0:T(8,128)S(1)} %bitcast.4, ...), custom_call_target="tpu_custom_call" | custom-call | flops 12000000 | bytes 4000000 | tf_op jit(solution)/shard_map/pallas_call | solution.py:832
  155.9 2.7 %shard_map.118 = (f32[4,8,8,8,128]{4,3,2,1,0:T(8,128)S(1)}, f32[4,8,8,8,128]{4,3,2,1,0:T(8,128)S(1)}, f32[3,8,8,128]{3,2,1,0:T(8,128)S(1)}, f32[3,8,8,128]{3,2,1...) custom-call(f32[4,8,8,8,128]{4,3,2,1,0:T(8,128)S(1)} %copy-done, ...), custom_call_target="tpu_custom_call" | custom-call | flops 16000000 | bytes 4000000 | tf_op jit(solution)/shard_map/pallas_call | solution.py:833
  160.7 8.8 %collective-permute-done.17.far_odd = f32[8,8,128]{2,1,0:T(8,128)S(1)} collective-permute-done((f32[8,8,128]{2,1,0:T(8,128)S(1)}, f32[8,8,128]{2,1,0:T(8,128)S(1)}, u32[]{:S(2)}, u32[]{:S(2)}) %collective-permute-start.17) | collective-permute-done | bytes 32800 | tf_op jit(solution)/shard_map/ppermute | solution.py:714
  169.6 3.9 %collective-permute-done.16.far_even = f32[8,8,128]{2,1,0:T(8,128)S(1)} collective-permute-done((f32[8,8,128]{2,1,0:T(8,128)S(1)}, f32[8,8,128]{2,1,0:T(8,128)S(1)}, u32[]{:S(2)}, u32[]{:S(2)}) %collective-permute-start.16) | collective-permute-done | bytes 32800 | tf_op jit(solution)/shard_map/ppermute | solution.py:714
  173.5 1.8 shard_map.120
  175.3 3.6 %shard_map.122 = (f32[3,8,8,8,128]{4,3,2,1,0:T(8,128)}, f32[4,8,8,8,128]{4,3,2,1,0:T(8,128)S(1)}, f32[2,8,8,128]{3,2,1,0:T(8,128)S(1)}, f32[2,8,8,128]{3,2,1,0:T(8,128)S(1)}) custom-call(f32[4,8,8,8,128]{4,3,2,1,0:T(8,128)S(1)} %get-tuple-element.61.w, f32[4,8,8,8,128]{4,3,2,1,0:T(8,128)S(1)} %get-tuple-element.62.r0, f32[6272,128]{1,0:T(8,128)} %bitcast.3.arrived_hbm, ...), custom_call_target="tpu_custom_call" | custom-call | flops 12000000 | bytes 4000000 | tf_op jit(solution)/shard_map/pallas_call | solution.py:844
  179.0 4.1 %collective-permute-start.19 = (f32[2,8,8,128]{3,2,1,0:T(8,128)S(1)}, f32[2,8,8,128]{3,2,1,0:T(8,128)S(1)}, u32[]{:S(2)}, u32[]{:S(2)}) collective-permute-start(f32[2,8,8,128]{3,2,1,0:T(8,128)S(1)} %get-tuple-element.74), channel_id=1, source_target_pairs={{1,2},{2,1},{3,4},{4,3},{5,6},{6,5},{7,8},{8,7},{9,10},{10,9},{11,... | collective-permute-start | bytes 196616 | tf_op jit(solution)/shard_map/ppermute | solution.py:714
  183.1 7.6 %shard_map.119 = f32[5,4,16,256]{3,2,1,0:T(8,128)} custom-call(f32[5,4,16,256]{3,2,1,0:T(8,128)S(1)} %get-tuple-element.40.refs_0_, f32[5,4,16,256]{3,2,1,0:T(8,128)S(1)} %copy-done.7, f32[5,1,32,256]{3,2,1,0:T(8,128)S(1)} %copy-done.13, f32[5,1,32,256]{3,2,1,0:T(8,128)S(1)} %copy-done.15, f32[5,2,16,256]{3,2,1,0:T(8,128)} %collective-permute-done.5.refs_4_, ...), custom_call_target="tpu_custom_call" | custom-call | flops 30000000 | bytes 4000000 | tf_op jit(solution)/shard_map/pallas_call | solution.py:799
  190.7 1.1 copy-done.5
  191.9 2.6 %shard_map.123 = (f32[4,8,8,8,128]{4,3,2,1,0:T(8,128)S(1)}, f32[4,8,8,8,128]{4,3,2,1,0:T(8,128)S(1)}) custom-call(f32[4,8,8,8,128]{4,3,2,1,0:T(8,128)S(1)} %get-tuple-element.61.w, f32[4,8,8,8,128]{4,3,2,1,0:T(8,128)S(1)} %get-tuple-element.69.s1, f32[3,8,8,8,128]{4,3,2,1,0:T(8,128)S(1)} %copy-done.5, f32[8,8,128]{2,1,0:T(8,128)S(1)} %copy-done.3), custom_call_target="tpu_custom_call" | custom-call | flops 16000000 | bytes 4000000 | tf_op jit(solution)/shard_map/pallas_call | solution.py:846
  194.5 1.5 shard_map.124
  (68 shorter events, 9.0 us)
Async XLA Ops:
  0.6 13.9 %collective-permute-start.9 = (f32[3,4,16,256]{3,2,1,0:T(8,128)}, f32[3,4,16,256]{3,2,1,0:T(8,128)S(1)}, u32[]{:S(2)}, u32[]{:S(2)}) collective-permute-start(f32[3,4,16,256]{3,2,1,0:T(8,128)} %refs_0_.1), channel_id=1, source_target_pairs={{0,1},{1,0},{2,3},{3,2},{4,5},{5,4},{6,7},{7,6},{8,9},{9,8},{10,11... | collective-permute-start | bytes 589832 | tf_op jit(solution)/shard_map/ppermute | solution.py:714
  1.6 11.2 %collective-permute-start.11 = (f32[3,1,16,256]{3,2,1,0:T(8,128)S(1)}, f32[3,1,16,256]{3,2,1,0:T(8,128)S(1)}, u32[]{:S(2)}, u32[]{:S(2)}) collective-permute-start(f32[3,1,16,256]{3,2,1,0:T(8,128)S(1)} %get-tuple-element.75), channel_id=1, source_target_pairs={{2,4},{4,2},{6,8},{8,6},{10,12},{12,10},{14,16},{16,14},{18,20},{2... | collective-permute-start | bytes 147464 | tf_op jit(solution)/shard_map/ppermute | solution.py:714
  10.4 4.1 %collective-permute-start.10 = (f32[3,1,16,256]{3,2,1,0:T(8,128)S(1)}, f32[3,1,16,256]{3,2,1,0:T(8,128)S(1)}, u32[]{:S(2)}, u32[]{:S(2)}) collective-permute-start(f32[3,1,16,256]{3,2,1,0:T(8,128)S(1)} %get-tuple-element.76), channel_id=1, source_target_pairs={{0,2},{2,0},{4,6},{6,4},{8,10},{10,8},{12,14},{14,12},{16,18},{18,... | collective-permute-start | bytes 147464 | tf_op jit(solution)/shard_map/ppermute | solution.py:714
  22.2 7.4 %copy-start.8 = (f32[5,4,16,256]{3,2,1,0:T(8,128)S(1)}, f32[5,4,16,256]{3,2,1,0:T(8,128)}, u32[]{:S(2)}) copy-start(f32[5,4,16,256]{3,2,1,0:T(8,128)} %get-tuple-element.39.refs_0_) | copy-start | bytes 983044
  22.2 77.2 %all-to-all-start = ((f32[128,1,6272]{2,1,0:T(1,128)}), f32[128,1,6272]{2,1,0:T(1,128)S(1)}, u32[]{:S(2)}, u32[]{:S(2)}) async-start(f32[128,1,6272]{2,1,0:T(1,128)} %bitcast.6), calls=%async_computation | async-start | bytes 6422528 | tf_op jit(solution)/shard_map/all_to_all | solution.py:718
  29.7 49.3 %collective-permute-start.1 = (f32[5,4,16,256]{3,2,1,0:T(8,128)S(1)}, f32[5,4,16,256]{3,2,1,0:T(8,128)S(1)}, u32[]{:S(2)}, u32[]{:S(2)}) collective-permute-start(f32[5,4,16,256]{3,2,1,0:T(8,128)S(1)} %copy-done.8), channel_id=1, source_target_pairs={{2,4},{4,2},{6,8},{8,6},{10,12},{12,10},{14,16},{16,14},{18,20},{2... | collective-permute-start | bytes 983048 | tf_op jit(solution)/shard_map/ppermute | solution.py:714
  37.0 41.9 %collective-permute-start = (f32[5,4,16,256]{3,2,1,0:T(8,128)S(1)}, f32[5,4,16,256]{3,2,1,0:T(8,128)S(1)}, u32[]{:S(2)}, u32[]{:S(2)}) collective-permute-start(f32[5,4,16,256]{3,2,1,0:T(8,128)S(1)} %copy-done.8), channel_id=1, source_target_pairs={{0,2},{2,0},{4,6},{6,4},{8,10},{10,8},{12,14},{14,12},{16,18},{18,... | collective-permute-start | bytes 983048 | tf_op jit(solution)/shard_map/ppermute | solution.py:714
  37.0 42.4 %collective-permute-start.2 = (f32[5,4,16,256]{3,2,1,0:T(8,128)S(1)}, f32[5,4,16,256]{3,2,1,0:T(8,128)S(1)}, u32[]{:S(2)}, u32[]{:S(2)}) collective-permute-start(f32[5,4,16,256]{3,2,1,0:T(8,128)S(1)} %copy-done.8), channel_id=1, source_target_pairs={{0,1},{1,0},{2,3},{3,2},{4,5},{5,4},{6,7},{7,6},{8,9},{9,8},{10,11... | collective-permute-start | bytes 983048 | tf_op jit(solution)/shard_map/ppermute | solution.py:714
  79.0 1.6 collective-permute-start.4
  79.0 2.1 %collective-permute-start.3 = (f32[5,4,16,256]{3,2,1,0:T(8,128)S(1)}, f32[5,4,16,256]{3,2,1,0:T(8,128)S(1)}, u32[]{:S(2)}, u32[]{:S(2)}) collective-permute-start(f32[5,4,16,256]{3,2,1,0:T(8,128)S(1)} %collective-permute-done.refs_1_), channel_id=1, source_target_pairs={{0,1},{1,0},{2,3},{3,2},{4,5},{5,4},{6,7},{7,6},{8,9},{9,8},{10,11... | collective-permute-start | bytes 983048 | tf_op jit(solution)/shard_map/ppermute | solution.py:714
  99.4 1.7 copy-start.1
  101.2 5.9 %copy-start.20 = (f32[5,2,16,256]{3,2,1,0:T(8,128)S(1)}, f32[5,2,16,256]{3,2,1,0:T(8,128)}, u32[]{:S(2)}) copy-start(f32[5,2,16,256]{3,2,1,0:T(8,128)} %copy-done.19) | copy-start | bytes 491524
  101.2 13.2 %copy-start = (f32[4,8,8,8,128]{4,3,2,1,0:T(8,128)S(1)}, f32[4,8,8,8,128]{4,3,2,1,0:T(8,128)}, u32[]{:S(2)}) copy-start(f32[4,8,8,8,128]{4,3,2,1,0:T(8,128)} %w.9) | copy-start | bytes 3145732
  101.2 51.5 %copy-start.3 = (f32[8,8,128]{2,1,0:T(8,128)S(1)}, f32[8,8,128]{2,1,0:T(8,128)}, u32[]{:S(2)}) copy-start(f32[8,8,128]{2,1,0:T(8,128)} %constant.18.clone.coef) | copy-start | bytes 98308
  101.2 74.1 %all-to-all-start.1 = ((f32[128,1,6272]{2,1,0:T(1,128)}), f32[128,1,6272]{2,1,0:T(1,128)}, u32[]{:S(2)}, u32[]{:S(2)}) async-start(f32[128,1,6272]{2,1,0:T(1,128)} %bitcast.5), calls=%async_computation.1 | async-start | bytes 6422528 | tf_op jit(solution)/shard_map/all_to_all | solution.py:718
  107.1 46.9 %copy-start.2 = (f32[128,1,6272]{2,1,0:T(1,128)S(1)}, f32[128,1,6272]{2,1,0:T(1,128)}, u32[]{:S(2)}) copy-start(f32[128,1,6272]{2,1,0:T(1,128)} %copy-done.1) | copy-start | bytes 9633796
  107.1 51.6 %collective-permute-start.6 = (f32[5,2,16,256]{3,2,1,0:T(8,128)S(1)}, f32[5,2,16,256]{3,2,1,0:T(8,128)}, u32[]{:S(2)}, u32[]{:S(2)}) collective-permute-start(f32[5,2,16,256]{3,2,1,0:T(8,128)S(1)} %copy-done.20), channel_id=1, source_target_pairs={{2,4},{4,2},{6,8},{8,6},{10,12},{12,10},{14,16},{16,14},{18,20},{2... | collective-permute-start | bytes 491528 | tf_op jit(solution)/shard_map/ppermute | solution.py:714
  114.4 44.3 %collective-permute-start.5 = (f32[5,2,16,256]{3,2,1,0:T(8,128)S(1)}, f32[5,2,16,256]{3,2,1,0:T(8,128)}, u32[]{:S(2)}, u32[]{:S(2)}) collective-permute-start(f32[5,2,16,256]{3,2,1,0:T(8,128)S(1)} %copy-done.20), channel_id=1, source_target_pairs={{0,2},{2,0},{4,6},{6,4},{8,10},{10,8},{12,14},{14,12},{16,18},{18,... | collective-permute-start | bytes 491528 | tf_op jit(solution)/shard_map/ppermute | solution.py:714
  114.4 1.3 collective-permute-start.7
  114.5 38.2 %collective-permute-start.8 = (f32[8,8,128]{2,1,0:T(8,128)S(1)}, f32[8,8,128]{2,1,0:T(8,128)S(1)}, u32[]{:S(2)}, u32[]{:S(2)}) collective-permute-start(f32[8,8,128]{2,1,0:T(8,128)S(1)} %get-tuple-element.46), channel_id=1, source_target_pairs={{1,2},{2,1},{3,4},{4,3},{5,6},{6,5},{7,8},{8,7},{9,10},{10,9},{11,... | collective-permute-start | bytes 98312 | tf_op jit(solution)/shard_map/ppermute | solution.py:714
  158.7 24.4 %collective-permute-start.12 = (f32[5,2,16,256]{3,2,1,0:T(8,128)}, f32[5,2,16,256]{3,2,1,0:T(8,128)}, u32[]{:S(2)}, u32[]{:S(2)}) collective-permute-start(f32[5,2,16,256]{3,2,1,0:T(8,128)} %collective-permute-done.5.refs_4_), channel_id=1, source_target_pairs={{0,1},{1,0},{2,3},{3,2},{4,5},{5,4},{6,7},{7,6},{8,9},{9,8},{10,11... | collective-permute-start | bytes 491528 | tf_op jit(solution)/shard_map/ppermute | solution.py:714
  158.8 24.3 %collective-permute-start.13 = (f32[5,2,16,256]{3,2,1,0:T(8,128)}, f32[5,2,16,256]{3,2,1,0:T(8,128)}, u32[]{:S(2)}, u32[]{:S(2)}) collective-permute-start(f32[5,2,16,256]{3,2,1,0:T(8,128)} %collective-permute-done.6.refs_5_), channel_id=1, source_target_pairs={{0,1},{1,0},{2,3},{3,2},{4,5},{5,4},{6,7},{7,6},{8,9},{9,8},{10,11... | collective-permute-start | bytes 491528 | tf_op jit(solution)/shard_map/ppermute | solution.py:714
  159.3 14.2 %collective-permute-start.14 = (f32[3,8,8,128]{3,2,1,0:T(8,128)S(1)}, f32[3,8,8,128]{3,2,1,0:T(8,128)S(1)}, u32[]{:S(2)}, u32[]{:S(2)}) collective-permute-start(f32[3,8,8,128]{3,2,1,0:T(8,128)S(1)} %get-tuple-element.58), channel_id=1, source_target_pairs={{0,1},{1,0},{2,3},{3,2},{4,5},{5,4},{6,7},{7,6},{8,9},{9,8},{10,11... | collective-permute-start | bytes 294920 | tf_op jit(solution)/shard_map/ppermute | solution.py:714
  159.4 14.1 %collective-permute-start.15 = (f32[3,8,8,128]{3,2,1,0:T(8,128)S(1)}, f32[3,8,8,128]{3,2,1,0:T(8,128)S(1)}, u32[]{:S(2)}, u32[]{:S(2)}) collective-permute-start(f32[3,8,8,128]{3,2,1,0:T(8,128)S(1)} %get-tuple-element.59), channel_id=1, source_target_pairs={{1,2},{2,1},{3,4},{4,3},{5,6},{6,5},{7,8},{8,7},{9,10},{10,9},{11,... | collective-permute-start | bytes 294920 | tf_op jit(solution)/shard_map/ppermute | solution.py:714
  159.9 9.6 %collective-permute-start.17 = (f32[8,8,128]{2,1,0:T(8,128)S(1)}, f32[8,8,128]{2,1,0:T(8,128)S(1)}, u32[]{:S(2)}, u32[]{:S(2)}) collective-permute-start(f32[8,8,128]{2,1,0:T(8,128)S(1)} %get-tuple-element.60), channel_id=1, source_target_pairs={{2,4},{4,2},{6,8},{8,6},{10,12},{12,10},{14,16},{16,14},{18,20},{2... | collective-permute-start | bytes 98312 | tf_op jit(solution)/shard_map/ppermute | solution.py:714
  169.6 3.9 %collective-permute-start.16 = (f32[8,8,128]{2,1,0:T(8,128)S(1)}, f32[8,8,128]{2,1,0:T(8,128)S(1)}, u32[]{:S(2)}, u32[]{:S(2)}) collective-permute-start(f32[8,8,128]{2,1,0:T(8,128)S(1)} %get-tuple-element.53), channel_id=1, source_target_pairs={{0,2},{2,0},{4,6},{6,4},{8,10},{10,8},{12,14},{14,12},{16,18},{18,... | collective-permute-start | bytes 98312 | tf_op jit(solution)/shard_map/ppermute | solution.py:714
  175.2 7.9 %copy-start.7 = (f32[5,4,16,256]{3,2,1,0:T(8,128)S(1)}, f32[5,4,16,256]{3,2,1,0:T(8,128)}, u32[]{:S(2)}) copy-start(f32[5,4,16,256]{3,2,1,0:T(8,128)} %copy-done.6) | copy-start | bytes 983044
  175.3 7.8 %copy-start.13 = (f32[5,1,32,256]{3,2,1,0:T(8,128)S(1)}, f32[5,1,32,256]{3,2,1,0:T(8,128)}, u32[]{:S(2)}) copy-start(f32[5,1,32,256]{3,2,1,0:T(8,128)} %copy-done.12) | copy-start | bytes 491524
  175.3 7.8 %copy-start.15 = (f32[5,1,32,256]{3,2,1,0:T(8,128)S(1)}, f32[5,1,32,256]{3,2,1,0:T(8,128)}, u32[]{:S(2)}) copy-start(f32[5,1,32,256]{3,2,1,0:T(8,128)} %copy-done.14) | copy-start | bytes 491524
  178.9 15.6 %collective-permute-start.18 = (f32[2,8,8,128]{3,2,1,0:T(8,128)S(1)}, f32[2,8,8,128]{3,2,1,0:T(8,128)S(1)}, u32[]{:S(2)}, u32[]{:S(2)}) collective-permute-start(f32[2,8,8,128]{3,2,1,0:T(8,128)S(1)} %get-tuple-element.73), channel_id=1, source_target_pairs={{0,1},{1,0},{2,3},{3,2},{4,5},{5,4},{6,7},{7,6},{8,9},{9,8},{10,11... | collective-permute-start | bytes 196616 | tf_op jit(solution)/shard_map/ppermute | solution.py:714
  179.0 15.5 %collective-permute-start.19 = (f32[2,8,8,128]{3,2,1,0:T(8,128)S(1)}, f32[2,8,8,128]{3,2,1,0:T(8,128)S(1)}, u32[]{:S(2)}, u32[]{:S(2)}) collective-permute-start(f32[2,8,8,128]{3,2,1,0:T(8,128)S(1)} %get-tuple-element.74), channel_id=1, source_target_pairs={{1,2},{2,1},{3,4},{4,3},{5,6},{6,5},{7,8},{8,7},{9,10},{10,9},{11,... | collective-permute-start | bytes 196616 | tf_op jit(solution)/shard_map/ppermute | solution.py:714
  190.7 1.1 copy-start.5
  (11 other events, 8.5 us)
